TPU v7x, 32 devices: a whole 2x2x4 slice. The times are simulated.
32 devices in a mesh: group: 8 (over y, x, core), shard: 4 (over z).
Axes of the slice: x: 2, y: 2, z: 4, core: 2. Of those that a mesh axis runs over, the one named last changes fastest.
Arguments:
- momentum: bfloat16 [8, 7168, 2048], P(None, ('group', 'shard'))
- gradient: bfloat16 [8, 7168, 2048], P(None, ('group', 'shard'))
- q_prev: bfloat16 [8, 3, 2048, 128], P('group', None, 'shard'), may hold values from -6 to 6
- owner_group: int32 [8], replicated, may hold values from 0 to 7, as said below
- group_counts: int32 [8], replicated, may hold values from 0 to 3, as said below
Outputs:
- momentum_next: bfloat16 [8, 7168, 2048], P(None, ('group', 'shard'))
- update: bfloat16 [8, 7168, 2048], P(None, ('group', 'shard'))
- q_next: bfloat16 [8, 3, 2048, 128], P('group', None, 'shard')
Inputs may be any that keep to these rules, and one draw needn't show every extreme that they name: `owner_group`: each group owns at most 3 experts and some group owns exactly 3; a group's experts fill its slots 0, 1, ... in increasing expert order. `group_counts`: entry g is the number of experts whose owner_group is g, except for one or two groups that own some experts, where it is one less; it equals 3 for some group that owns 3 experts.
All inputs are finite; a program needn't handle non-finite values.
Results may differ from a plain program's by a relative error of at most 0.0059.
Values may be sent and summed in bfloat16 or wider, within the bound.
No kernel may reach another device: no remote copies, remote signals or barrier semaphores. Data moves between devices by JAX's collectives and lax.ppermute only.
A program may use at most 128 MiB of HBM per device.

v0:
```python
import functools
import math

import jax
import jax.numpy as jnp
from jax import lax
from jax.experimental import pallas as pl
from jax.experimental.pallas import tpu as pltpu
from jax.sharding import PartitionSpec as P


stability_offset = 1e-06
momentum_decay = 0.6
DOWN = 2.0**-64
UP = 2.0**64
WEIGHT = 8
AXES = ("group", "shard")


def owner_slots(owner_group):
    experts = owner_group.shape[0]
    expert_ids = jnp.arange(experts, dtype=jnp.int32)
    same_owner = owner_group[:, None] == owner_group[None, :]
    earlier = expert_ids[None, :] < expert_ids[:, None]
    return jnp.sum((same_owner & earlier).astype(jnp.int32), axis=1)


def bits_of(size):
    bits = []
    bit = 1
    while bit < size:
        bits.append(bit)
        bit *= 2
    assert bit == size
    return bits


class Links:
    def __init__(self, groups, shards):
        self.groups, self.shards = groups, shards

    def swap_group(self, x, bit):
        pairs = [
            (g * self.shards + s, (g ^ bit) * self.shards + s)
            for g in range(self.groups)
            for s in range(self.shards)
        ]
        return lax.ppermute(x, AXES, pairs)

    def swap_shard(self, x, bit):
        pairs = [
            (g * self.shards + s, g * self.shards + (s ^ bit))
            for g in range(self.groups)
            for s in range(self.shards)
        ]
        return lax.ppermute(x, AXES, pairs)

    def shift_shard(self, x, step):
        pairs = [
            (g * self.shards + s, g * self.shards + (s + step) % self.shards)
            for g in range(self.groups)
            for s in range(self.shards)
        ]
        return lax.ppermute(x, AXES, pairs)

    def orders(self):
        near, *far = bits_of(self.groups)
        return near, (far, far[::-1])

    def levels(self):
        return len(self.orders()[1][0])

    def cross(self, x, level):
        near, orders = self.orders()
        turn = [orders[1 if g & near else 0][level] for g in range(self.groups)]
        pairs = [
            (g * self.shards + s, (g ^ turn[g]) * self.shards + s)
            for g in range(self.groups)
            for s in range(self.shards)
        ]
        return lax.ppermute(x, AXES, pairs)

    def spread(self, own):
        held = {0: own}
        for level in range(self.levels()):
            for name in list(held):
                held[name | 1 << level] = self.cross(held[name], level)
        return held

    def collect(self, held):
        held = {name: list(pieces) for name, pieces in held.items()}
        for level in reversed(range(self.levels())):
            for name in [name for name in held if name >> level & 1]:
                terms = held.pop(name)
                sent = sum(term.astype(jnp.float32) for term in terms).astype(jnp.bfloat16)
                held[name ^ 1 << level].append(self.cross(sent, level))
        return held[0]


def add_body(m_ref, g_ref, c_ref):
    c_ref[...] = (m_ref[...].astype(jnp.float32) + g_ref[...].astype(jnp.float32)).astype(
        jnp.bfloat16
    )


def add_call(momentum, gradient):
    experts, rows, hidden = momentum.shape
    block = pl.BlockSpec((1, rows, hidden), lambda i: (i, 0, 0))
    return pl.pallas_call(
        add_body,
        grid=(experts,),
        in_specs=[block, block],
        out_specs=block,
        out_shape=jax.ShapeDtypeStruct(momentum.shape, jnp.bfloat16),
        cost_estimate=pl.CostEstimate(
            flops=WEIGHT * experts * 2 * rows * hidden * 128,
            bytes_accessed=6 * momentum.size,
            transcendentals=0,
        ),
        name="add",
    )(momentum, gradient)


def split_body(shard_count, where, *refs):
    ins, outs, total_ref = refs[: -shard_count - 1], refs[-shard_count - 1 : -1], refs[-1]
    total = ins[0][...].astype(jnp.float32)
    for ref in ins[1:]:
        total = total + ref[...].astype(jnp.float32)
    total_ref[...] = total
    piece = outs[0].shape[0]
    for step, out in enumerate(outs):
        start = lax.rem(where[2, 0] + step, shard_count) * piece
        out[...] = total_ref[pl.ds(pl.multiple_of(start, piece), piece), :].astype(jnp.bfloat16)


def split_call(where, terms, shard_count):
    rank, hidden = terms[0].shape
    piece = rank // shard_count
    return pl.pallas_call(
        functools.partial(split_body, shard_count),
        grid_spec=pltpu.PrefetchScalarGridSpec(
            num_scalar_prefetch=1,
            grid=(1,),
            in_specs=[fixed((rank, hidden))] * len(terms),
            out_specs=[fixed((piece, hidden))] * shard_count,
            scratch_shapes=[pltpu.VMEM((rank, hidden), jnp.float32)],
        ),
        out_shape=[jax.ShapeDtypeStruct((piece, hidden), jnp.bfloat16)] * shard_count,
        name="split",
    )(where, *terms)


def load(refs, buf, sems):
    step = pl.program_id(0)

    @pl.when(step == 0)
    def _():
        for j, ref in enumerate(refs):
            pltpu.make_async_copy(ref, buf.at[j], sems.at[j]).start()

    for j, ref in enumerate(refs):

        @pl.when(step == j)
        def _():
            pltpu.make_async_copy(ref, buf.at[j], sems.at[j]).wait()

    return buf[step]


def first_body(count, where, c_ref, *refs):
    q_refs, refs = refs[:count], refs[count:]
    left_ref, right_refs, (buf, sems) = refs[0], refs[1:-2], refs[-2:]
    hidden = c_ref.shape[2]
    step = pl.program_id(0)
    combined = c_ref[0]
    q = load(q_refs, buf, sems)
    left = jnp.dot(combined, q, preferred_element_type=jnp.float32)
    left_ref[0] = left
    squares = jnp.sum(left * left, axis=0, keepdims=True)
    squares = jnp.broadcast_to(squares, (squares.shape[1],) * 2).T.astype(jnp.bfloat16)
    small = (left * DOWN).astype(jnp.bfloat16)
    dims = (((0,), (0,)), ((), ()))
    right = lax.dot_general(small, combined, dims, preferred_element_type=jnp.float32)
    right = right.astype(jnp.bfloat16)
    for j in range(count):

        @pl.when(step == j)
        def _():
            right_refs[j][:, :hidden] = right
            right_refs[j][:, hidden:] = squares


def fixed(shape):
    return pl.BlockSpec(shape, lambda i, w: (0,) * len(shape))


def first_call(where, base, combined, qs):
    _, rows, hidden = combined.shape
    count = len(qs)
    _, rank = qs[0].shape
    outs = pl.pallas_call(
        functools.partial(first_body, count),
        grid_spec=pltpu.PrefetchScalarGridSpec(
            num_scalar_prefetch=1,
            grid=(count,),
            in_specs=[pl.BlockSpec((1, rows, hidden), lambda i, w: (w[0, base + i], 0, 0))]
            + [pl.BlockSpec(memory_space=pl.ANY)] * count,
            out_specs=[pl.BlockSpec((1, rows, rank), lambda i, w: (i, 0, 0))]
            + [fixed((rank, hidden + rank))] * count,
            scratch_shapes=[
                pltpu.VMEM((count, hidden, rank), jnp.bfloat16),
                pltpu.SemaphoreType.DMA((count,)),
            ],
        ),
        out_shape=[jax.ShapeDtypeStruct((count, rows, rank), jnp.float32)]
        + [jax.ShapeDtypeStruct((rank, hidden + rank), jnp.bfloat16)] * count,
        cost_estimate=pl.CostEstimate(
            flops=WEIGHT * count * 4 * rows * hidden * rank,
            bytes_accessed=count * 2 * (rows + 2 * rank) * hidden,
            transcendentals=0,
        ),
        name="first",
    )(where, combined, *qs)
    return outs[0], outs[1:]


def last_body(count, multiplier, cap, base, fresh, where, c_ref, left_ref, *refs):
    right_refs, refs = refs[:count], refs[count:]
    mom_ref, upd_ref, q_ref, buf, sems = refs[-5:]
    step = pl.program_id(0)

    @pl.when(step == 0)
    def _():
        if fresh:
            q_ref[...] = jnp.zeros_like(q_ref)
        else:
            q_ref[...] = refs[0][...]

    hidden = c_ref.shape[2]
    arrived = load(right_refs, buf, sems)
    squares = arrived[:, hidden : hidden + 1].astype(jnp.float32)
    n_col = lax.rsqrt(squares + stability_offset)
    n_row = jnp.broadcast_to(n_col, (n_col.shape[0],) * 2).T[0:1, :]
    n_col = n_col * UP
    left = (left_ref[0] * n_row).astype(jnp.bfloat16)
    right = arrived[:, :hidden].astype(jnp.float32) * n_col
    total = jnp.sum(right * right, axis=1, keepdims=True)
    scale = lax.rsqrt(total / right.shape[1] + stability_offset)
    low = jnp.dot(left, right.astype(jnp.bfloat16), preferred_element_type=jnp.float32)
    kept = c_ref[0].astype(jnp.float32)
    mom_ref[0] = (kept - (1.0 - momentum_decay) * low).astype(jnp.bfloat16)
    q_new = (right * scale).astype(jnp.bfloat16)
    upd = jnp.dot(left, q_new, preferred_element_type=jnp.float32) * multiplier
    upd_ref[0] = upd.astype(jnp.bfloat16)
    slot = where[1, base + step]

    @pl.when(slot < cap)
    def _():
        share = q_ref.shape[1]
        start = pl.multiple_of(where[2, 0] * share, share)
        own = buf[step, :, pl.ds(start, share)].astype(jnp.float32) * n_col * scale
        q_ref[slot] = own.T.astype(jnp.bfloat16)


def last_call(where, base, combined, left, rights, outs, cap, share, multiplier):
    experts, rows, hidden = combined.shape
    count = len(rights)
    rank, width = rights[0].shape
    block = pl.BlockSpec((1, rows, hidden), lambda i, w: (w[0, base + i], 0, 0))
    anywhere = pl.BlockSpec(memory_space=pl.ANY)
    extra = [] if outs is None else [outs[2], outs[0], outs[1]]
    return pl.pallas_call(
        functools.partial(last_body, count, multiplier, cap, base, outs is None),
        grid_spec=pltpu.PrefetchScalarGridSpec(
            num_scalar_prefetch=1,
            grid=(count,),
            in_specs=[
                block,
                pl.BlockSpec((1, rows, rank), lambda i, w: (i, 0, 0)),
            ]
            + [pl.BlockSpec(memory_space=pl.ANY)] * count
            + ([] if outs is None else [fixed((cap, share, rank)), anywhere, anywhere]),
            out_specs=[block, block, fixed((cap, share, rank))],
            scratch_shapes=[
                pltpu.VMEM((count, rank, width), jnp.bfloat16),
                pltpu.SemaphoreType.DMA((count,)),
            ],
        ),
        out_shape=[
            jax.ShapeDtypeStruct((experts, rows, hidden), jnp.bfloat16),
            jax.ShapeDtypeStruct((experts, rows, hidden), jnp.bfloat16),
            jax.ShapeDtypeStruct((cap, share, rank), jnp.bfloat16),
        ],
        input_output_aliases={} if outs is None else {4 + count: 0, 5 + count: 1},
        cost_estimate=pl.CostEstimate(
            flops=WEIGHT * count * 4 * rows * hidden * rank,
            bytes_accessed=count * 2 * (3 * rows + 2 * rank) * hidden,
            transcendentals=0,
        ),
        name="last",
    )(where, combined, left, *rights, *extra)


def step(momentum, gradient, q_prev, owner_group, group_counts):
    groups = lax.axis_size("group")
    shard_count = lax.axis_size("shard")
    mine = lax.axis_index("group")
    shard = lax.axis_index("shard")
    experts, rows, _ = momentum.shape
    _, cap, share, rank = q_prev.shape
    assert experts == groups
    links = Links(groups, shard_count)
    near, orders = links.orders()

    names = range(1 << links.levels())
    most = max(name.bit_count() for name in names)
    sets = [[name for name in names if name.bit_count() == n] for n in range(most + 1)]

    def distances(side):
        reach = lambda name, at: sum(bit for i, bit in enumerate(orders[at]) if name >> i & 1)
        return [
            reach(name, side ^ far) ^ (near if far else 0)
            for members in sets
            for far in (0, 1)
            for name in members
        ]

    slot_of = owner_slots(owner_group)
    owned = (slot_of < group_counts[owner_group]) & (owner_group == mine)
    slots = jnp.where(owned, slot_of, cap)
    chosen = mine ^ jnp.where(
        mine & near > 0, jnp.array(distances(1), jnp.int32), jnp.array(distances(0), jnp.int32)
    )
    where = jnp.stack([chosen, slots[chosen], jnp.full_like(chosen, shard)]).astype(jnp.int32)

    uppers = [r for r in range(groups) if not r & near]

    def outgoing(members):
        picked = slots[mine ^ jnp.array(members, jnp.int32)]
        sent = jnp.zeros((len(members), share, rank), q_prev.dtype)
        for slot in range(cap):
            sent = jnp.where((picked == slot)[:, None, None], q_prev[0, slot][None], sent)
        return sent

    arrived = links.swap_group(outgoing([r ^ near for r in uppers]), near)
    kept = outgoing(uppers)
    parts = [kept[i] + arrived[i] for i in range(len(uppers))]
    q_own = parts[0]
    for part, r in zip(parts[1:], uppers[1:]):
        q_own = q_own + links.swap_group(part, r)
    combined = add_call(momentum, gradient)
    q_own, combined = lax.optimization_barrier((q_own, combined))
    q_full = lax.all_gather(q_own, "shard", axis=0, tiled=True)
    qs = links.spread(q_full)
    qs_far = {name: links.swap_group(piece, near) for name, piece in qs.items()}

    lefts, rights, bases = [], {}, []
    base = 0
    for members in sets:
        count = len(members)
        left, outs = first_call(
            where, base, combined, [qs[n] for n in members] + [qs_far[n] for n in members]
        )
        lefts.append(left)
        for j, name in enumerate(members):
            rights[name] = [outs[j], links.swap_group(outs[count + j], near)]
        bases.append(base)
        base += 2 * count

    pieces = split_call(where, links.collect(rights), shard_count)
    mine_sum = pieces[0].astype(jnp.float32)
    for d in range(1, shard_count):
        mine_sum = mine_sum + links.shift_shard(pieces[d], d).astype(jnp.float32)
    right_own = lax.all_gather(mine_sum.astype(jnp.bfloat16), "shard", axis=0, tiled=True)
    full = links.spread(right_own)
    full_far = {name: links.swap_group(piece, near) for name, piece in full.items()}

    multiplier = math.sqrt(rows * groups * shard_count / rank)
    outs = None
    for i, members in enumerate(sets):
        pieces = [full[name] for name in members] + [full_far[name] for name in members]
        outs = last_call(where, bases[i], combined, lefts[i], pieces, outs, cap, share, multiplier)
    momentum_next, update, q_next = outs
    return momentum_next, update, q_next[None]


def solution(mesh):
    return jax.shard_map(
        step,
        mesh=mesh,
        in_specs=(
            P(None, ("group", "shard"), None),
            P(None, ("group", "shard"), None),
            P("group", None, "shard", None),
            P(),
            P(),
        ),
        out_specs=(
            P(None, ("group", "shard"), None),
            P(None, ("group", "shard"), None),
            P("group", None, "shard", None),
        ),
        check_vma=False,
    )
```

profile of v0, /device:TPU:0, one launch (start us, length us, event | category | flops | bytes accessed | tf_op | source)
XLA Modules:
  0.0 188.0 jit_solution(3148406187275359428)
XLA Ops:
  6.4 1.5 collective-permute-done
  8.0 2.9 %collective-permute-start.1 = (bf16[512,128]{1,0:T(8,128)(2,1)S(1)}, bf16[512,128]{1,0:T(8,128)(2,1)S(1)}, u32[]{:S(2)}, u32[]{:S(2)}) collective-permute-start(bf16[512,128]{1,0:T(8,128)(2,1)S(1)} %get-tuple-element.55), channel_id=1, source_target_pairs={{0,8},{1,9},{2,10},{3,11},{4,12},{5,13},{6,14},{7,15},{8,0},{9,1},... | collective-permute-start | bytes 393224 | tf_op jit(solution)/shard_map/ppermute | solution.py:48
  10.9 1.5 collective-permute-start.2
  12.5 10.4 %add.131.c_ref = bf16[8,224,2048]{2,1,0:T(8,128)(2,1)} custom-call(bf16[8,224,2048]{2,1,0:T(8,128)(2,1)} %m_ref.1, bf16[8,224,2048]{2,1,0:T(8,128)(2,1)} %g_ref.1), custom_call_target="tpu_custom_call" | custom-call | flops 7516192768 | bytes 22020096 | tf_op jit(solution)/shard_map/add/pallas_call | solution.py:109
  22.9 15.9 %all_gather.6.refs_0_ = bf16[2048,128]{1,0:T(8,128)(2,1)S(1)} all-gather(bf16[512,128]{1,0:T(8,128)(2,1)S(1)} %fusion.6), channel_id=1, replica_groups=mesh['group'=8,'shard'=4] {'shard'}, dimensions={0}, use_global_device_ids=true | all-gather | bytes 655360 | tf_op jit(solution)/shard_map/all_gather | solution.py:353
  38.8 1.5 collective-permute-start.4
  40.3 8.5 %collective-permute-done.4.refs_0_ = bf16[2048,128]{1,0:T(8,128)(2,1)S(1)} collective-permute-done((bf16[2048,128]{1,0:T(8,128)(2,1)S(1)}, bf16[2048,128]{1,0:T(8,128)(2,1)S(1)}, u32[]{:S(2)}, u32[]{:S(2)}) %collective-permute-start.4) | collective-permute-done | bytes 524320 | tf_op jit(solution)/shard_map/ppermute | solution.py:81
  48.8 1.5 collective-permute-start.5
  51.6 6.4 %collective-permute-done.5.refs_0_ = bf16[2048,128]{1,0:T(8,128)(2,1)S(1)} collective-permute-done((bf16[2048,128]{1,0:T(8,128)(2,1)S(1)}, bf16[2048,128]{1,0:T(8,128)(2,1)S(1)}, u32[]{:S(2)}, u32[]{:S(2)}) %collective-permute-start.5) | collective-permute-done | bytes 524320 | tf_op jit(solution)/shard_map/ppermute | solution.py:81
  59.1 4.5 %collective-permute-done.9.refs_1_ = bf16[2048,128]{1,0:T(8,128)(2,1)S(1)} collective-permute-done((bf16[2048,128]{1,0:T(8,128)(2,1)S(1)}, bf16[2048,128]{1,0:T(8,128)(2,1)S(1)}, u32[]{:S(2)}, u32[]{:S(2)}) %collective-permute-start.9) | collective-permute-done | bytes 524320 | tf_op jit(solution)/shard_map/ppermute | solution.py:81
  64.5 5.8 %first.4 = (f32[2,224,128]{2,1,0:T(8,128)}, bf16[128,2176]{1,0:T(8,128)(2,1)}, bf16[128,2176]{1,0:T(8,128)(2,1)}) custom-call(s32[3,8]{1,0:T(4,128)} %add_add_fusion.where, bf16[8,224,2048]{2,1,0:T(8,128)(2,1)} %add.131.c_ref, bf16[2048,128]{1,0:T(8,128)(2,1)} %copy-done.10, bf16[2048,128]{1,0:T(8,128)(2,1)} %copy-done.21), custom_call_target="tpu_custom_call" | custom-call | flops 3758096384 | bytes 3932160 | tf_op jit(solution)/shard_map/first/pallas_call | solution.py:201
  70.8 5.7 %first.3 = (f32[2,224,128]{2,1,0:T(8,128)}, bf16[128,2176]{1,0:T(8,128)(2,1)}, bf16[128,2176]{1,0:T(8,128)(2,1)}) custom-call(s32[3,8]{1,0:T(4,128)} %add_add_fusion.where, bf16[8,224,2048]{2,1,0:T(8,128)(2,1)} %add.131.c_ref, bf16[2048,128]{1,0:T(8,128)(2,1)} %copy-done.19, bf16[2048,128]{1,0:T(8,128)(2,1)} %collective-permute-done.6.refs_1_), custom_call_target="tpu_custom_call" | custom-call | flops 3758096384 | bytes 3932160 | tf_op jit(solution)/shard_map/first/pallas_call | solution.py:201
  77.4 8.2 %first.5 = (f32[4,224,128]{2,1,0:T(8,128)}, bf16[128,2176]{1,0:T(8,128)(2,1)}, bf16[128,2176]{1,0:T(8,128)(2,1)}, bf16[128,2176]{1,0:T(8,128)(2,1)}, bf16[128,2176]{1,0:T(8,128)(2,1)}) custom-call(s32[3,8]{1,0:T(4,128)} %add_add_fusion.where, bf16[8,224,2048]{2,1,0:T(8,128)(2,1)} %add.131.c_ref, bf16[2048,128]{1,0:T(8,128)(2,1)} %copy-done.17, ...), custom_call_target="tpu_custom_call" | custom-call | flops 7516192768 | bytes 7864320 | tf_op jit(solution)/shard_map/first/pallas_call | solution.py:201
  86.4 1.6 collective-permute-start.16
  88.9 1.6 collective-permute-start.13
  90.5 5.5 %collective-permute-done.16 = bf16[128,2176]{1,0:T(8,128)(2,1)S(1)} collective-permute-done((bf16[128,2176]{1,0:T(8,128)(2,1)S(1)}, bf16[128,2176]{1,0:T(8,128)(2,1)S(1)}, u32[]{:S(2)}, u32[]{:S(2)}) %collective-permute-start.16) | collective-permute-done | bytes 557088 | tf_op jit(solution)/shard_map/ppermute | solution.py:81
  96.2 1.6 collective-permute-start.17
  97.7 7.7 %collective-permute-done.13.refs_2_ = bf16[128,2176]{1,0:T(8,128)(2,1)S(1)} collective-permute-done((bf16[128,2176]{1,0:T(8,128)(2,1)S(1)}, bf16[128,2176]{1,0:T(8,128)(2,1)S(1)}, u32[]{:S(2)}, u32[]{:S(2)}) %collective-permute-start.13) | collective-permute-done | bytes 557088 | tf_op jit(solution)/shard_map/ppermute | solution.py:81
  105.5 1.9 %collective-permute-done.17.refs_3_ = bf16[128,2176]{1,0:T(8,128)(2,1)S(1)} collective-permute-done((bf16[128,2176]{1,0:T(8,128)(2,1)S(1)}, bf16[128,2176]{1,0:T(8,128)(2,1)S(1)}, u32[]{:S(2)}, u32[]{:S(2)}) %collective-permute-start.17) | collective-permute-done | bytes 557088 | tf_op jit(solution)/shard_map/ppermute | solution.py:81
  108.2 3.5 %split.1 = (bf16[32,2176]{1,0:T(8,128)(2,1)}, bf16[32,2176]{1,0:T(8,128)(2,1)}, bf16[32,2176]{1,0:T(8,128)(2,1)}, bf16[32,2176]{1,0:T(8,128)(2,1)}) custom-call(s32[3,8]{1,0:T(4,128)} %add_add_fusion.where, bf16[128,2176]{1,0:T(8,128)(2,1)} %get-tuple-element.32.refs_0_, bf16[128,2176]{1,0:T(8,128)(2,1)} %copy-done.3, bf16[128,2176]{1,0:T(8,128)(2,1)} %copy-done.7, ...), custom_call_target="tpu_custom_call" | custom-call | tf_op jit(solution)/shard_map/split/pallas_call | solution.py:139
  111.7 4.1 %collective-permute-start.18 = (bf16[32,2176]{1,0:T(8,128)(2,1)}, bf16[32,2176]{1,0:T(8,128)(2,1)S(1)}, u32[]{:S(2)}, u32[]{:S(2)}) collective-permute-start(bf16[32,2176]{1,0:T(8,128)(2,1)} %get-tuple-element.41), channel_id=1, source_target_pairs={{0,1},{1,2},{2,3},{3,0},{4,5},{5,6},{6,7},{7,4},{8,9},{9,10},{10,1... | collective-permute-start | bytes 417800 | tf_op jit(solution)/shard_map/ppermute | solution.py:64
  115.8 2.6 %collective-permute-start.19 = (bf16[32,2176]{1,0:T(8,128)(2,1)}, bf16[32,2176]{1,0:T(8,128)(2,1)S(1)}, u32[]{:S(2)}, u32[]{:S(2)}) collective-permute-start(bf16[32,2176]{1,0:T(8,128)(2,1)} %get-tuple-element.42), channel_id=1, source_target_pairs={{0,2},{1,3},{2,0},{3,1},{4,6},{5,7},{6,4},{7,5},{8,10},{9,11},{10,... | collective-permute-start | bytes 417800 | tf_op jit(solution)/shard_map/ppermute | solution.py:64
  118.4 4.3 %collective-permute-done.18 = bf16[32,2176]{1,0:T(8,128)(2,1)S(1)} collective-permute-done((bf16[32,2176]{1,0:T(8,128)(2,1)}, bf16[32,2176]{1,0:T(8,128)(2,1)S(1)}, u32[]{:S(2)}, u32[]{:S(2)}) %collective-permute-start.18) | collective-permute-done | bytes 139296 | tf_op jit(solution)/shard_map/ppermute | solution.py:64
  122.6 5.6 %collective-permute-done.19 = bf16[32,2176]{1,0:T(8,128)(2,1)S(1)} collective-permute-done((bf16[32,2176]{1,0:T(8,128)(2,1)}, bf16[32,2176]{1,0:T(8,128)(2,1)S(1)}, u32[]{:S(2)}, u32[]{:S(2)}) %collective-permute-start.19) | collective-permute-done | bytes 139296 | tf_op jit(solution)/shard_map/ppermute | solution.py:64
  129.3 16.3 %all_gather.7.refs_0_ = bf16[128,2176]{1,0:T(8,128)(2,1)S(1)} all-gather(bf16[32,2176]{1,0:T(8,128)(2,1)S(1)} %add_convert_fusion.3), channel_id=1, replica_groups=mesh['group'=8,'shard'=4] {'shard'}, dimensions={0}, use_global_device_ids=true | all-gather | bytes 696320 | tf_op jit(solution)/shard_map/all_gather | solution.py:374
  145.5 1.5 collective-permute-start.21
  147.0 1.5 collective-permute-start.24
  148.5 12.5 %collective-permute-done.21.refs_0_ = bf16[128,2176]{1,0:T(8,128)(2,1)S(1)} collective-permute-done((bf16[128,2176]{1,0:T(8,128)(2,1)S(1)}, bf16[128,2176]{1,0:T(8,128)(2,1)S(1)}, u32[]{:S(2)}, u32[]{:S(2)}) %collective-permute-start.21) | collective-permute-done | bytes 557088 | tf_op jit(solution)/shard_map/ppermute | solution.py:81
  162.4 6.3 %last.3 = (bf16[8,224,2048]{2,1,0:T(8,128)(2,1)}, bf16[8,224,2048]{2,1,0:T(8,128)(2,1)}, bf16[3,512,128]{2,1,0:T(8,128)(2,1)}) custom-call(s32[3,8]{1,0:T(4,128)} %add_add_fusion.where, bf16[8,224,2048]{2,1,0:T(8,128)(2,1)} %add.131.c_ref, f32[2,224,128]{2,1,0:T(8,128)} %get-tuple-element.45.left_ref, bf16[128,2176]{1,0:T(8,128)(2,1)} %copy-done.5, ...), custom_call_target="tpu_custom_call" | custom-call | flops 3758096384 | bytes 7602176 | tf_op jit(solution)/shard_map/last/pallas_call | solution.py:272
  168.7 1.8 collective-permute-done.22.refs_0_
  171.6 9.2 %last.4 = (bf16[8,224,2048]{2,1,0:T(8,128)(2,1)}, bf16[8,224,2048]{2,1,0:T(8,128)(2,1)}, bf16[3,512,128]{2,1,0:T(8,128)(2,1)}) custom-call(s32[3,8]{1,0:T(4,128)} %add_add_fusion.where, bf16[8,224,2048]{2,1,0:T(8,128)(2,1)} %add.131.c_ref, f32[4,224,128]{2,1,0:T(8,128)} %get-tuple-element.44.left_ref, ...), custom_call_target="tpu_custom_call", output_to_operand_aliasing={{0}: (8, {}), {1}: (9, {})} | custom-call | flops 7516192768 | bytes 15204352 | tf_op jit(solution)/shard_map/last/pallas_call | solution.py:272
  181.7 6.3 %last.5 = (bf16[8,224,2048]{2,1,0:T(8,128)(2,1)}, bf16[8,224,2048]{2,1,0:T(8,128)(2,1)}, bf16[3,512,128]{2,1,0:T(8,128)(2,1)}) custom-call(s32[3,8]{1,0:T(4,128)} %add_add_fusion.where, bf16[8,224,2048]{2,1,0:T(8,128)(2,1)} %add.131.c_ref, f32[2,224,128]{2,1,0:T(8,128)} %get-tuple-element.31.left_ref, ...), custom_call_target="tpu_custom_call", output_to_operand_aliasing={{0}: (6, {}), {1}: (7, {})} | custom-call | flops 3758096384 | bytes 7602176 | tf_op jit(solution)/shard_map/last/pallas_call | solution.py:272
  (102 shorter events, 17.5 us)
Async XLA Ops:
  5.9 2.1 %collective-permute-start = (bf16[4,512,128]{2,1,0:T(8,128)(2,1)S(1)}, bf16[4,512,128]{2,1,0:T(8,128)(2,1)S(1)}, u32[]{:S(2)}, u32[]{:S(2)}) collective-permute-start(bf16[4,512,128]{2,1,0:T(8,128)(2,1)S(1)} %get-tuple-element.59), channel_id=1, source_target_pairs={{0,4},{1,5},{2,6},{3,7},{4,0},{5,1},{6,2},{7,3},{8,12},{9,13},{10,... | collective-permute-start | bytes 1572872 | tf_op jit(solution)/shard_map/ppermute | solution.py:48
  8.0 14.8 %collective-permute-start.1 = (bf16[512,128]{1,0:T(8,128)(2,1)S(1)}, bf16[512,128]{1,0:T(8,128)(2,1)S(1)}, u32[]{:S(2)}, u32[]{:S(2)}) collective-permute-start(bf16[512,128]{1,0:T(8,128)(2,1)S(1)} %get-tuple-element.55), channel_id=1, source_target_pairs={{0,8},{1,9},{2,10},{3,11},{4,12},{5,13},{6,14},{7,15},{8,0},{9,1},... | collective-permute-start | bytes 393224 | tf_op jit(solution)/shard_map/ppermute | solution.py:48
  10.9 11.9 %collective-permute-start.2 = (bf16[512,128]{1,0:T(8,128)(2,1)S(1)}, bf16[512,128]{1,0:T(8,128)(2,1)S(1)}, u32[]{:S(2)}, u32[]{:S(2)}) collective-permute-start(bf16[512,128]{1,0:T(8,128)(2,1)S(1)} %get-tuple-element.57), channel_id=1, source_target_pairs={{0,16},{1,17},{2,18},{3,19},{4,20},{5,21},{6,22},{7,23},{8,24},{9,... | collective-permute-start | bytes 393224 | tf_op jit(solution)/shard_map/ppermute | solution.py:48
  12.4 10.4 %collective-permute-start.3 = (bf16[512,128]{1,0:T(8,128)(2,1)S(1)}, bf16[512,128]{1,0:T(8,128)(2,1)S(1)}, u32[]{:S(2)}, u32[]{:S(2)}) collective-permute-start(bf16[512,128]{1,0:T(8,128)(2,1)S(1)} %get-tuple-element.56), channel_id=1, source_target_pairs={{0,24},{1,25},{2,26},{3,27},{4,28},{5,29},{6,30},{7,31},{8,16},{9,... | collective-permute-start | bytes 393224 | tf_op jit(solution)/shard_map/ppermute | solution.py:48
  38.8 24.8 %copy-start.10 = (bf16[2048,128]{1,0:T(8,128)(2,1)}, bf16[2048,128]{1,0:T(8,128)(2,1)S(1)}, u32[]{:S(2)}) copy-start(bf16[2048,128]{1,0:T(8,128)(2,1)S(1)} %all_gather.6.refs_0_) | copy-start | bytes 1572868
  38.8 10.0 %collective-permute-start.4 = (bf16[2048,128]{1,0:T(8,128)(2,1)S(1)}, bf16[2048,128]{1,0:T(8,128)(2,1)S(1)}, u32[]{:S(2)}, u32[]{:S(2)}) collective-permute-start(bf16[2048,128]{1,0:T(8,128)(2,1)S(1)} %all_gather.6.refs_0_), channel_id=1, source_target_pairs={{0,8},{1,9},{2,10},{3,11},{4,20},{5,21},{6,22},{7,23},{8,0},{9,1},... | collective-permute-start | bytes 1572872 | tf_op jit(solution)/shard_map/ppermute | solution.py:81
  48.8 21.4 %copy-start.17 = (bf16[2048,128]{1,0:T(8,128)(2,1)}, bf16[2048,128]{1,0:T(8,128)(2,1)S(1)}, u32[]{:S(2)}) copy-start(bf16[2048,128]{1,0:T(8,128)(2,1)S(1)} %collective-permute-done.4.refs_0_) | copy-start | bytes 1572868
  48.8 9.2 %collective-permute-start.5 = (bf16[2048,128]{1,0:T(8,128)(2,1)S(1)}, bf16[2048,128]{1,0:T(8,128)(2,1)S(1)}, u32[]{:S(2)}, u32[]{:S(2)}) collective-permute-start(bf16[2048,128]{1,0:T(8,128)(2,1)S(1)} %collective-permute-done.4.refs_0_), channel_id=1, source_target_pairs={{0,16},{1,17},{2,18},{3,19},{4,12},{5,13},{6,14},{7,15},{8,24},{9,... | collective-permute-start | bytes 1572872 | tf_op jit(solution)/shard_map/ppermute | solution.py:81
  50.4 13.3 %collective-permute-start.9 = (bf16[2048,128]{1,0:T(8,128)(2,1)S(1)}, bf16[2048,128]{1,0:T(8,128)(2,1)S(1)}, u32[]{:S(2)}, u32[]{:S(2)}) collective-permute-start(bf16[2048,128]{1,0:T(8,128)(2,1)S(1)} %all_gather.6.refs_0_), channel_id=1, source_target_pairs={{0,16},{1,17},{2,18},{3,19},{4,12},{5,13},{6,14},{7,15},{8,24},{9,... | collective-permute-start | bytes 1572872 | tf_op jit(solution)/shard_map/ppermute | solution.py:81
  50.9 12.8 %collective-permute-start.7 = (bf16[2048,128]{1,0:T(8,128)(2,1)S(1)}, bf16[2048,128]{1,0:T(8,128)(2,1)S(1)}, u32[]{:S(2)}, u32[]{:S(2)}) collective-permute-start(bf16[2048,128]{1,0:T(8,128)(2,1)S(1)} %all_gather.6.refs_0_), channel_id=1, source_target_pairs={{0,4},{1,5},{2,6},{3,7},{4,0},{5,1},{6,2},{7,3},{8,12},{9,13},{10,... | collective-permute-start | bytes 1572872 | tf_op jit(solution)/shard_map/ppermute | solution.py:48
  58.0 12.3 %copy-start.19 = (bf16[2048,128]{1,0:T(8,128)(2,1)}, bf16[2048,128]{1,0:T(8,128)(2,1)S(1)}, u32[]{:S(2)}) copy-start(bf16[2048,128]{1,0:T(8,128)(2,1)S(1)} %collective-permute-done.5.refs_0_) | copy-start | bytes 1572868
  58.0 12.8 %collective-permute-start.6 = (bf16[2048,128]{1,0:T(8,128)(2,1)S(1)}, bf16[2048,128]{1,0:T(8,128)(2,1)}, u32[]{:S(2)}, u32[]{:S(2)}) collective-permute-start(bf16[2048,128]{1,0:T(8,128)(2,1)S(1)} %collective-permute-done.5.refs_0_), channel_id=1, source_target_pairs={{0,4},{1,5},{2,6},{3,7},{4,0},{5,1},{6,2},{7,3},{8,12},{9,13},{10,... | collective-permute-start | bytes 1572872 | tf_op jit(solution)/shard_map/ppermute | solution.py:48
  58.7 17.9 %collective-permute-start.10 = (bf16[2048,128]{1,0:T(8,128)(2,1)S(1)}, bf16[2048,128]{1,0:T(8,128)(2,1)S(1)}, u32[]{:S(2)}, u32[]{:S(2)}) collective-permute-start(bf16[2048,128]{1,0:T(8,128)(2,1)S(1)} %collective-permute-done.4.refs_0_), channel_id=1, source_target_pairs={{0,4},{1,5},{2,6},{3,7},{4,0},{5,1},{6,2},{7,3},{8,12},{9,13},{10,... | collective-permute-start | bytes 1572872 | tf_op jit(solution)/shard_map/ppermute | solution.py:48
  63.6 13.0 %collective-permute-start.11 = (bf16[2048,128]{1,0:T(8,128)(2,1)S(1)}, bf16[2048,128]{1,0:T(8,128)(2,1)}, u32[]{:S(2)}, u32[]{:S(2)}) collective-permute-start(bf16[2048,128]{1,0:T(8,128)(2,1)S(1)} %collective-permute-done.9.refs_1_), channel_id=1, source_target_pairs={{0,4},{1,5},{2,6},{3,7},{4,0},{5,1},{6,2},{7,3},{8,12},{9,13},{10,... | collective-permute-start | bytes 1572872 | tf_op jit(solution)/shard_map/ppermute | solution.py:48
  70.3 27.4 %collective-permute-start.8 = (bf16[128,2176]{1,0:T(8,128)(2,1)}, bf16[128,2176]{1,0:T(8,128)(2,1)S(1)}, u32[]{:S(2)}, u32[]{:S(2)}) collective-permute-start(bf16[128,2176]{1,0:T(8,128)(2,1)} %get-tuple-element.33), channel_id=1, source_target_pairs={{0,4},{1,5},{2,6},{3,7},{4,0},{5,1},{6,2},{7,3},{8,12},{9,13},{10,... | collective-permute-start | bytes 1671176 | tf_op jit(solution)/shard_map/ppermute | solution.py:48
  76.5 9.7 %collective-permute-start.15 = (bf16[128,2176]{1,0:T(8,128)(2,1)}, bf16[128,2176]{1,0:T(8,128)(2,1)S(1)}, u32[]{:S(2)}, u32[]{:S(2)}) collective-permute-start(bf16[128,2176]{1,0:T(8,128)(2,1)} %get-tuple-element.39), channel_id=1, source_target_pairs={{0,4},{1,5},{2,6},{3,7},{4,0},{5,1},{6,2},{7,3},{8,12},{9,13},{10,... | collective-permute-start | bytes 1671176 | tf_op jit(solution)/shard_map/ppermute | solution.py:48
  85.7 4.8 %collective-permute-start.14 = (bf16[128,2176]{1,0:T(8,128)(2,1)}, bf16[128,2176]{1,0:T(8,128)(2,1)S(1)}, u32[]{:S(2)}, u32[]{:S(2)}) collective-permute-start(bf16[128,2176]{1,0:T(8,128)(2,1)} %get-tuple-element.37), channel_id=1, source_target_pairs={{0,4},{1,5},{2,6},{3,7},{4,0},{5,1},{6,2},{7,3},{8,12},{9,13},{10,... | collective-permute-start | bytes 1671176 | tf_op jit(solution)/shard_map/ppermute | solution.py:48
  86.1 2.6 %collective-permute-start.12 = (bf16[128,2176]{1,0:T(8,128)(2,1)}, bf16[128,2176]{1,0:T(8,128)(2,1)S(1)}, u32[]{:S(2)}, u32[]{:S(2)}) collective-permute-start(bf16[128,2176]{1,0:T(8,128)(2,1)} %get-tuple-element.35), channel_id=1, source_target_pairs={{0,4},{1,5},{2,6},{3,7},{4,0},{5,1},{6,2},{7,3},{8,12},{9,13},{10,... | collective-permute-start | bytes 1671176 | tf_op jit(solution)/shard_map/ppermute | solution.py:48
  86.4 9.6 %collective-permute-start.16 = (bf16[128,2176]{1,0:T(8,128)(2,1)S(1)}, bf16[128,2176]{1,0:T(8,128)(2,1)S(1)}, u32[]{:S(2)}, u32[]{:S(2)}) collective-permute-start(bf16[128,2176]{1,0:T(8,128)(2,1)S(1)} %add_convert_fusion.1), channel_id=1, source_target_pairs={{0,16},{1,17},{2,18},{3,19},{4,12},{5,13},{6,14},{7,15},{8,24},{9,... | collective-permute-start | bytes 1671176 | tf_op jit(solution)/shard_map/ppermute | solution.py:81
  88.9 16.6 %collective-permute-start.13 = (bf16[128,2176]{1,0:T(8,128)(2,1)S(1)}, bf16[128,2176]{1,0:T(8,128)(2,1)S(1)}, u32[]{:S(2)}, u32[]{:S(2)}) collective-permute-start(bf16[128,2176]{1,0:T(8,128)(2,1)S(1)} %add_convert_fusion.2), channel_id=1, source_target_pairs={{0,16},{1,17},{2,18},{3,19},{4,12},{5,13},{6,14},{7,15},{8,24},{9,... | collective-permute-start | bytes 1671176 | tf_op jit(solution)/shard_map/ppermute | solution.py:81
  96.2 11.2 %collective-permute-start.17 = (bf16[128,2176]{1,0:T(8,128)(2,1)S(1)}, bf16[128,2176]{1,0:T(8,128)(2,1)S(1)}, u32[]{:S(2)}, u32[]{:S(2)}) collective-permute-start(bf16[128,2176]{1,0:T(8,128)(2,1)S(1)} %add_convert_fusion), channel_id=1, source_target_pairs={{0,8},{1,9},{2,10},{3,11},{4,20},{5,21},{6,22},{7,23},{8,0},{9,1},... | collective-permute-start | bytes 1671176 | tf_op jit(solution)/shard_map/ppermute | solution.py:81
  111.7 10.9 %collective-permute-start.18 = (bf16[32,2176]{1,0:T(8,128)(2,1)}, bf16[32,2176]{1,0:T(8,128)(2,1)S(1)}, u32[]{:S(2)}, u32[]{:S(2)}) collective-permute-start(bf16[32,2176]{1,0:T(8,128)(2,1)} %get-tuple-element.41), channel_id=1, source_target_pairs={{0,1},{1,2},{2,3},{3,0},{4,5},{5,6},{6,7},{7,4},{8,9},{9,10},{10,1... | collective-permute-start | bytes 417800 | tf_op jit(solution)/shard_map/ppermute | solution.py:64
  115.8 12.4 %collective-permute-start.19 = (bf16[32,2176]{1,0:T(8,128)(2,1)}, bf16[32,2176]{1,0:T(8,128)(2,1)S(1)}, u32[]{:S(2)}, u32[]{:S(2)}) collective-permute-start(bf16[32,2176]{1,0:T(8,128)(2,1)} %get-tuple-element.42), channel_id=1, source_target_pairs={{0,2},{1,3},{2,0},{3,1},{4,6},{5,7},{6,4},{7,5},{8,10},{9,11},{10,... | collective-permute-start | bytes 417800 | tf_op jit(solution)/shard_map/ppermute | solution.py:64
  118.4 9.9 %collective-permute-start.20 = (bf16[32,2176]{1,0:T(8,128)(2,1)}, bf16[32,2176]{1,0:T(8,128)(2,1)S(1)}, u32[]{:S(2)}, u32[]{:S(2)}) collective-permute-start(bf16[32,2176]{1,0:T(8,128)(2,1)} %get-tuple-element.43), channel_id=1, source_target_pairs={{0,3},{1,0},{2,1},{3,2},{4,7},{5,4},{6,5},{7,6},{8,11},{9,8},{10,9... | collective-permute-start | bytes 417800 | tf_op jit(solution)/shard_map/ppermute | solution.py:64
  145.5 16.9 %copy-start.5 = (bf16[128,2176]{1,0:T(8,128)(2,1)}, bf16[128,2176]{1,0:T(8,128)(2,1)S(1)}, u32[]{:S(2)}) copy-start(bf16[128,2176]{1,0:T(8,128)(2,1)S(1)} %all_gather.7.refs_0_) | copy-start | bytes 1671172
  145.5 15.5 %collective-permute-start.21 = (bf16[128,2176]{1,0:T(8,128)(2,1)S(1)}, bf16[128,2176]{1,0:T(8,128)(2,1)S(1)}, u32[]{:S(2)}, u32[]{:S(2)}) collective-permute-start(bf16[128,2176]{1,0:T(8,128)(2,1)S(1)} %all_gather.7.refs_0_), channel_id=1, source_target_pairs={{0,8},{1,9},{2,10},{3,11},{4,20},{5,21},{6,22},{7,23},{8,0},{9,1},... | collective-permute-start | bytes 1671176 | tf_op jit(solution)/shard_map/ppermute | solution.py:81
  147.0 14.1 %collective-permute-start.24 = (bf16[128,2176]{1,0:T(8,128)(2,1)S(1)}, bf16[128,2176]{1,0:T(8,128)(2,1)S(1)}, u32[]{:S(2)}, u32[]{:S(2)}) collective-permute-start(bf16[128,2176]{1,0:T(8,128)(2,1)S(1)} %all_gather.7.refs_0_), channel_id=1, source_target_pairs={{0,16},{1,17},{2,18},{3,19},{4,12},{5,13},{6,14},{7,15},{8,24},{9,... | collective-permute-start | bytes 1671176 | tf_op jit(solution)/shard_map/ppermute | solution.py:81
  148.5 13.1 %collective-permute-start.27 = (bf16[128,2176]{1,0:T(8,128)(2,1)S(1)}, bf16[128,2176]{1,0:T(8,128)(2,1)S(1)}, u32[]{:S(2)}, u32[]{:S(2)}) collective-permute-start(bf16[128,2176]{1,0:T(8,128)(2,1)S(1)} %all_gather.7.refs_0_), channel_id=1, source_target_pairs={{0,4},{1,5},{2,6},{3,7},{4,0},{5,1},{6,2},{7,3},{8,12},{9,13},{10,... | collective-permute-start | bytes 1671176 | tf_op jit(solution)/shard_map/ppermute | solution.py:48
  161.0 9.5 %collective-permute-start.22 = (bf16[128,2176]{1,0:T(8,128)(2,1)S(1)}, bf16[128,2176]{1,0:T(8,128)(2,1)S(1)}, u32[]{:S(2)}, u32[]{:S(2)}) collective-permute-start(bf16[128,2176]{1,0:T(8,128)(2,1)S(1)} %collective-permute-done.21.refs_0_), channel_id=1, source_target_pairs={{0,16},{1,17},{2,18},{3,19},{4,12},{5,13},{6,14},{7,15},{8,24},{9,... | collective-permute-start | bytes 1671176 | tf_op jit(solution)/shard_map/ppermute | solution.py:81
  161.1 9.5 %collective-permute-start.25 = (bf16[128,2176]{1,0:T(8,128)(2,1)S(1)}, bf16[128,2176]{1,0:T(8,128)(2,1)S(1)}, u32[]{:S(2)}, u32[]{:S(2)}) collective-permute-start(bf16[128,2176]{1,0:T(8,128)(2,1)S(1)} %collective-permute-done.21.refs_0_), channel_id=1, source_target_pairs={{0,4},{1,5},{2,6},{3,7},{4,0},{5,1},{6,2},{7,3},{8,12},{9,13},{10,... | collective-permute-start | bytes 1671176 | tf_op jit(solution)/shard_map/ppermute | solution.py:48
  161.1 9.5 %collective-permute-start.26 = (bf16[128,2176]{1,0:T(8,128)(2,1)S(1)}, bf16[128,2176]{1,0:T(8,128)(2,1)S(1)}, u32[]{:S(2)}, u32[]{:S(2)}) collective-permute-start(bf16[128,2176]{1,0:T(8,128)(2,1)S(1)} %collective-permute-done.24.refs_1_), channel_id=1, source_target_pairs={{0,4},{1,5},{2,6},{3,7},{4,0},{5,1},{6,2},{7,3},{8,12},{9,13},{10,... | collective-permute-start | bytes 1671176 | tf_op jit(solution)/shard_map/ppermute | solution.py:48
  170.6 10.3 %collective-permute-start.23 = (bf16[128,2176]{1,0:T(8,128)(2,1)S(1)}, bf16[128,2176]{1,0:T(8,128)(2,1)S(1)}, u32[]{:S(2)}, u32[]{:S(2)}) collective-permute-start(bf16[128,2176]{1,0:T(8,128)(2,1)S(1)} %collective-permute-done.22.refs_0_), channel_id=1, source_target_pairs={{0,4},{1,5},{2,6},{3,7},{4,0},{5,1},{6,2},{7,3},{8,12},{9,13},{10,... | collective-permute-start | bytes 1671176 | tf_op jit(solution)/shard_map/ppermute | solution.py:48
  (18 other events, 79.6 us)
where the time goes:
time: 189 us; the launch traced here: 188 us
  waiting for transfers between devices  61.1 us (32%)
  Pallas kernels  55.3 us (29%)
  blocking collectives  32.2 us (17%)
  starting transfers between devices  25.1 us (13%)
  local copies, waits for them, and re-layouts  7.93 us (4%)
  other arithmetic  5.45 us (3%)
    ppermute x9, waiting for transfers between devices, cross(): return lax.ppermute(x, AXES, pairs)  48.9 us
    pallas_call x3, Pallas kernels, last_call(): pl.pallas_call(functools.partial(last_body, count, multiplier, cap, base,...  21.8 us
    pallas_call x3, Pallas kernels, first_call(): pl.pallas_call(functools.partial(first_body, count), grid_spec=pltpu.Pref...  19.6 us
    all_gather x1, blocking collectives, step(): lax.all_gather(mine_sum.astype(jnp.bfloat16), 'shard', axis=0, tiled=True)  16.3 us
    all_gather x1, blocking collectives, step(): q_full = lax.all_gather(q_own, 'shard', axis=0, tiled=True)  15.9 us
    ppermute x9, starting transfers between devices, cross(): return lax.ppermute(x, AXES, pairs)  11.3 us
    pallas_call x1, Pallas kernels, add_call(): pl.pallas_call(add_body, grid=(experts,), in_specs=[block, block], out_sp...  10.4 us
    ppermute x3, waiting for transfers between devices, shift_shard(): return lax.ppermute(x, AXES, pairs)  9.88 us
  transfers between devices with their start and end apart: 28, of which 12 were waited for; matrix products, arithmetic and copies ran while one was open for 1% of the time, Pallas kernels for 24%

commit v1 on v0

--- a/solution.py
+++ b/solution.py
@@ -14,6 +14,7 @@
 DOWN = 2.0**-64
 UP = 2.0**64
 WEIGHT = 8
+GRANT = 28 * 2**20
 AXES = ("group", "shard")
 
 
@@ -105,10 +106,10 @@
 
 def add_call(momentum, gradient):
     experts, rows, hidden = momentum.shape
-    block = pl.BlockSpec((1, rows, hidden), lambda i: (i, 0, 0))
+    block = pl.BlockSpec((2, rows, hidden), lambda i: (i, 0, 0))
     return pl.pallas_call(
         add_body,
-        grid=(experts,),
+        grid=(experts // 2,),
         in_specs=[block, block],
         out_specs=block,
         out_shape=jax.ShapeDtypeStruct(momentum.shape, jnp.bfloat16),
@@ -117,6 +118,7 @@
             bytes_accessed=6 * momentum.size,
             transcendentals=0,
         ),
+        compiler_params=pltpu.CompilerParams(vmem_limit_bytes=GRANT),
         name="add",
     )(momentum, gradient)
 
@@ -141,39 +143,30 @@
         grid_spec=pltpu.PrefetchScalarGridSpec(
             num_scalar_prefetch=1,
             grid=(1,),
-            in_specs=[fixed((rank, hidden))] * len(terms),
-            out_specs=[fixed((piece, hidden))] * shard_count,
+            in_specs=[pl.BlockSpec(memory_space=pltpu.VMEM)] * len(terms),
+            out_specs=[pl.BlockSpec(memory_space=pltpu.VMEM)] * shard_count,
             scratch_shapes=[pltpu.VMEM((rank, hidden), jnp.float32)],
         ),
         out_shape=[jax.ShapeDtypeStruct((piece, hidden), jnp.bfloat16)] * shard_count,
+        compiler_params=pltpu.CompilerParams(vmem_limit_bytes=GRANT),
         name="split",
     )(where, *terms)
 
 
-def load(refs, buf, sems):
-    step = pl.program_id(0)
-
-    @pl.when(step == 0)
-    def _():
-        for j, ref in enumerate(refs):
-            pltpu.make_async_copy(ref, buf.at[j], sems.at[j]).start()
-
-    for j, ref in enumerate(refs):
-
-        @pl.when(step == j)
-        def _():
-            pltpu.make_async_copy(ref, buf.at[j], sems.at[j]).wait()
-
-    return buf[step]
+def pick(refs):
+    value = refs[0][...]
+    for j in range(1, len(refs)):
+        value = jnp.where(pl.program_id(0) == j, refs[j][...], value)
+    return value
 
 
 def first_body(count, where, c_ref, *refs):
     q_refs, refs = refs[:count], refs[count:]
-    left_ref, right_refs, (buf, sems) = refs[0], refs[1:-2], refs[-2:]
+    left_ref, right_refs = refs[0], refs[1:]
     hidden = c_ref.shape[2]
     step = pl.program_id(0)
     combined = c_ref[0]
-    q = load(q_refs, buf, sems)
+    q = pick(q_refs)
     left = jnp.dot(combined, q, preferred_element_type=jnp.float32)
     left_ref[0] = left
     squares = jnp.sum(left * left, axis=0, keepdims=True)
@@ -204,13 +197,9 @@
             num_scalar_prefetch=1,
             grid=(count,),
             in_specs=[pl.BlockSpec((1, rows, hidden), lambda i, w: (w[0, base + i], 0, 0))]
-            + [pl.BlockSpec(memory_space=pl.ANY)] * count,
+            + [pl.BlockSpec(memory_space=pltpu.VMEM)] * count,
             out_specs=[pl.BlockSpec((1, rows, rank), lambda i, w: (i, 0, 0))]
-            + [fixed((rank, hidden + rank))] * count,
-            scratch_shapes=[
-                pltpu.VMEM((count, hidden, rank), jnp.bfloat16),
-                pltpu.SemaphoreType.DMA((count,)),
-            ],
+            + [pl.BlockSpec(memory_space=pltpu.VMEM)] * count,
         ),
         out_shape=[jax.ShapeDtypeStruct((count, rows, rank), jnp.float32)]
         + [jax.ShapeDtypeStruct((rank, hidden + rank), jnp.bfloat16)] * count,
@@ -219,6 +208,7 @@
             bytes_accessed=count * 2 * (rows + 2 * rank) * hidden,
             transcendentals=0,
         ),
+        compiler_params=pltpu.CompilerParams(vmem_limit_bytes=GRANT),
         name="first",
     )(where, combined, *qs)
     return outs[0], outs[1:]
@@ -226,7 +216,7 @@
 
 def last_body(count, multiplier, cap, base, fresh, where, c_ref, left_ref, *refs):
     right_refs, refs = refs[:count], refs[count:]
-    mom_ref, upd_ref, q_ref, buf, sems = refs[-5:]
+    mom_ref, upd_ref, q_ref, buf = refs[-4:]
     step = pl.program_id(0)
 
     @pl.when(step == 0)
@@ -237,7 +227,8 @@
             q_ref[...] = refs[0][...]
 
     hidden = c_ref.shape[2]
-    arrived = load(right_refs, buf, sems)
+    arrived = pick(right_refs)
+    buf[...] = arrived
     squares = arrived[:, hidden : hidden + 1].astype(jnp.float32)
     n_col = lax.rsqrt(squares + stability_offset)
     n_row = jnp.broadcast_to(n_col, (n_col.shape[0],) * 2).T[0:1, :]
@@ -258,7 +249,7 @@
     def _():
         share = q_ref.shape[1]
         start = pl.multiple_of(where[2, 0] * share, share)
-        own = buf[step, :, pl.ds(start, share)].astype(jnp.float32) * n_col * scale
+        own = buf[:, pl.ds(start, share)].astype(jnp.float32) * n_col * scale
         q_ref[slot] = own.T.astype(jnp.bfloat16)
 
 
@@ -278,13 +269,10 @@
                 block,
                 pl.BlockSpec((1, rows, rank), lambda i, w: (i, 0, 0)),
             ]
-            + [pl.BlockSpec(memory_space=pl.ANY)] * count
+            + [pl.BlockSpec(memory_space=pltpu.VMEM)] * count
             + ([] if outs is None else [fixed((cap, share, rank)), anywhere, anywhere]),
             out_specs=[block, block, fixed((cap, share, rank))],
-            scratch_shapes=[
-                pltpu.VMEM((count, rank, width), jnp.bfloat16),
-                pltpu.SemaphoreType.DMA((count,)),
-            ],
+            scratch_shapes=[pltpu.VMEM((rank, width), jnp.bfloat16)],
         ),
         out_shape=[
             jax.ShapeDtypeStruct((experts, rows, hidden), jnp.bfloat16),
@@ -297,6 +285,7 @@
             bytes_accessed=count * 2 * (3 * rows + 2 * rank) * hidden,
             transcendentals=0,
         ),
+        compiler_params=pltpu.CompilerParams(vmem_limit_bytes=GRANT),
         name="last",
     )(where, combined, left, *rights, *extra)
 
@@ -349,7 +338,7 @@
     for part, r in zip(parts[1:], uppers[1:]):
         q_own = q_own + links.swap_group(part, r)
     combined = add_call(momentum, gradient)
-    q_own, combined = lax.optimization_barrier((q_own, combined))
+    q_own, combined, where = lax.optimization_barrier((q_own, combined, where))
     q_full = lax.all_gather(q_own, "shard", axis=0, tiled=True)
     qs = links.spread(q_full)
     qs_far = {name: links.swap_group(piece, near) for name, piece in qs.items()}

time: 189 us -> 166 us (0.88)
  Pallas kernels: 55.3 us -> 24.5 us
  waiting for transfers between devices: 61.1 us -> 70.4 us
    pallas_call x3, Pallas kernels: 19.6 us -> 8.42 us  [first_call(): pl.pallas_call(functools.partial(first_body, count), grid_spec=pltpu.Pref...]
    pallas_call x1, Pallas kernels: 10.4 us -> 1.71 us  [add_call(): pl.pallas_call(add_body, grid=(experts // 2,), in_specs=[block, block], o...]
    pallas_call x3, Pallas kernels: 21.8 us -> 13.3 us  [last_call(): pl.pallas_call(functools.partial(last_body, count, multiplier, cap, base,...]
    ppermute x9, waiting for transfers between devices: 48.9 us -> 53.8 us  [cross(): return lax.ppermute(x, AXES, pairs)]
    ppermute x16, waiting for transfers between devices: 2.33 us -> 6.93 us  [swap_group(): return lax.ppermute(x, AXES, pairs)]
    pallas_call x1, Pallas kernels: 3.5 us -> 1.09 us  [split_call(): pl.pallas_call(functools.partial(split_body, shard_count), grid_spec=pltp...]
    unnamed x44 -> x8, local copies, waits for them, and re-layouts: 5.26 us -> 6.19 us
  transfers between devices with their start and end apart: 28 -> 28, of which waited for: 12 -> 13; matrix products, arithmetic and copies ran while one was open for 1% -> 1% of each run, Pallas kernels for 24% -> 12%
where the time goes in v1:
time: 166 us
  waiting for transfers between devices  70.4 us (42%)
  blocking collectives  31.7 us (19%)
  starting transfers between devices  25.6 us (15%)
  Pallas kernels  24.5 us (15%)
  local copies, waits for them, and re-layouts  8.85 us (5%)
  other arithmetic  3.9 us (2%)
    ppermute x9, waiting for transfers between devices, cross(): return lax.ppermute(x, AXES, pairs)  53.8 us
    all_gather x1, blocking collectives, step(): lax.all_gather(mine_sum.astype(jnp.bfloat16), 'shard', axis=0, tiled=True)  16.3 us
    all_gather x1, blocking collectives, step(): q_full = lax.all_gather(q_own, 'shard', axis=0, tiled=True)  15.4 us
    pallas_call x3, Pallas kernels, last_call(): pl.pallas_call(functools.partial(last_body, count, multiplier, cap, base,...  13.3 us
    ppermute x9, starting transfers between devices, cross(): return lax.ppermute(x, AXES, pairs)  11.5 us
    ppermute x3, waiting for transfers between devices, shift_shard(): return lax.ppermute(x, AXES, pairs)  9.68 us
    pallas_call x3, Pallas kernels, first_call(): pl.pallas_call(functools.partial(first_body, count), grid_spec=pltpu.Pref...  8.42 us
    ppermute x3, starting transfers between devices, shift_shard(): return lax.ppermute(x, AXES, pairs)  7.13 us
  transfers between devices with their start and end apart: 28, of which 13 were waited for; matrix products, arithmetic and copies ran while one was open for 1% of the time, Pallas kernels for 12%

profile of v1, /device:TPU:0, one launch (start us, length us, event | category | flops | bytes accessed | tf_op | source)
XLA Modules:
  0.0 165.7 jit_solution(2412984857000727086)
XLA Ops:
  7.1 3.1 %copy-done.1 = bf16[8,224,2048]{2,1,0:T(8,128)(2,1)S(1)} copy-done((bf16[8,224,2048]{2,1,0:T(8,128)(2,1)S(1)}, bf16[8,224,2048]{2,1,0:T(8,128)(2,1)}, u32[]{:S(2)}) %copy-start.1) | copy-done | bytes 7340056
  10.2 3.1 %copy-done.2 = bf16[8,224,2048]{2,1,0:T(8,128)(2,1)S(1)} copy-done((bf16[8,224,2048]{2,1,0:T(8,128)(2,1)S(1)}, bf16[8,224,2048]{2,1,0:T(8,128)(2,1)}, u32[]{:S(2)}) %copy-start.2) | copy-done | bytes 7340056
  13.3 1.7 %add.131.c_ref = bf16[8,224,2048]{2,1,0:T(8,128)(2,1)S(1)} custom-call(bf16[8,224,2048]{2,1,0:T(8,128)(2,1)S(1)} %copy-done.1, bf16[8,224,2048]{2,1,0:T(8,128)(2,1)S(1)} %copy-done.2), custom_call_target="tpu_custom_call" | custom-call | flops 7516192768 | bytes 22020096 | tf_op jit(solution)/shard_map/add/pallas_call | solution.py:110
  15.1 2.6 %collective-permute-start.1 = (bf16[512,128]{1,0:T(8,128)(2,1)S(1)}, bf16[512,128]{1,0:T(8,128)(2,1)S(1)}, u32[]{:S(2)}, u32[]{:S(2)}) collective-permute-start(bf16[512,128]{1,0:T(8,128)(2,1)S(1)} %get-tuple-element.57), channel_id=1, source_target_pairs={{0,8},{1,9},{2,10},{3,11},{4,12},{5,13},{6,14},{7,15},{8,0},{9,1},... | collective-permute-start | bytes 393224 | tf_op jit(solution)/shard_map/ppermute | solution.py:49
  19.3 2.7 %collective-permute-done.1 = bf16[512,128]{1,0:T(8,128)(2,1)S(1)} collective-permute-done((bf16[512,128]{1,0:T(8,128)(2,1)S(1)}, bf16[512,128]{1,0:T(8,128)(2,1)S(1)}, u32[]{:S(2)}, u32[]{:S(2)}) %collective-permute-start.1) | collective-permute-done | bytes 131104 | tf_op jit(solution)/shard_map/ppermute | solution.py:49
  22.0 4.1 %collective-permute-done.2 = bf16[512,128]{1,0:T(8,128)(2,1)S(1)} collective-permute-done((bf16[512,128]{1,0:T(8,128)(2,1)S(1)}, bf16[512,128]{1,0:T(8,128)(2,1)S(1)}, u32[]{:S(2)}, u32[]{:S(2)}) %collective-permute-start.2) | collective-permute-done | bytes 131104 | tf_op jit(solution)/shard_map/ppermute | solution.py:49
  26.1 15.4 %all_gather.6.refs_0_ = bf16[2048,128]{1,0:T(8,128)(2,1)S(1)} all-gather(bf16[512,128]{1,0:T(8,128)(2,1)S(1)} %fusion.6), channel_id=1, replica_groups=mesh['group'=8,'shard'=4] {'shard'}, dimensions={0}, use_global_device_ids=true | all-gather | bytes 655360 | tf_op jit(solution)/shard_map/all_gather | solution.py:342
  41.5 1.6 collective-permute-start.4
  43.2 8.0 %collective-permute-done.4.refs_0_ = bf16[2048,128]{1,0:T(8,128)(2,1)S(1)} collective-permute-done((bf16[2048,128]{1,0:T(8,128)(2,1)S(1)}, bf16[2048,128]{1,0:T(8,128)(2,1)S(1)}, u32[]{:S(2)}, u32[]{:S(2)}) %collective-permute-start.4) | collective-permute-done | bytes 524320 | tf_op jit(solution)/shard_map/ppermute | solution.py:82
  51.1 2.1 %collective-permute-start.5 = (bf16[2048,128]{1,0:T(8,128)(2,1)S(1)}, bf16[2048,128]{1,0:T(8,128)(2,1)S(1)}, u32[]{:S(2)}, u32[]{:S(2)}) collective-permute-start(bf16[2048,128]{1,0:T(8,128)(2,1)S(1)} %collective-permute-done.4.refs_0_), channel_id=1, source_target_pairs={{0,16},{1,17},{2,18},{3,19},{4,12},{5,13},{6,14},{7,15},{8,24},{9,... | collective-permute-start | bytes 1572872 | tf_op jit(solution)/shard_map/ppermute | solution.py:82
  53.2 7.1 %collective-permute-done.5.refs_0_ = bf16[2048,128]{1,0:T(8,128)(2,1)S(1)} collective-permute-done((bf16[2048,128]{1,0:T(8,128)(2,1)S(1)}, bf16[2048,128]{1,0:T(8,128)(2,1)S(1)}, u32[]{:S(2)}, u32[]{:S(2)}) %collective-permute-start.5) | collective-permute-done | bytes 524320 | tf_op jit(solution)/shard_map/ppermute | solution.py:82
  60.9 5.1 %collective-permute-done.9.refs_1_ = bf16[2048,128]{1,0:T(8,128)(2,1)S(1)} collective-permute-done((bf16[2048,128]{1,0:T(8,128)(2,1)S(1)}, bf16[2048,128]{1,0:T(8,128)(2,1)S(1)}, u32[]{:S(2)}, u32[]{:S(2)}) %collective-permute-start.9) | collective-permute-done | bytes 524320 | tf_op jit(solution)/shard_map/ppermute | solution.py:82
  66.0 2.2 %first.4 = (f32[2,224,128]{2,1,0:T(8,128)S(1)}, bf16[128,2176]{1,0:T(8,128)(2,1)S(1)}, bf16[128,2176]{1,0:T(8,128)(2,1)S(1)}) custom-call(s32[3,8]{1,0:T(4,128)S(1)} %add_add_fusion.where, bf16[8,224,2048]{2,1,0:T(8,128)(2,1)S(1)} %add.131.c_ref, bf16[2048,128]{1,0:T(8,128)(2,1)S(1)} %all_gather.6.refs_0_, bf16[2048,128]{1,0:T(8,128)(2,1)S(1)} %collective-permute-done.7.refs_1_), custom_call_target="tpu_custom_call" | custom-call | flops 3758096384 | bytes 3932160 | tf_op jit(solution)/shard_map/first/pallas_call | solution.py:194
  68.8 2.2 %first.3 = (f32[2,224,128]{2,1,0:T(8,128)S(1)}, bf16[128,2176]{1,0:T(8,128)(2,1)S(1)}, bf16[128,2176]{1,0:T(8,128)(2,1)S(1)}) custom-call(s32[3,8]{1,0:T(4,128)S(1)} %add_add_fusion.where, bf16[8,224,2048]{2,1,0:T(8,128)(2,1)S(1)} %add.131.c_ref, bf16[2048,128]{1,0:T(8,128)(2,1)S(1)} %collective-permute-done.5.refs_0_, ...), custom_call_target="tpu_custom_call" | custom-call | flops 3758096384 | bytes 3932160 | tf_op jit(solution)/shard_map/first/pallas_call | solution.py:194
  71.1 4.0 %first.5 = (f32[4,224,128]{2,1,0:T(8,128)S(1)}, bf16[128,2176]{1,0:T(8,128)(2,1)S(1)}, bf16[128,2176]{1,0:T(8,128)(2,1)S(1)}, bf16[128,2176]{1,0:T(8,128)(2,1)S(1)}, bf16[128,2176]{1,0:T(8,128)(2,1)S(1)}) custom-call(s32[3,8]{1,0:T(4,128)S(1)} %add_add_fusion.where, bf16[8,224,2048]{2,1,0:T(8,128)(2,1)S(1)} %add.131.c_ref, ...), custom_call_target="tpu_custom_call" | custom-call | flops 7516192768 | bytes 7864320 | tf_op jit(solution)/shard_map/first/pallas_call | solution.py:194
  75.9 2.1 %collective-permute-start.16 = (bf16[128,2176]{1,0:T(8,128)(2,1)S(1)}, bf16[128,2176]{1,0:T(8,128)(2,1)S(1)}, u32[]{:S(2)}, u32[]{:S(2)}) collective-permute-start(bf16[128,2176]{1,0:T(8,128)(2,1)S(1)} %add_convert_fusion.1), channel_id=1, source_target_pairs={{0,16},{1,17},{2,18},{3,19},{4,12},{5,13},{6,14},{7,15},{8,24},{9,... | collective-permute-start | bytes 1671176 | tf_op jit(solution)/shard_map/ppermute | solution.py:82
  78.2 2.1 %collective-permute-start.13 = (bf16[128,2176]{1,0:T(8,128)(2,1)S(1)}, bf16[128,2176]{1,0:T(8,128)(2,1)S(1)}, u32[]{:S(2)}, u32[]{:S(2)}) collective-permute-start(bf16[128,2176]{1,0:T(8,128)(2,1)S(1)} %add_convert_fusion.2), channel_id=1, source_target_pairs={{0,16},{1,17},{2,18},{3,19},{4,12},{5,13},{6,14},{7,15},{8,24},{9,... | collective-permute-start | bytes 1671176 | tf_op jit(solution)/shard_map/ppermute | solution.py:82
  80.2 5.2 %collective-permute-done.16 = bf16[128,2176]{1,0:T(8,128)(2,1)S(1)} collective-permute-done((bf16[128,2176]{1,0:T(8,128)(2,1)S(1)}, bf16[128,2176]{1,0:T(8,128)(2,1)S(1)}, u32[]{:S(2)}, u32[]{:S(2)}) %collective-permute-start.16) | collective-permute-done | bytes 557088 | tf_op jit(solution)/shard_map/ppermute | solution.py:82
  85.7 1.5 collective-permute-start.17
  87.2 7.5 %collective-permute-done.13.refs_2_ = bf16[128,2176]{1,0:T(8,128)(2,1)S(1)} collective-permute-done((bf16[128,2176]{1,0:T(8,128)(2,1)S(1)}, bf16[128,2176]{1,0:T(8,128)(2,1)S(1)}, u32[]{:S(2)}, u32[]{:S(2)}) %collective-permute-start.13) | collective-permute-done | bytes 557088 | tf_op jit(solution)/shard_map/ppermute | solution.py:82
  94.7 2.2 %collective-permute-done.17.refs_3_ = bf16[128,2176]{1,0:T(8,128)(2,1)S(1)} collective-permute-done((bf16[128,2176]{1,0:T(8,128)(2,1)S(1)}, bf16[128,2176]{1,0:T(8,128)(2,1)S(1)}, u32[]{:S(2)}, u32[]{:S(2)}) %collective-permute-start.17) | collective-permute-done | bytes 557088 | tf_op jit(solution)/shard_map/ppermute | solution.py:82
  97.9 4.6 %collective-permute-start.18 = (bf16[32,2176]{1,0:T(8,128)(2,1)S(1)}, bf16[32,2176]{1,0:T(8,128)(2,1)S(1)}, u32[]{:S(2)}, u32[]{:S(2)}) collective-permute-start(bf16[32,2176]{1,0:T(8,128)(2,1)S(1)} %get-tuple-element.43), channel_id=1, source_target_pairs={{0,1},{1,2},{2,3},{3,0},{4,5},{5,6},{6,7},{7,4},{8,9},{9,10},{10,1... | collective-permute-start | bytes 417800 | tf_op jit(solution)/shard_map/ppermute | solution.py:65
  102.5 2.6 %collective-permute-start.19 = (bf16[32,2176]{1,0:T(8,128)(2,1)S(1)}, bf16[32,2176]{1,0:T(8,128)(2,1)S(1)}, u32[]{:S(2)}, u32[]{:S(2)}) collective-permute-start(bf16[32,2176]{1,0:T(8,128)(2,1)S(1)} %get-tuple-element.44), channel_id=1, source_target_pairs={{0,2},{1,3},{2,0},{3,1},{4,6},{5,7},{6,4},{7,5},{8,10},{9,11},{10,... | collective-permute-start | bytes 417800 | tf_op jit(solution)/shard_map/ppermute | solution.py:65
  105.1 4.1 %collective-permute-done.18 = bf16[32,2176]{1,0:T(8,128)(2,1)S(1)} collective-permute-done((bf16[32,2176]{1,0:T(8,128)(2,1)S(1)}, bf16[32,2176]{1,0:T(8,128)(2,1)S(1)}, u32[]{:S(2)}, u32[]{:S(2)}) %collective-permute-start.18) | collective-permute-done | bytes 139296 | tf_op jit(solution)/shard_map/ppermute | solution.py:65
  109.1 5.6 %collective-permute-done.19 = bf16[32,2176]{1,0:T(8,128)(2,1)S(1)} collective-permute-done((bf16[32,2176]{1,0:T(8,128)(2,1)S(1)}, bf16[32,2176]{1,0:T(8,128)(2,1)S(1)}, u32[]{:S(2)}, u32[]{:S(2)}) %collective-permute-start.19) | collective-permute-done | bytes 139296 | tf_op jit(solution)/shard_map/ppermute | solution.py:65
  114.8 16.3 %all_gather.7.refs_0_ = bf16[128,2176]{1,0:T(8,128)(2,1)S(1)} all-gather(bf16[32,2176]{1,0:T(8,128)(2,1)S(1)} %add_convert_fusion.3), channel_id=1, replica_groups=mesh['group'=8,'shard'=4] {'shard'}, dimensions={0}, use_global_device_ids=true | all-gather | bytes 696320 | tf_op jit(solution)/shard_map/all_gather | solution.py:363
  131.1 1.6 collective-permute-start.21
  133.2 13.4 %collective-permute-done.21.refs_0_ = bf16[128,2176]{1,0:T(8,128)(2,1)S(1)} collective-permute-done((bf16[128,2176]{1,0:T(8,128)(2,1)S(1)}, bf16[128,2176]{1,0:T(8,128)(2,1)S(1)}, u32[]{:S(2)}, u32[]{:S(2)}) %collective-permute-start.21) | collective-permute-done | bytes 557088 | tf_op jit(solution)/shard_map/ppermute | solution.py:82
  147.1 3.7 %last.3 = (bf16[8,224,2048]{2,1,0:T(8,128)(2,1)}, bf16[8,224,2048]{2,1,0:T(8,128)(2,1)}, bf16[3,512,128]{2,1,0:T(8,128)(2,1)S(1)}) custom-call(s32[3,8]{1,0:T(4,128)S(1)} %add_add_fusion.where, bf16[8,224,2048]{2,1,0:T(8,128)(2,1)S(1)} %add.131.c_ref, f32[2,224,128]{2,1,0:T(8,128)S(1)} %get-tuple-element.47.left_ref, ...), custom_call_target="tpu_custom_call" | custom-call | flops 3758096384 | bytes 7602176 | tf_op jit(solution)/shard_map/last/pallas_call | solution.py:263
  150.9 5.3 %collective-permute-done.22.refs_0_ = bf16[128,2176]{1,0:T(8,128)(2,1)S(1)} collective-permute-done((bf16[128,2176]{1,0:T(8,128)(2,1)S(1)}, bf16[128,2176]{1,0:T(8,128)(2,1)S(1)}, u32[]{:S(2)}, u32[]{:S(2)}) %collective-permute-start.22) | collective-permute-done | bytes 557088 | tf_op jit(solution)/shard_map/ppermute | solution.py:82
  156.1 5.8 %last.4 = (bf16[8,224,2048]{2,1,0:T(8,128)(2,1)}, bf16[8,224,2048]{2,1,0:T(8,128)(2,1)}, bf16[3,512,128]{2,1,0:T(8,128)(2,1)S(1)}) custom-call(s32[3,8]{1,0:T(4,128)S(1)} %add_add_fusion.where, bf16[8,224,2048]{2,1,0:T(8,128)(2,1)S(1)} %add.131.c_ref, f32[4,224,128]{2,1,0:T(8,128)S(1)} %get-tuple-element.46.left_ref, ...), custom_call_target="tpu_custom_call", output_to_operand_aliasing={{0}: (8, {}), {1}: (9, {})} | custom-call | flops 7516192768 | bytes 15204352 | tf_op jit(solution)/shard_map/last/pallas_call | solution.py:263
  162.0 3.8 %last.5 = (bf16[8,224,2048]{2,1,0:T(8,128)(2,1)}, bf16[8,224,2048]{2,1,0:T(8,128)(2,1)}, bf16[3,512,128]{2,1,0:T(8,128)(2,1)}) custom-call(s32[3,8]{1,0:T(4,128)S(1)} %add_add_fusion.where, bf16[8,224,2048]{2,1,0:T(8,128)(2,1)S(1)} %add.131.c_ref, f32[2,224,128]{2,1,0:T(8,128)S(1)} %get-tuple-element.33.left_ref, ...), custom_call_target="tpu_custom_call", output_to_operand_aliasing={{0}: (6, {}), {1}: (7, {})} | custom-call | flops 3758096384 | bytes 7602176 | tf_op jit(solution)/shard_map/last/pallas_call | solution.py:263
  (66 shorter events, 12.7 us)
Async XLA Ops:
  0.6 2.3 %copy-start = (s32[8]{0:T(128)S(1)}, s32[8]{0:T(128)}, u32[]{:S(2)}) copy-start(s32[8]{0:T(128)} %param.13) | copy-start | bytes 100
  0.6 5.0 %copy-start.3 = (bf16[1,3,512,128]{3,2,1,0:T(8,128)(2,1)S(1)}, bf16[1,3,512,128]{3,2,1,0:T(8,128)(2,1)}, u32[]{:S(2)}) copy-start(bf16[1,3,512,128]{3,2,1,0:T(8,128)(2,1)} %param.11) | copy-start | bytes 1179652
  5.9 9.2 %collective-permute-start = (bf16[4,512,128]{2,1,0:T(8,128)(2,1)S(1)}, bf16[4,512,128]{2,1,0:T(8,128)(2,1)S(1)}, u32[]{:S(2)}, u32[]{:S(2)}) collective-permute-start(bf16[4,512,128]{2,1,0:T(8,128)(2,1)S(1)} %get-tuple-element.61), channel_id=1, source_target_pairs={{0,4},{1,5},{2,6},{3,7},{4,0},{5,1},{6,2},{7,3},{8,12},{9,13},{10,... | collective-permute-start | bytes 1572872 | tf_op jit(solution)/shard_map/ppermute | solution.py:49
  7.1 3.1 %copy-start.1 = (bf16[8,224,2048]{2,1,0:T(8,128)(2,1)S(1)}, bf16[8,224,2048]{2,1,0:T(8,128)(2,1)}, u32[]{:S(2)}) copy-start(bf16[8,224,2048]{2,1,0:T(8,128)(2,1)} %m_ref.1) | copy-start | bytes 22020100
  10.2 3.1 %copy-start.2 = (bf16[8,224,2048]{2,1,0:T(8,128)(2,1)S(1)}, bf16[8,224,2048]{2,1,0:T(8,128)(2,1)}, u32[]{:S(2)}) copy-start(bf16[8,224,2048]{2,1,0:T(8,128)(2,1)} %g_ref.1) | copy-start | bytes 22020100
  15.1 6.9 %collective-permute-start.1 = (bf16[512,128]{1,0:T(8,128)(2,1)S(1)}, bf16[512,128]{1,0:T(8,128)(2,1)S(1)}, u32[]{:S(2)}, u32[]{:S(2)}) collective-permute-start(bf16[512,128]{1,0:T(8,128)(2,1)S(1)} %get-tuple-element.57), channel_id=1, source_target_pairs={{0,8},{1,9},{2,10},{3,11},{4,12},{5,13},{6,14},{7,15},{8,0},{9,1},... | collective-permute-start | bytes 393224 | tf_op jit(solution)/shard_map/ppermute | solution.py:49
  17.7 8.4 %collective-permute-start.2 = (bf16[512,128]{1,0:T(8,128)(2,1)S(1)}, bf16[512,128]{1,0:T(8,128)(2,1)S(1)}, u32[]{:S(2)}, u32[]{:S(2)}) collective-permute-start(bf16[512,128]{1,0:T(8,128)(2,1)S(1)} %get-tuple-element.59), channel_id=1, source_target_pairs={{0,16},{1,17},{2,18},{3,19},{4,20},{5,21},{6,22},{7,23},{8,24},{9,... | collective-permute-start | bytes 393224 | tf_op jit(solution)/shard_map/ppermute | solution.py:49
  19.2 6.9 %collective-permute-start.3 = (bf16[512,128]{1,0:T(8,128)(2,1)S(1)}, bf16[512,128]{1,0:T(8,128)(2,1)S(1)}, u32[]{:S(2)}, u32[]{:S(2)}) collective-permute-start(bf16[512,128]{1,0:T(8,128)(2,1)S(1)} %get-tuple-element.58), channel_id=1, source_target_pairs={{0,24},{1,25},{2,26},{3,27},{4,28},{5,29},{6,30},{7,31},{8,16},{9,... | collective-permute-start | bytes 393224 | tf_op jit(solution)/shard_map/ppermute | solution.py:49
  41.5 9.6 %collective-permute-start.4 = (bf16[2048,128]{1,0:T(8,128)(2,1)S(1)}, bf16[2048,128]{1,0:T(8,128)(2,1)S(1)}, u32[]{:S(2)}, u32[]{:S(2)}) collective-permute-start(bf16[2048,128]{1,0:T(8,128)(2,1)S(1)} %all_gather.6.refs_0_), channel_id=1, source_target_pairs={{0,8},{1,9},{2,10},{3,11},{4,20},{5,21},{6,22},{7,23},{8,0},{9,1},... | collective-permute-start | bytes 1572872 | tf_op jit(solution)/shard_map/ppermute | solution.py:82
  51.1 9.2 %collective-permute-start.5 = (bf16[2048,128]{1,0:T(8,128)(2,1)S(1)}, bf16[2048,128]{1,0:T(8,128)(2,1)S(1)}, u32[]{:S(2)}, u32[]{:S(2)}) collective-permute-start(bf16[2048,128]{1,0:T(8,128)(2,1)S(1)} %collective-permute-done.4.refs_0_), channel_id=1, source_target_pairs={{0,16},{1,17},{2,18},{3,19},{4,12},{5,13},{6,14},{7,15},{8,24},{9,... | collective-permute-start | bytes 1572872 | tf_op jit(solution)/shard_map/ppermute | solution.py:82
  53.2 12.8 %collective-permute-start.9 = (bf16[2048,128]{1,0:T(8,128)(2,1)S(1)}, bf16[2048,128]{1,0:T(8,128)(2,1)S(1)}, u32[]{:S(2)}, u32[]{:S(2)}) collective-permute-start(bf16[2048,128]{1,0:T(8,128)(2,1)S(1)} %all_gather.6.refs_0_), channel_id=1, source_target_pairs={{0,16},{1,17},{2,18},{3,19},{4,12},{5,13},{6,14},{7,15},{8,24},{9,... | collective-permute-start | bytes 1572872 | tf_op jit(solution)/shard_map/ppermute | solution.py:82
  53.2 12.8 %collective-permute-start.7 = (bf16[2048,128]{1,0:T(8,128)(2,1)S(1)}, bf16[2048,128]{1,0:T(8,128)(2,1)S(1)}, u32[]{:S(2)}, u32[]{:S(2)}) collective-permute-start(bf16[2048,128]{1,0:T(8,128)(2,1)S(1)} %all_gather.6.refs_0_), channel_id=1, source_target_pairs={{0,4},{1,5},{2,6},{3,7},{4,0},{5,1},{6,2},{7,3},{8,12},{9,13},{10,... | collective-permute-start | bytes 1572872 | tf_op jit(solution)/shard_map/ppermute | solution.py:49
  60.4 8.4 %collective-permute-start.6 = (bf16[2048,128]{1,0:T(8,128)(2,1)S(1)}, bf16[2048,128]{1,0:T(8,128)(2,1)S(1)}, u32[]{:S(2)}, u32[]{:S(2)}) collective-permute-start(bf16[2048,128]{1,0:T(8,128)(2,1)S(1)} %collective-permute-done.5.refs_0_), channel_id=1, source_target_pairs={{0,4},{1,5},{2,6},{3,7},{4,0},{5,1},{6,2},{7,3},{8,12},{9,13},{10,... | collective-permute-start | bytes 1572872 | tf_op jit(solution)/shard_map/ppermute | solution.py:49
  60.4 10.7 %collective-permute-start.10 = (bf16[2048,128]{1,0:T(8,128)(2,1)S(1)}, bf16[2048,128]{1,0:T(8,128)(2,1)S(1)}, u32[]{:S(2)}, u32[]{:S(2)}) collective-permute-start(bf16[2048,128]{1,0:T(8,128)(2,1)S(1)} %collective-permute-done.4.refs_0_), channel_id=1, source_target_pairs={{0,4},{1,5},{2,6},{3,7},{4,0},{5,1},{6,2},{7,3},{8,12},{9,13},{10,... | collective-permute-start | bytes 1572872 | tf_op jit(solution)/shard_map/ppermute | solution.py:49
  66.0 5.1 %collective-permute-start.11 = (bf16[2048,128]{1,0:T(8,128)(2,1)S(1)}, bf16[2048,128]{1,0:T(8,128)(2,1)S(1)}, u32[]{:S(2)}, u32[]{:S(2)}) collective-permute-start(bf16[2048,128]{1,0:T(8,128)(2,1)S(1)} %collective-permute-done.9.refs_1_), channel_id=1, source_target_pairs={{0,4},{1,5},{2,6},{3,7},{4,0},{5,1},{6,2},{7,3},{8,12},{9,13},{10,... | collective-permute-start | bytes 1572872 | tf_op jit(solution)/shard_map/ppermute | solution.py:49
  68.2 19.0 %collective-permute-start.8 = (bf16[128,2176]{1,0:T(8,128)(2,1)S(1)}, bf16[128,2176]{1,0:T(8,128)(2,1)S(1)}, u32[]{:S(2)}, u32[]{:S(2)}) collective-permute-start(bf16[128,2176]{1,0:T(8,128)(2,1)S(1)} %get-tuple-element.35), channel_id=1, source_target_pairs={{0,4},{1,5},{2,6},{3,7},{4,0},{5,1},{6,2},{7,3},{8,12},{9,13},{10,... | collective-permute-start | bytes 1671176 | tf_op jit(solution)/shard_map/ppermute | solution.py:49
  71.0 4.7 %collective-permute-start.15 = (bf16[128,2176]{1,0:T(8,128)(2,1)S(1)}, bf16[128,2176]{1,0:T(8,128)(2,1)S(1)}, u32[]{:S(2)}, u32[]{:S(2)}) collective-permute-start(bf16[128,2176]{1,0:T(8,128)(2,1)S(1)} %get-tuple-element.41), channel_id=1, source_target_pairs={{0,4},{1,5},{2,6},{3,7},{4,0},{5,1},{6,2},{7,3},{8,12},{9,13},{10,... | collective-permute-start | bytes 1671176 | tf_op jit(solution)/shard_map/ppermute | solution.py:49
  75.1 5.1 %collective-permute-start.14 = (bf16[128,2176]{1,0:T(8,128)(2,1)S(1)}, bf16[128,2176]{1,0:T(8,128)(2,1)S(1)}, u32[]{:S(2)}, u32[]{:S(2)}) collective-permute-start(bf16[128,2176]{1,0:T(8,128)(2,1)S(1)} %get-tuple-element.39), channel_id=1, source_target_pairs={{0,4},{1,5},{2,6},{3,7},{4,0},{5,1},{6,2},{7,3},{8,12},{9,13},{10,... | collective-permute-start | bytes 1671176 | tf_op jit(solution)/shard_map/ppermute | solution.py:49
  75.6 2.4 %collective-permute-start.12 = (bf16[128,2176]{1,0:T(8,128)(2,1)S(1)}, bf16[128,2176]{1,0:T(8,128)(2,1)S(1)}, u32[]{:S(2)}, u32[]{:S(2)}) collective-permute-start(bf16[128,2176]{1,0:T(8,128)(2,1)S(1)} %get-tuple-element.37), channel_id=1, source_target_pairs={{0,4},{1,5},{2,6},{3,7},{4,0},{5,1},{6,2},{7,3},{8,12},{9,13},{10,... | collective-permute-start | bytes 1671176 | tf_op jit(solution)/shard_map/ppermute | solution.py:49
  75.9 9.6 %collective-permute-start.16 = (bf16[128,2176]{1,0:T(8,128)(2,1)S(1)}, bf16[128,2176]{1,0:T(8,128)(2,1)S(1)}, u32[]{:S(2)}, u32[]{:S(2)}) collective-permute-start(bf16[128,2176]{1,0:T(8,128)(2,1)S(1)} %add_convert_fusion.1), channel_id=1, source_target_pairs={{0,16},{1,17},{2,18},{3,19},{4,12},{5,13},{6,14},{7,15},{8,24},{9,... | collective-permute-start | bytes 1671176 | tf_op jit(solution)/shard_map/ppermute | solution.py:82
  78.2 16.5 %collective-permute-start.13 = (bf16[128,2176]{1,0:T(8,128)(2,1)S(1)}, bf16[128,2176]{1,0:T(8,128)(2,1)S(1)}, u32[]{:S(2)}, u32[]{:S(2)}) collective-permute-start(bf16[128,2176]{1,0:T(8,128)(2,1)S(1)} %add_convert_fusion.2), channel_id=1, source_target_pairs={{0,16},{1,17},{2,18},{3,19},{4,12},{5,13},{6,14},{7,15},{8,24},{9,... | collective-permute-start | bytes 1671176 | tf_op jit(solution)/shard_map/ppermute | solution.py:82
  85.7 11.2 %collective-permute-start.17 = (bf16[128,2176]{1,0:T(8,128)(2,1)S(1)}, bf16[128,2176]{1,0:T(8,128)(2,1)S(1)}, u32[]{:S(2)}, u32[]{:S(2)}) collective-permute-start(bf16[128,2176]{1,0:T(8,128)(2,1)S(1)} %add_convert_fusion), channel_id=1, source_target_pairs={{0,8},{1,9},{2,10},{3,11},{4,20},{5,21},{6,22},{7,23},{8,0},{9,1},... | collective-permute-start | bytes 1671176 | tf_op jit(solution)/shard_map/ppermute | solution.py:82
  97.9 11.2 %collective-permute-start.18 = (bf16[32,2176]{1,0:T(8,128)(2,1)S(1)}, bf16[32,2176]{1,0:T(8,128)(2,1)S(1)}, u32[]{:S(2)}, u32[]{:S(2)}) collective-permute-start(bf16[32,2176]{1,0:T(8,128)(2,1)S(1)} %get-tuple-element.43), channel_id=1, source_target_pairs={{0,1},{1,2},{2,3},{3,0},{4,5},{5,6},{6,7},{7,4},{8,9},{9,10},{10,1... | collective-permute-start | bytes 417800 | tf_op jit(solution)/shard_map/ppermute | solution.py:65
  102.5 12.2 %collective-permute-start.19 = (bf16[32,2176]{1,0:T(8,128)(2,1)S(1)}, bf16[32,2176]{1,0:T(8,128)(2,1)S(1)}, u32[]{:S(2)}, u32[]{:S(2)}) collective-permute-start(bf16[32,2176]{1,0:T(8,128)(2,1)S(1)} %get-tuple-element.44), channel_id=1, source_target_pairs={{0,2},{1,3},{2,0},{3,1},{4,6},{5,7},{6,4},{7,5},{8,10},{9,11},{10,... | collective-permute-start | bytes 417800 | tf_op jit(solution)/shard_map/ppermute | solution.py:65
  105.1 9.7 %collective-permute-start.20 = (bf16[32,2176]{1,0:T(8,128)(2,1)S(1)}, bf16[32,2176]{1,0:T(8,128)(2,1)S(1)}, u32[]{:S(2)}, u32[]{:S(2)}) collective-permute-start(bf16[32,2176]{1,0:T(8,128)(2,1)S(1)} %get-tuple-element.45), channel_id=1, source_target_pairs={{0,3},{1,0},{2,1},{3,2},{4,7},{5,4},{6,5},{7,6},{8,11},{9,8},{10,9... | collective-permute-start | bytes 417800 | tf_op jit(solution)/shard_map/ppermute | solution.py:65
  131.1 15.5 %collective-permute-start.21 = (bf16[128,2176]{1,0:T(8,128)(2,1)S(1)}, bf16[128,2176]{1,0:T(8,128)(2,1)S(1)}, u32[]{:S(2)}, u32[]{:S(2)}) collective-permute-start(bf16[128,2176]{1,0:T(8,128)(2,1)S(1)} %all_gather.7.refs_0_), channel_id=1, source_target_pairs={{0,8},{1,9},{2,10},{3,11},{4,20},{5,21},{6,22},{7,23},{8,0},{9,1},... | collective-permute-start | bytes 1671176 | tf_op jit(solution)/shard_map/ppermute | solution.py:82
  132.7 13.9 %collective-permute-start.24 = (bf16[128,2176]{1,0:T(8,128)(2,1)S(1)}, bf16[128,2176]{1,0:T(8,128)(2,1)S(1)}, u32[]{:S(2)}, u32[]{:S(2)}) collective-permute-start(bf16[128,2176]{1,0:T(8,128)(2,1)S(1)} %all_gather.7.refs_0_), channel_id=1, source_target_pairs={{0,16},{1,17},{2,18},{3,19},{4,12},{5,13},{6,14},{7,15},{8,24},{9,... | collective-permute-start | bytes 1671176 | tf_op jit(solution)/shard_map/ppermute | solution.py:82
  133.2 13.9 %collective-permute-start.27 = (bf16[128,2176]{1,0:T(8,128)(2,1)S(1)}, bf16[128,2176]{1,0:T(8,128)(2,1)S(1)}, u32[]{:S(2)}, u32[]{:S(2)}) collective-permute-start(bf16[128,2176]{1,0:T(8,128)(2,1)S(1)} %all_gather.7.refs_0_), channel_id=1, source_target_pairs={{0,4},{1,5},{2,6},{3,7},{4,0},{5,1},{6,2},{7,3},{8,12},{9,13},{10,... | collective-permute-start | bytes 1671176 | tf_op jit(solution)/shard_map/ppermute | solution.py:49
  146.6 9.5 %collective-permute-start.22 = (bf16[128,2176]{1,0:T(8,128)(2,1)S(1)}, bf16[128,2176]{1,0:T(8,128)(2,1)S(1)}, u32[]{:S(2)}, u32[]{:S(2)}) collective-permute-start(bf16[128,2176]{1,0:T(8,128)(2,1)S(1)} %collective-permute-done.21.refs_0_), channel_id=1, source_target_pairs={{0,16},{1,17},{2,18},{3,19},{4,12},{5,13},{6,14},{7,15},{8,24},{9,... | collective-permute-start | bytes 1671176 | tf_op jit(solution)/shard_map/ppermute | solution.py:82
  146.6 9.5 %collective-permute-start.25 = (bf16[128,2176]{1,0:T(8,128)(2,1)S(1)}, bf16[128,2176]{1,0:T(8,128)(2,1)S(1)}, u32[]{:S(2)}, u32[]{:S(2)}) collective-permute-start(bf16[128,2176]{1,0:T(8,128)(2,1)S(1)} %collective-permute-done.21.refs_0_), channel_id=1, source_target_pairs={{0,4},{1,5},{2,6},{3,7},{4,0},{5,1},{6,2},{7,3},{8,12},{9,13},{10,... | collective-permute-start | bytes 1671176 | tf_op jit(solution)/shard_map/ppermute | solution.py:49
  146.6 9.5 %collective-permute-start.26 = (bf16[128,2176]{1,0:T(8,128)(2,1)S(1)}, bf16[128,2176]{1,0:T(8,128)(2,1)S(1)}, u32[]{:S(2)}, u32[]{:S(2)}) collective-permute-start(bf16[128,2176]{1,0:T(8,128)(2,1)S(1)} %collective-permute-done.24.refs_1_), channel_id=1, source_target_pairs={{0,4},{1,5},{2,6},{3,7},{4,0},{5,1},{6,2},{7,3},{8,12},{9,13},{10,... | collective-permute-start | bytes 1671176 | tf_op jit(solution)/shard_map/ppermute | solution.py:49
  156.1 5.8 %collective-permute-start.23 = (bf16[128,2176]{1,0:T(8,128)(2,1)S(1)}, bf16[128,2176]{1,0:T(8,128)(2,1)S(1)}, u32[]{:S(2)}, u32[]{:S(2)}) collective-permute-start(bf16[128,2176]{1,0:T(8,128)(2,1)S(1)} %collective-permute-done.22.refs_0_), channel_id=1, source_target_pairs={{0,4},{1,5},{2,6},{3,7},{4,0},{5,1},{6,2},{7,3},{8,12},{9,13},{10,... | collective-permute-start | bytes 1671176 | tf_op jit(solution)/shard_map/ppermute | solution.py:49

commit v2 on v1

--- a/solution.py
+++ b/solution.py
@@ -16,14 +16,6 @@
 WEIGHT = 8
 GRANT = 28 * 2**20
 AXES = ("group", "shard")
-
-
-def owner_slots(owner_group):
-    experts = owner_group.shape[0]
-    expert_ids = jnp.arange(experts, dtype=jnp.int32)
-    same_owner = owner_group[:, None] == owner_group[None, :]
-    earlier = expert_ids[None, :] < expert_ids[:, None]
-    return jnp.sum((same_owner & earlier).astype(jnp.int32), axis=1)
 
 
 def bits_of(size):
@@ -56,13 +48,12 @@
         ]
         return lax.ppermute(x, AXES, pairs)
 
-    def shift_shard(self, x, step):
-        pairs = [
-            (g * self.shards + s, g * self.shards + (s + step) % self.shards)
-            for g in range(self.groups)
-            for s in range(self.shards)
-        ]
-        return lax.ppermute(x, AXES, pairs)
+    def gather_shard(self, x):
+        pieces = [x]
+        for d in range(1, self.shards):
+            pieces.append(self.swap_shard(x, d))
+        half = self.shards // 2
+        return [jnp.concatenate(pieces[i : i + half], axis=0) for i in (0, half)]
 
     def orders(self):
         near, *far = bits_of(self.groups)
@@ -88,14 +79,68 @@
                 held[name | 1 << level] = self.cross(held[name], level)
         return held
 
-    def collect(self, held):
-        held = {name: list(pieces) for name, pieces in held.items()}
+    def collect(self, held, early):
+        held = {name: list(terms) for name, terms in held.items()}
         for level in reversed(range(self.levels())):
             for name in [name for name in held if name >> level & 1]:
                 terms = held.pop(name)
-                sent = sum(term.astype(jnp.float32) for term in terms).astype(jnp.bfloat16)
+                if early and level + 1 < self.levels():
+                    sent = sum_call(terms)
+                else:
+                    sent = sum(term.astype(jnp.float32) for term in terms).astype(jnp.bfloat16)
                 held[name ^ 1 << level].append(self.cross(sent, level))
         return held[0]
+
+
+def plan_body(distances, near, uppers, owner_ref, count_ref, q_ref, table_ref, *refs):
+    kept_refs, sent_ref, slots_ref = refs[:-2], refs[-2], refs[-1]
+    mine, shard = lax.axis_index("group"), lax.axis_index("shard")
+    experts, cap = owner_ref.shape[0], q_ref.shape[1]
+    owners = [owner_ref[e] for e in range(experts)]
+    for e in range(experts):
+        slot = jnp.int32(0)
+        for other in owners[:e]:
+            slot = slot + (other == owners[e]).astype(jnp.int32)
+        live = (slot < count_ref[owners[e]]) & (owners[e] == mine)
+        slots_ref[e] = jnp.where(live, slot, cap)
+    side = (mine & near) > 0
+    for i, (zero, one) in enumerate(zip(*distances)):
+        chosen = mine ^ jnp.where(side, one, zero)
+        table_ref[0, i] = chosen
+        table_ref[1, i] = slots_ref[chosen]
+        table_ref[2, i] = shard
+
+    def outgoing(r):
+        slot = slots_ref[mine ^ r]
+        piece = q_ref[0, jnp.minimum(slot, cap - 1)]
+        return jnp.where(slot < cap, piece, jnp.zeros_like(piece))
+
+    for i, r in enumerate(uppers):
+        sent_ref[i] = outgoing(r ^ near)
+        kept_refs[i][...] = outgoing(r)
+
+
+def plan_call(owner_group, group_counts, q_prev, distances, near, uppers):
+    experts = owner_group.shape[0]
+    _, _, share, rank = q_prev.shape
+    scalars, vector = (pl.BlockSpec(memory_space=m) for m in (pltpu.SMEM, pltpu.VMEM))
+    piece = jax.ShapeDtypeStruct((share, rank), q_prev.dtype)
+    outs = pl.pallas_call(
+        functools.partial(plan_body, distances, near, uppers),
+        grid_spec=pltpu.PrefetchScalarGridSpec(
+            num_scalar_prefetch=2,
+            grid=(1,),
+            in_specs=[pl.BlockSpec(q_prev.shape, lambda i, *_: (0,) * 4)],
+            out_specs=[scalars] + [vector] * (len(uppers) + 1),
+            scratch_shapes=[pltpu.SMEM((experts,), jnp.int32)],
+        ),
+        out_shape=[jax.ShapeDtypeStruct((3, experts), jnp.int32)]
+        + [piece] * len(uppers)
+        + [jax.ShapeDtypeStruct((len(uppers), share, rank), q_prev.dtype)],
+        compiler_params=pltpu.CompilerParams(vmem_limit_bytes=GRANT),
+        name="plan",
+    )(owner_group, group_counts, q_prev)
+    return outs[0], outs[1:-1], outs[-1]
 
 
 def add_body(m_ref, g_ref, c_ref):
@@ -123,34 +168,50 @@
     )(momentum, gradient)
 
 
-def split_body(shard_count, where, *refs):
-    ins, outs, total_ref = refs[: -shard_count - 1], refs[-shard_count - 1 : -1], refs[-1]
-    total = ins[0][...].astype(jnp.float32)
-    for ref in ins[1:]:
-        total = total + ref[...].astype(jnp.float32)
-    total_ref[...] = total
+def sum_body(*refs):
+    refs[-1][...] = sum(ref[...].astype(jnp.float32) for ref in refs[:-1]).astype(jnp.bfloat16)
+
+
+def sum_call(terms):
+    vector = pl.BlockSpec(memory_space=pltpu.VMEM)
+    return pl.pallas_call(
+        sum_body,
+        in_specs=[vector] * len(terms),
+        out_specs=vector,
+        out_shape=jax.ShapeDtypeStruct(terms[0].shape, jnp.bfloat16),
+        compiler_params=pltpu.CompilerParams(vmem_limit_bytes=GRANT),
+        name="sum",
+    )(*terms)
+
+
+def split_body(half, wholes, where, *refs):
+    outs, total_ref = refs[wholes:-1], refs[-1]
+    rows = slice(half * total_ref.shape[0], (half + 1) * total_ref.shape[0])
+    terms = [ref[rows, :] for ref in refs[:2]] + [ref[...] for ref in refs[2:wholes]]
+    total_ref[...] = sum(term.astype(jnp.float32) for term in terms)
     piece = outs[0].shape[0]
     for step, out in enumerate(outs):
-        start = lax.rem(where[2, 0] + step, shard_count) * piece
+        start = (where[2, 0] ^ step) * piece
         out[...] = total_ref[pl.ds(pl.multiple_of(start, piece), piece), :].astype(jnp.bfloat16)
 
 
-def split_call(where, terms, shard_count):
-    rank, hidden = terms[0].shape
-    piece = rank // shard_count
+def split_call(where, half, own, parts, shard_count):
+    rows, hidden = parts[0].shape
+    piece = rows // shard_count
+    vector = pl.BlockSpec(memory_space=pltpu.VMEM)
     return pl.pallas_call(
-        functools.partial(split_body, shard_count),
+        functools.partial(split_body, half, len(own) + len(parts)),
         grid_spec=pltpu.PrefetchScalarGridSpec(
             num_scalar_prefetch=1,
             grid=(1,),
-            in_specs=[pl.BlockSpec(memory_space=pltpu.VMEM)] * len(terms),
-            out_specs=[pl.BlockSpec(memory_space=pltpu.VMEM)] * shard_count,
-            scratch_shapes=[pltpu.VMEM((rank, hidden), jnp.float32)],
+            in_specs=[vector] * (len(own) + len(parts)),
+            out_specs=[vector] * shard_count,
+            scratch_shapes=[pltpu.VMEM((rows, hidden), jnp.float32)],
         ),
         out_shape=[jax.ShapeDtypeStruct((piece, hidden), jnp.bfloat16)] * shard_count,
         compiler_params=pltpu.CompilerParams(vmem_limit_bytes=GRANT),
         name="split",
-    )(where, *terms)
+    )(where, *own, *parts)
 
 
 def pick(refs):
@@ -160,14 +221,21 @@
     return value
 
 
-def first_body(count, where, c_ref, *refs):
-    q_refs, refs = refs[:count], refs[count:]
+def first_body(count, shard_count, where, c_ref, *refs):
+    q_refs, refs = refs[: 2 * count], refs[2 * count :]
     left_ref, right_refs = refs[0], refs[1:]
     hidden = c_ref.shape[2]
     step = pl.program_id(0)
     combined = c_ref[0]
-    q = pick(q_refs)
-    left = jnp.dot(combined, q, preferred_element_type=jnp.float32)
+    halves = [pick(q_refs[:count]), pick(q_refs[count:])]
+    share = hidden // shard_count
+    left = jnp.zeros(left_ref.shape[1:], jnp.float32)
+    for d in range(shard_count):
+        start = (where[2, 0] ^ d) * share
+        columns = c_ref[0, :, pl.ds(pl.multiple_of(start, share), share)]
+        half, at = divmod(d, shard_count // 2)
+        part = halves[half][at * share : (at + 1) * share]
+        left = left + jnp.dot(columns, part, preferred_element_type=jnp.float32)
     left_ref[0] = left
     squares = jnp.sum(left * left, axis=0, keepdims=True)
     squares = jnp.broadcast_to(squares, (squares.shape[1],) * 2).T.astype(jnp.bfloat16)
@@ -187,17 +255,17 @@
     return pl.BlockSpec(shape, lambda i, w: (0,) * len(shape))
 
 
-def first_call(where, base, combined, qs):
+def first_call(where, base, combined, qs, shard_count):
     _, rows, hidden = combined.shape
-    count = len(qs)
+    count = len(qs) // 2
     _, rank = qs[0].shape
     outs = pl.pallas_call(
-        functools.partial(first_body, count),
+        functools.partial(first_body, count, shard_count),
         grid_spec=pltpu.PrefetchScalarGridSpec(
             num_scalar_prefetch=1,
             grid=(count,),
             in_specs=[pl.BlockSpec((1, rows, hidden), lambda i, w: (w[0, base + i], 0, 0))]
-            + [pl.BlockSpec(memory_space=pltpu.VMEM)] * count,
+            + [pl.BlockSpec(memory_space=pltpu.VMEM)] * len(qs),
             out_specs=[pl.BlockSpec((1, rows, rank), lambda i, w: (i, 0, 0))]
             + [pl.BlockSpec(memory_space=pltpu.VMEM)] * count,
         ),
@@ -215,7 +283,7 @@
 
 
 def last_body(count, multiplier, cap, base, fresh, where, c_ref, left_ref, *refs):
-    right_refs, refs = refs[:count], refs[count:]
+    right_refs, refs = refs[: 2 * count], refs[2 * count :]
     mom_ref, upd_ref, q_ref, buf = refs[-4:]
     step = pl.program_id(0)
 
@@ -227,14 +295,23 @@
             q_ref[...] = refs[0][...]
 
     hidden = c_ref.shape[2]
-    arrived = pick(right_refs)
-    buf[...] = arrived
-    squares = arrived[:, hidden : hidden + 1].astype(jnp.float32)
+    halves = [pick(right_refs[:count]), pick(right_refs[count:])]
+    shard_count = hidden // q_ref.shape[1]
+    piece = buf.shape[0] // (2 * shard_count)
+    for d in range(shard_count):
+        start = (where[2, 0] ^ d) * piece
+        half, at = divmod(d, shard_count // 2)
+        for i in (0, 1):
+            rows = halves[half][(2 * at + i) * piece : (2 * at + i + 1) * piece]
+            to = pl.multiple_of(start + i * piece * shard_count, piece)
+            buf[pl.ds(to, piece), :] = rows.astype(jnp.float32)
+    arrived = buf[...]
+    squares = arrived[:, hidden : hidden + 1]
     n_col = lax.rsqrt(squares + stability_offset)
     n_row = jnp.broadcast_to(n_col, (n_col.shape[0],) * 2).T[0:1, :]
     n_col = n_col * UP
     left = (left_ref[0] * n_row).astype(jnp.bfloat16)
-    right = arrived[:, :hidden].astype(jnp.float32) * n_col
+    right = arrived[:, :hidden] * n_col
     total = jnp.sum(right * right, axis=1, keepdims=True)
     scale = lax.rsqrt(total / right.shape[1] + stability_offset)
     low = jnp.dot(left, right.astype(jnp.bfloat16), preferred_element_type=jnp.float32)
@@ -249,14 +326,15 @@
     def _():
         share = q_ref.shape[1]
         start = pl.multiple_of(where[2, 0] * share, share)
-        own = buf[:, pl.ds(start, share)].astype(jnp.float32) * n_col * scale
+        own = buf[:, pl.ds(start, share)] * n_col * scale
         q_ref[slot] = own.T.astype(jnp.bfloat16)
 
 
 def last_call(where, base, combined, left, rights, outs, cap, share, multiplier):
     experts, rows, hidden = combined.shape
-    count = len(rights)
+    count = len(rights) // 2
     rank, width = rights[0].shape
+    rank *= 2
     block = pl.BlockSpec((1, rows, hidden), lambda i, w: (w[0, base + i], 0, 0))
     anywhere = pl.BlockSpec(memory_space=pl.ANY)
     extra = [] if outs is None else [outs[2], outs[0], outs[1]]
@@ -269,17 +347,17 @@
                 block,
                 pl.BlockSpec((1, rows, rank), lambda i, w: (i, 0, 0)),
             ]
-            + [pl.BlockSpec(memory_space=pltpu.VMEM)] * count
+            + [pl.BlockSpec(memory_space=pltpu.VMEM)] * len(rights)
             + ([] if outs is None else [fixed((cap, share, rank)), anywhere, anywhere]),
             out_specs=[block, block, fixed((cap, share, rank))],
-            scratch_shapes=[pltpu.VMEM((rank, width), jnp.bfloat16)],
+            scratch_shapes=[pltpu.VMEM((rank, width), jnp.float32)],
         ),
         out_shape=[
             jax.ShapeDtypeStruct((experts, rows, hidden), jnp.bfloat16),
             jax.ShapeDtypeStruct((experts, rows, hidden), jnp.bfloat16),
             jax.ShapeDtypeStruct((cap, share, rank), jnp.bfloat16),
         ],
-        input_output_aliases={} if outs is None else {4 + count: 0, 5 + count: 1},
+        input_output_aliases={} if outs is None else {4 + 2 * count: 0, 5 + 2 * count: 1},
         cost_estimate=pl.CostEstimate(
             flops=WEIGHT * count * 4 * rows * hidden * rank,
             bytes_accessed=count * 2 * (3 * rows + 2 * rank) * hidden,
@@ -293,9 +371,7 @@
 def step(momentum, gradient, q_prev, owner_group, group_counts):
     groups = lax.axis_size("group")
     shard_count = lax.axis_size("shard")
-    mine = lax.axis_index("group")
-    shard = lax.axis_index("shard")
-    experts, rows, _ = momentum.shape
+    experts, block, _ = momentum.shape
     _, cap, share, rank = q_prev.shape
     assert experts == groups
     links = Links(groups, shard_count)
@@ -314,41 +390,33 @@
             for name in members
         ]
 
-    slot_of = owner_slots(owner_group)
-    owned = (slot_of < group_counts[owner_group]) & (owner_group == mine)
-    slots = jnp.where(owned, slot_of, cap)
-    chosen = mine ^ jnp.where(
-        mine & near > 0, jnp.array(distances(1), jnp.int32), jnp.array(distances(0), jnp.int32)
+    uppers = [r for r in range(groups) if not r & near]
+    where, kept, sent = plan_call(
+        owner_group, group_counts, q_prev, (distances(0), distances(1)), near, uppers
     )
-    where = jnp.stack([chosen, slots[chosen], jnp.full_like(chosen, shard)]).astype(jnp.int32)
-
-    uppers = [r for r in range(groups) if not r & near]
-
-    def outgoing(members):
-        picked = slots[mine ^ jnp.array(members, jnp.int32)]
-        sent = jnp.zeros((len(members), share, rank), q_prev.dtype)
-        for slot in range(cap):
-            sent = jnp.where((picked == slot)[:, None, None], q_prev[0, slot][None], sent)
-        return sent
-
-    arrived = links.swap_group(outgoing([r ^ near for r in uppers]), near)
-    kept = outgoing(uppers)
+    arrived = links.swap_group(sent, near)
     parts = [kept[i] + arrived[i] for i in range(len(uppers))]
     q_own = parts[0]
     for part, r in zip(parts[1:], uppers[1:]):
         q_own = q_own + links.swap_group(part, r)
     combined = add_call(momentum, gradient)
-    q_own, combined, where = lax.optimization_barrier((q_own, combined, where))
-    q_full = lax.all_gather(q_own, "shard", axis=0, tiled=True)
-    qs = links.spread(q_full)
-    qs_far = {name: links.swap_group(piece, near) for name, piece in qs.items()}
+    q_own, combined = lax.optimization_barrier((q_own, combined))
+    q_full = links.gather_shard(q_own)
+    qs = [links.spread(part) for part in q_full]
+    qs_far = [{n: links.swap_group(x, near) for n, x in part.items()} for part in qs]
 
     lefts, rights, bases = [], {}, []
     base = 0
     for members in sets:
         count = len(members)
         left, outs = first_call(
-            where, base, combined, [qs[n] for n in members] + [qs_far[n] for n in members]
+            where,
+            base,
+            combined,
+            [
+                side[half][n] for half in (0, 1) for side in (qs, qs_far) for n in members
+            ],
+            shard_count,
         )
         lefts.append(left)
         for j, name in enumerate(members):
@@ -356,18 +424,28 @@
         bases.append(base)
         base += 2 * count
 
-    pieces = split_call(where, links.collect(rights), shard_count)
-    mine_sum = pieces[0].astype(jnp.float32)
-    for d in range(1, shard_count):
-        mine_sum = mine_sum + links.shift_shard(pieces[d], d).astype(jnp.float32)
-    right_own = lax.all_gather(mine_sum.astype(jnp.bfloat16), "shard", axis=0, tiled=True)
-    full = links.spread(right_own)
-    full_far = {name: links.swap_group(piece, near) for name, piece in full.items()}
-
-    multiplier = math.sqrt(rows * groups * shard_count / rank)
+    own = rights.pop(0)
+    sums = []
+    for i in (0, 1):
+        rows = slice(i * rank // 2, (i + 1) * rank // 2)
+        held = {name: [term[rows] for term in terms] for name, terms in rights.items()}
+        parts = links.collect({0: [], **held}, i == 0)
+        pieces = split_call(where, i, own, parts, shard_count)
+        mine_sum = pieces[0].astype(jnp.float32)
+        for d in range(1, shard_count):
+            mine_sum = mine_sum + links.swap_shard(pieces[d], d).astype(jnp.float32)
+        sums.append(mine_sum)
+    mine_sum = jnp.concatenate(sums, axis=0)
+    right_own = links.gather_shard(mine_sum.astype(jnp.bfloat16))
+    full = [links.spread(part) for part in right_own]
+    full_far = [{n: links.swap_group(x, near) for n, x in part.items()} for part in full]
+
+    multiplier = math.sqrt(block * groups * shard_count / rank)
     outs = None
     for i, members in enumerate(sets):
-        pieces = [full[name] for name in members] + [full_far[name] for name in members]
+        pieces = [
+            side[half][n] for half in (0, 1) for side in (full, full_far) for n in members
+        ]
         outs = last_call(where, bases[i], combined, lefts[i], pieces, outs, cap, share, multiplier)
     momentum_next, update, q_next = outs
     return momentum_next, update, q_next[None]

time: 166 us -> 140 us (0.84)
  blocking collectives: 31.7 us -> 0 us
  starting transfers between devices: 25.6 us -> 50.9 us
  waiting for transfers between devices: 70.4 us -> 51.1 us
  other arithmetic: 3.9 us -> 0.58 us
  Pallas kernels: 24.5 us -> 27.5 us
    all_gather x2 -> x0, blocking collectives: 31.7 us -> none  [the longest x1 16.3 us: step(): lax.all_gather(mine_sum.astype(jnp.bfloat16), 'shard', axis=0, tiled=True)]
    ppermute x9 -> x18, waiting for transfers between devices: 53.8 us -> 29.8 us  [cross(): return lax.ppermute(x, AXES, pairs)]
    ppermute x9 -> x18, starting transfers between devices: 11.5 us -> 24.9 us  [cross(): return lax.ppermute(x, AXES, pairs)]
    ppermute x3 -> x12, starting transfers between devices: 7.13 us -> 17.4 us  [swap_shard(): return lax.ppermute(x, AXES, pairs)]
    ppermute x3 -> x12, waiting for transfers between devices: 9.68 us -> 19.8 us  [swap_shard(): return lax.ppermute(x, AXES, pairs)]
    ppermute x16 -> x24, waiting for transfers between devices: 6.93 us -> 1.6 us  [swap_group(): return lax.ppermute(x, AXES, pairs)]
    gather x4 -> x0, local copies, waits for them, and re-layouts: 2.56 us -> none  [the longest x2 1.28 us: outgoing(): picked = slots[mine ^ jnp.array(members, jnp.int32)]]
    unnamed x8 -> x13, local copies, waits for them, and re-layouts: 6.19 us -> 8.49 us
  transfers between devices with their start and end apart: 28 -> 54, of which waited for: 13 -> 14; matrix products, arithmetic and copies ran while one was open for 1% -> 0% of each run, Pallas kernels for 12% -> 16%
where the time goes in v2:
time: 140 us
  waiting for transfers between devices  51.1 us (36%)
  starting transfers between devices  50.9 us (36%)
  Pallas kernels  27.5 us (20%)
  local copies, waits for them, and re-layouts  8.59 us (6%)
    ppermute x18, waiting for transfers between devices, cross(): return lax.ppermute(x, AXES, pairs)  29.8 us
    ppermute x18, starting transfers between devices, cross(): return lax.ppermute(x, AXES, pairs)  24.9 us
    ppermute x12, waiting for transfers between devices, swap_shard(): return lax.ppermute(x, AXES, pairs)  19.8 us
    ppermute x12, starting transfers between devices, swap_shard(): return lax.ppermute(x, AXES, pairs)  17.4 us
    pallas_call x3, Pallas kernels, last_call(): pl.pallas_call(functools.partial(last_body, count, multiplier, cap, base,...  14.3 us
    ppermute x24, starting transfers between devices, swap_group(): return lax.ppermute(x, AXES, pairs)  8.59 us
    unnamed x13, local copies, waits for them, and re-layouts  8.49 us
    pallas_call x3, Pallas kernels, first_call(): pl.pallas_call(functools.partial(first_body, count, shard_count), grid_sp...  8.38 us
  transfers between devices with their start and end apart: 54, of which 14 were waited for; matrix products, arithmetic and copies ran while one was open for 0% of the time, Pallas kernels for 16%

profile of v2, /device:TPU:0, one launch (start us, length us, event | category | flops | bytes accessed | tf_op | source)
XLA Modules:
  0.0 139.6 jit_solution(2731472429992300923)
XLA Ops:
  6.6 2.9 %collective-permute-start.1 = (bf16[512,128]{1,0:T(8,128)(2,1)S(1)}, bf16[512,128]{1,0:T(8,128)(2,1)S(1)}, u32[]{:S(2)}, u32[]{:S(2)}) collective-permute-start(bf16[512,128]{1,0:T(8,128)(2,1)S(1)} %get-tuple-element.79), channel_id=1, source_target_pairs={{0,8},{1,9},{2,10},{3,11},{4,12},{5,13},{6,14},{7,15},{8,0},{9,1},... | collective-permute-start | bytes 393224 | tf_op jit(solution)/shard_map/ppermute | solution.py:41
  11.0 3.1 %copy-done.3 = bf16[8,224,2048]{2,1,0:T(8,128)(2,1)S(1)} copy-done((bf16[8,224,2048]{2,1,0:T(8,128)(2,1)S(1)}, bf16[8,224,2048]{2,1,0:T(8,128)(2,1)}, u32[]{:S(2)}) %copy-start.3) | copy-done | bytes 7340056
  14.1 3.1 %copy-done.4 = bf16[8,224,2048]{2,1,0:T(8,128)(2,1)S(1)} copy-done((bf16[8,224,2048]{2,1,0:T(8,128)(2,1)S(1)}, bf16[8,224,2048]{2,1,0:T(8,128)(2,1)}, u32[]{:S(2)}) %copy-start.4) | copy-done | bytes 7340056
  17.2 1.7 %add.108.c_ref = bf16[8,224,2048]{2,1,0:T(8,128)(2,1)S(1)} custom-call(bf16[8,224,2048]{2,1,0:T(8,128)(2,1)S(1)} %copy-done.3, bf16[8,224,2048]{2,1,0:T(8,128)(2,1)S(1)} %copy-done.4), custom_call_target="tpu_custom_call" | custom-call | flops 7516192768 | bytes 22020096 | tf_op jit(solution)/shard_map/add/pallas_call | solution.py:155
  19.0 3.1 %collective-permute-start.8 = (bf16[512,128]{1,0:T(8,128)(2,1)S(1)}, bf16[512,128]{1,0:T(8,128)(2,1)S(1)}, u32[]{:S(2)}, u32[]{:S(2)}) collective-permute-start(bf16[512,128]{1,0:T(8,128)(2,1)S(1)} %fusion.6), channel_id=1, source_target_pairs={{0,2},{1,3},{2,0},{3,1},{4,6},{5,7},{6,4},{7,5},{8,10},{9,11},{10,... | collective-permute-start | bytes 393224 | tf_op jit(solution)/shard_map/ppermute | solution.py:49
  23.7 8.1 %collective-permute-done.8 = bf16[512,128]{1,0:T(8,128)(2,1)S(1)} collective-permute-done((bf16[512,128]{1,0:T(8,128)(2,1)S(1)}, bf16[512,128]{1,0:T(8,128)(2,1)S(1)}, u32[]{:S(2)}, u32[]{:S(2)}) %collective-permute-start.8) | collective-permute-done | bytes 131104 | tf_op jit(solution)/shard_map/ppermute | solution.py:49
  34.1 5.4 %collective-permute-done.10.refs_4_ = bf16[1024,128]{1,0:T(8,128)(2,1)S(1)} collective-permute-done((bf16[1024,128]{1,0:T(8,128)(2,1)S(1)}, bf16[1024,128]{1,0:T(8,128)(2,1)S(1)}, u32[]{:S(2)}, u32[]{:S(2)}) %collective-permute-start.10) | collective-permute-done | bytes 262176 | tf_op jit(solution)/shard_map/ppermute | solution.py:73
  41.0 4.1 %collective-permute-done.5.refs_0_ = bf16[1024,128]{1,0:T(8,128)(2,1)S(1)} collective-permute-done((bf16[1024,128]{1,0:T(8,128)(2,1)S(1)}, bf16[1024,128]{1,0:T(8,128)(2,1)S(1)}, u32[]{:S(2)}, u32[]{:S(2)}) %collective-permute-start.5) | collective-permute-done | bytes 262176 | tf_op jit(solution)/shard_map/ppermute | solution.py:73
  48.7 2.8 %collective-permute-done.6.refs_0_ = bf16[1024,128]{1,0:T(8,128)(2,1)S(1)} collective-permute-done((bf16[1024,128]{1,0:T(8,128)(2,1)S(1)}, bf16[1024,128]{1,0:T(8,128)(2,1)S(1)}, u32[]{:S(2)}, u32[]{:S(2)}) %collective-permute-start.6) | collective-permute-done | bytes 262176 | tf_op jit(solution)/shard_map/ppermute | solution.py:73
  51.5 2.2 %first.4 = (f32[2,224,128]{2,1,0:T(8,128)S(1)}, bf16[128,2176]{1,0:T(8,128)(2,1)S(1)}, bf16[128,2176]{1,0:T(8,128)(2,1)S(1)}) custom-call(s32[3,8]{1,0:T(4,128)S(1)} %get-tuple-element.39.where, bf16[8,224,2048]{2,1,0:T(8,128)(2,1)S(1)} %add.108.c_ref, bf16[1024,128]{1,0:T(8,128)(2,1)S(1)} %constant_dynamic-update-slice_fusion.refs_0_, ...), custom_call_target="tpu_custom_call" | custom-call | flops 3758096384 | bytes 3932160 | tf_op jit(solution)/shard_map/first/pallas_call | solution.py:262
  54.3 2.8 %collective-permute-done.16.refs_1_ = bf16[1024,128]{1,0:T(8,128)(2,1)S(1)} collective-permute-done((bf16[1024,128]{1,0:T(8,128)(2,1)S(1)}, bf16[1024,128]{1,0:T(8,128)(2,1)S(1)}, u32[]{:S(2)}, u32[]{:S(2)}) %collective-permute-start.16) | collective-permute-done | bytes 262176 | tf_op jit(solution)/shard_map/ppermute | solution.py:73
  57.7 2.2 %first.3 = (f32[2,224,128]{2,1,0:T(8,128)S(1)}, bf16[128,2176]{1,0:T(8,128)(2,1)S(1)}, bf16[128,2176]{1,0:T(8,128)(2,1)S(1)}) custom-call(s32[3,8]{1,0:T(4,128)S(1)} %get-tuple-element.39.where, bf16[8,224,2048]{2,1,0:T(8,128)(2,1)S(1)} %add.108.c_ref, bf16[1024,128]{1,0:T(8,128)(2,1)S(1)} %collective-permute-done.6.refs_0_, ...), custom_call_target="tpu_custom_call" | custom-call | flops 3758096384 | bytes 3932160 | tf_op jit(solution)/shard_map/first/pallas_call | solution.py:262
  60.4 4.0 %first.5 = (f32[4,224,128]{2,1,0:T(8,128)S(1)}, bf16[128,2176]{1,0:T(8,128)(2,1)S(1)}, bf16[128,2176]{1,0:T(8,128)(2,1)S(1)}, bf16[128,2176]{1,0:T(8,128)(2,1)S(1)}, bf16[128,2176]{1,0:T(8,128)(2,1)S(1)}) custom-call(s32[3,8]{1,0:T(4,128)S(1)} %get-tuple-element.39.where, bf16[8,224,2048]{2,1,0:T(8,128)(2,1)S(1)} %add.108.c_ref, ...), custom_call_target="tpu_custom_call" | custom-call | flops 7516192768 | bytes 7864320 | tf_op jit(solution)/shard_map/first/pallas_call | solution.py:262
  65.2 1.6 %collective-permute-start.26 = (bf16[64,2176]{1,0:T(8,128)(2,1)S(1)}, bf16[64,2176]{1,0:T(8,128)(2,1)S(1)}, u32[]{:S(2)}, u32[]{:S(2)}) collective-permute-start(bf16[64,2176]{1,0:T(8,128)(2,1)S(1)} %get-tuple-element.75), channel_id=1, source_target_pairs={{0,16},{1,17},{2,18},{3,19},{4,12},{5,13},{6,14},{7,15},{8,24},{9,... | collective-permute-start | bytes 835592 | tf_op jit(solution)/shard_map/ppermute | solution.py:73
  67.4 1.6 %collective-permute-start.23 = (bf16[64,2176]{1,0:T(8,128)(2,1)S(1)}, bf16[64,2176]{1,0:T(8,128)(2,1)S(1)}, u32[]{:S(2)}, u32[]{:S(2)}) collective-permute-start(bf16[64,2176]{1,0:T(8,128)(2,1)S(1)} %get-tuple-element.77), channel_id=1, source_target_pairs={{0,16},{1,17},{2,18},{3,19},{4,12},{5,13},{6,14},{7,15},{8,24},{9,... | collective-permute-start | bytes 835592 | tf_op jit(solution)/shard_map/ppermute | solution.py:73
  69.6 2.3 %collective-permute-done.26.refs_2_ = bf16[64,2176]{1,0:T(8,128)(2,1)S(1)} collective-permute-done((bf16[64,2176]{1,0:T(8,128)(2,1)S(1)}, bf16[64,2176]{1,0:T(8,128)(2,1)S(1)}, u32[]{:S(2)}, u32[]{:S(2)}) %collective-permute-start.26) | collective-permute-done | bytes 278560 | tf_op jit(solution)/shard_map/ppermute | solution.py:73
  71.9 1.6 %collective-permute-start.27 = (bf16[64,2176]{1,0:T(8,128)(2,1)S(1)}, bf16[64,2176]{1,0:T(8,128)(2,1)S(1)}, u32[]{:S(2)}, u32[]{:S(2)}) collective-permute-start(bf16[64,2176]{1,0:T(8,128)(2,1)S(1)} %sum.1), channel_id=1, source_target_pairs={{0,8},{1,9},{2,10},{3,11},{4,20},{5,21},{6,22},{7,23},{8,0},{9,1},... | collective-permute-start | bytes 835592 | tf_op jit(solution)/shard_map/ppermute | solution.py:73
  73.5 2.3 %collective-permute-done.32 = bf16[64,2176]{1,0:T(8,128)(2,1)S(1)} collective-permute-done((bf16[64,2176]{1,0:T(8,128)(2,1)S(1)}, bf16[64,2176]{1,0:T(8,128)(2,1)S(1)}, u32[]{:S(2)}, u32[]{:S(2)}) %collective-permute-start.32) | collective-permute-done | bytes 278560 | tf_op jit(solution)/shard_map/ppermute | solution.py:73
  77.4 4.3 %collective-permute-done.23.refs_2_ = bf16[64,2176]{1,0:T(8,128)(2,1)S(1)} collective-permute-done((bf16[64,2176]{1,0:T(8,128)(2,1)S(1)}, bf16[64,2176]{1,0:T(8,128)(2,1)S(1)}, u32[]{:S(2)}, u32[]{:S(2)}) %collective-permute-start.23) | collective-permute-done | bytes 278560 | tf_op jit(solution)/shard_map/ppermute | solution.py:73
  84.0 3.0 %collective-permute-start.30 = (bf16[16,2176]{1,0:T(8,128)(2,1)S(1)}, bf16[16,2176]{1,0:T(8,128)(2,1)S(1)}, u32[]{:S(2)}, u32[]{:S(2)}) collective-permute-start(bf16[16,2176]{1,0:T(8,128)(2,1)S(1)} %get-tuple-element.59), channel_id=1, source_target_pairs={{0,3},{1,2},{2,1},{3,0},{4,7},{5,6},{6,5},{7,4},{8,11},{9,10},{10,... | collective-permute-start | bytes 208904 | tf_op jit(solution)/shard_map/ppermute | solution.py:49
  89.3 3.0 %collective-permute-start.36 = (bf16[16,2176]{1,0:T(8,128)(2,1)S(1)}, bf16[16,2176]{1,0:T(8,128)(2,1)S(1)}, u32[]{:S(2)}, u32[]{:S(2)}) collective-permute-start(bf16[16,2176]{1,0:T(8,128)(2,1)S(1)} %get-tuple-element.63), channel_id=1, source_target_pairs={{0,3},{1,2},{2,1},{3,0},{4,7},{5,6},{6,5},{7,4},{8,11},{9,10},{10,... | collective-permute-start | bytes 208904 | tf_op jit(solution)/shard_map/ppermute | solution.py:49
  92.3 3.7 %collective-permute-done.35 = bf16[16,2176]{1,0:T(8,128)(2,1)S(1)} collective-permute-done((bf16[16,2176]{1,0:T(8,128)(2,1)S(1)}, bf16[16,2176]{1,0:T(8,128)(2,1)S(1)}, u32[]{:S(2)}, u32[]{:S(2)}) %collective-permute-start.35) | collective-permute-done | bytes 69664 | tf_op jit(solution)/shard_map/ppermute | solution.py:49
  96.1 2.2 %collective-permute-start.41 = (bf16[32,2176]{1,0:T(8,128)(2,1)S(1)}, bf16[32,2176]{1,0:T(8,128)(2,1)S(1)}, u32[]{:S(2)}, u32[]{:S(2)}) collective-permute-start(bf16[32,2176]{1,0:T(8,128)(2,1)S(1)} %pad_maximum_fusion.1), channel_id=1, source_target_pairs={{0,2},{1,3},{2,0},{3,1},{4,6},{5,7},{6,4},{7,5},{8,10},{9,11},{10,... | collective-permute-start | bytes 417800 | tf_op jit(solution)/shard_map/ppermute | solution.py:49
  99.8 8.0 %collective-permute-done.41 = bf16[32,2176]{1,0:T(8,128)(2,1)S(1)} collective-permute-done((bf16[32,2176]{1,0:T(8,128)(2,1)S(1)}, bf16[32,2176]{1,0:T(8,128)(2,1)S(1)}, u32[]{:S(2)}, u32[]{:S(2)}) %collective-permute-start.41) | collective-permute-done | bytes 139296 | tf_op jit(solution)/shard_map/ppermute | solution.py:49
  111.7 1.6 %collective-permute-start.46 = (bf16[64,2176]{1,0:T(8,128)(2,1)S(1)}, bf16[64,2176]{1,0:T(8,128)(2,1)S(1)}, u32[]{:S(2)}, u32[]{:S(2)}) collective-permute-start(bf16[64,2176]{1,0:T(8,128)(2,1)S(1)} %pad_maximum_fusion.refs_0_), channel_id=1, source_target_pairs={{0,16},{1,17},{2,18},{3,19},{4,12},{5,13},{6,14},{7,15},{8,24},{9,... | collective-permute-start | bytes 835592 | tf_op jit(solution)/shard_map/ppermute | solution.py:73
  113.3 1.8 %collective-permute-done.43.refs_4_ = bf16[64,2176]{1,0:T(8,128)(2,1)S(1)} collective-permute-done((bf16[64,2176]{1,0:T(8,128)(2,1)S(1)}, bf16[64,2176]{1,0:T(8,128)(2,1)S(1)}, u32[]{:S(2)}, u32[]{:S(2)}) %collective-permute-start.43) | collective-permute-done | bytes 278560 | tf_op jit(solution)/shard_map/ppermute | solution.py:73
  115.1 2.7 %collective-permute-start.44 = (bf16[64,2176]{1,0:T(8,128)(2,1)S(1)}, bf16[64,2176]{1,0:T(8,128)(2,1)S(1)}, u32[]{:S(2)}, u32[]{:S(2)}) collective-permute-start(bf16[64,2176]{1,0:T(8,128)(2,1)S(1)} %collective-permute-done.43.refs_4_), channel_id=1, source_target_pairs={{0,16},{1,17},{2,18},{3,19},{4,12},{5,13},{6,14},{7,15},{8,24},{9,... | collective-permute-start | bytes 835592 | tf_op jit(solution)/shard_map/ppermute | solution.py:73
  117.7 3.3 %collective-permute-done.38.refs_0_ = bf16[64,2176]{1,0:T(8,128)(2,1)S(1)} collective-permute-done((bf16[64,2176]{1,0:T(8,128)(2,1)S(1)}, bf16[64,2176]{1,0:T(8,128)(2,1)S(1)}, u32[]{:S(2)}, u32[]{:S(2)}) %collective-permute-start.38) | collective-permute-done | bytes 278560 | tf_op jit(solution)/shard_map/ppermute | solution.py:73
  121.1 2.7 %collective-permute-start.39 = (bf16[64,2176]{1,0:T(8,128)(2,1)S(1)}, bf16[64,2176]{1,0:T(8,128)(2,1)S(1)}, u32[]{:S(2)}, u32[]{:S(2)}) collective-permute-start(bf16[64,2176]{1,0:T(8,128)(2,1)S(1)} %collective-permute-done.38.refs_0_), channel_id=1, source_target_pairs={{0,16},{1,17},{2,18},{3,19},{4,12},{5,13},{6,14},{7,15},{8,24},{9,... | collective-permute-start | bytes 835592 | tf_op jit(solution)/shard_map/ppermute | solution.py:73
  124.2 3.9 %last.3 = (bf16[8,224,2048]{2,1,0:T(8,128)(2,1)}, bf16[8,224,2048]{2,1,0:T(8,128)(2,1)}, bf16[3,512,128]{2,1,0:T(8,128)(2,1)S(1)}) custom-call(s32[3,8]{1,0:T(4,128)S(1)} %get-tuple-element.39.where, bf16[8,224,2048]{2,1,0:T(8,128)(2,1)S(1)} %add.108.c_ref, f32[2,224,128]{2,1,0:T(8,128)S(1)} %get-tuple-element.65.left_ref, ...), custom_call_target="tpu_custom_call" | custom-call | flops 3758096384 | bytes 7602176 | tf_op jit(solution)/shard_map/last/pallas_call | solution.py:341
  129.3 6.4 %last.4 = (bf16[8,224,2048]{2,1,0:T(8,128)(2,1)}, bf16[8,224,2048]{2,1,0:T(8,128)(2,1)}, bf16[3,512,128]{2,1,0:T(8,128)(2,1)S(1)}) custom-call(s32[3,8]{1,0:T(4,128)S(1)} %get-tuple-element.39.where, bf16[8,224,2048]{2,1,0:T(8,128)(2,1)S(1)} %add.108.c_ref, ...), custom_call_target="tpu_custom_call", output_to_operand_aliasing={{0}: (12, {}), {1}: (13, {})} | custom-call | flops 7516192768 | bytes 15204352 | tf_op jit(solution)/shard_map/last/pallas_call | solution.py:341
  135.7 3.9 %last.5 = (bf16[8,224,2048]{2,1,0:T(8,128)(2,1)}, bf16[8,224,2048]{2,1,0:T(8,128)(2,1)}, bf16[3,512,128]{2,1,0:T(8,128)(2,1)}) custom-call(s32[3,8]{1,0:T(4,128)S(1)} %get-tuple-element.39.where, bf16[8,224,2048]{2,1,0:T(8,128)(2,1)S(1)} %add.108.c_ref, f32[2,224,128]{2,1,0:T(8,128)S(1)} %get-tuple-element.47.left_ref, ...), custom_call_target="tpu_custom_call", output_to_operand_aliasing={{0}: (8, {}), {1}: (9, {})} | custom-call | flops 3758096384 | bytes 7602176 | tf_op jit(solution)/shard_map/last/pallas_call | solution.py:341
  (114 shorter events, 33.7 us)
Async XLA Ops:
  6.6 12.3 %collective-permute-start.1 = (bf16[512,128]{1,0:T(8,128)(2,1)S(1)}, bf16[512,128]{1,0:T(8,128)(2,1)S(1)}, u32[]{:S(2)}, u32[]{:S(2)}) collective-permute-start(bf16[512,128]{1,0:T(8,128)(2,1)S(1)} %get-tuple-element.79), channel_id=1, source_target_pairs={{0,8},{1,9},{2,10},{3,11},{4,12},{5,13},{6,14},{7,15},{8,0},{9,1},... | collective-permute-start | bytes 393224 | tf_op jit(solution)/shard_map/ppermute | solution.py:41
  9.5 9.4 %collective-permute-start.2 = (bf16[512,128]{1,0:T(8,128)(2,1)S(1)}, bf16[512,128]{1,0:T(8,128)(2,1)S(1)}, u32[]{:S(2)}, u32[]{:S(2)}) collective-permute-start(bf16[512,128]{1,0:T(8,128)(2,1)S(1)} %get-tuple-element.81), channel_id=1, source_target_pairs={{0,16},{1,17},{2,18},{3,19},{4,20},{5,21},{6,22},{7,23},{8,24},{9,... | collective-permute-start | bytes 393224 | tf_op jit(solution)/shard_map/ppermute | solution.py:41
  11.0 7.9 %collective-permute-start.3 = (bf16[512,128]{1,0:T(8,128)(2,1)S(1)}, bf16[512,128]{1,0:T(8,128)(2,1)S(1)}, u32[]{:S(2)}, u32[]{:S(2)}) collective-permute-start(bf16[512,128]{1,0:T(8,128)(2,1)S(1)} %get-tuple-element.80), channel_id=1, source_target_pairs={{0,24},{1,25},{2,26},{3,27},{4,28},{5,29},{6,30},{7,31},{8,16},{9,... | collective-permute-start | bytes 393224 | tf_op jit(solution)/shard_map/ppermute | solution.py:41
  19.0 12.9 %collective-permute-start.8 = (bf16[512,128]{1,0:T(8,128)(2,1)S(1)}, bf16[512,128]{1,0:T(8,128)(2,1)S(1)}, u32[]{:S(2)}, u32[]{:S(2)}) collective-permute-start(bf16[512,128]{1,0:T(8,128)(2,1)S(1)} %fusion.6), channel_id=1, source_target_pairs={{0,2},{1,3},{2,0},{3,1},{4,6},{5,7},{6,4},{7,5},{8,10},{9,11},{10,... | collective-permute-start | bytes 393224 | tf_op jit(solution)/shard_map/ppermute | solution.py:49
  22.1 9.8 %collective-permute-start.9 = (bf16[512,128]{1,0:T(8,128)(2,1)S(1)}, bf16[512,128]{1,0:T(8,128)(2,1)S(1)}, u32[]{:S(2)}, u32[]{:S(2)}) collective-permute-start(bf16[512,128]{1,0:T(8,128)(2,1)S(1)} %fusion.6), channel_id=1, source_target_pairs={{0,3},{1,2},{2,1},{3,0},{4,7},{5,6},{6,5},{7,4},{8,11},{9,10},{10,... | collective-permute-start | bytes 393224 | tf_op jit(solution)/shard_map/ppermute | solution.py:49
  23.4 10.0 %collective-permute-start.4 = (bf16[512,128]{1,0:T(8,128)(2,1)S(1)}, bf16[512,128]{1,0:T(8,128)(2,1)S(1)}, u32[]{:S(2)}, u32[]{:S(2)}) collective-permute-start(bf16[512,128]{1,0:T(8,128)(2,1)S(1)} %fusion.6), channel_id=1, source_target_pairs={{0,1},{1,0},{2,3},{3,2},{4,5},{5,4},{6,7},{7,6},{8,9},{9,8},{10,11... | collective-permute-start | bytes 393224 | tf_op jit(solution)/shard_map/ppermute | solution.py:49
  31.9 7.6 %collective-permute-start.10 = (bf16[1024,128]{1,0:T(8,128)(2,1)S(1)}, bf16[1024,128]{1,0:T(8,128)(2,1)S(1)}, u32[]{:S(2)}, u32[]{:S(2)}) collective-permute-start(bf16[1024,128]{1,0:T(8,128)(2,1)S(1)} %constant_dynamic-update-slice_fusion.2.refs_2_), channel_id=1, source_target_pairs={{0,8},{1,9},{2,10},{3,11},{4,20},{5,21},{6,22},{7,23},{8,0},{9,1},... | collective-permute-start | bytes 786440 | tf_op jit(solution)/shard_map/ppermute | solution.py:73
  33.5 11.6 %collective-permute-start.5 = (bf16[1024,128]{1,0:T(8,128)(2,1)S(1)}, bf16[1024,128]{1,0:T(8,128)(2,1)S(1)}, u32[]{:S(2)}, u32[]{:S(2)}) collective-permute-start(bf16[1024,128]{1,0:T(8,128)(2,1)S(1)} %constant_dynamic-update-slice_fusion.refs_0_), channel_id=1, source_target_pairs={{0,8},{1,9},{2,10},{3,11},{4,20},{5,21},{6,22},{7,23},{8,0},{9,1},... | collective-permute-start | bytes 786440 | tf_op jit(solution)/shard_map/ppermute | solution.py:73
  34.1 13.1 %collective-permute-start.14 = (bf16[1024,128]{1,0:T(8,128)(2,1)S(1)}, bf16[1024,128]{1,0:T(8,128)(2,1)S(1)}, u32[]{:S(2)}, u32[]{:S(2)}) collective-permute-start(bf16[1024,128]{1,0:T(8,128)(2,1)S(1)} %constant_dynamic-update-slice_fusion.2.refs_2_), channel_id=1, source_target_pairs={{0,4},{1,5},{2,6},{3,7},{4,0},{5,1},{6,2},{7,3},{8,12},{9,13},{10,... | collective-permute-start | bytes 786440 | tf_op jit(solution)/shard_map/ppermute | solution.py:41
  39.5 9.2 %collective-permute-start.11 = (bf16[1024,128]{1,0:T(8,128)(2,1)S(1)}, bf16[1024,128]{1,0:T(8,128)(2,1)S(1)}, u32[]{:S(2)}, u32[]{:S(2)}) collective-permute-start(bf16[1024,128]{1,0:T(8,128)(2,1)S(1)} %collective-permute-done.10.refs_4_), channel_id=1, source_target_pairs={{0,16},{1,17},{2,18},{3,19},{4,12},{5,13},{6,14},{7,15},{8,24},{9,... | collective-permute-start | bytes 786440 | tf_op jit(solution)/shard_map/ppermute | solution.py:73
  46.6 7.7 %collective-permute-start.19 = (bf16[1024,128]{1,0:T(8,128)(2,1)S(1)}, bf16[1024,128]{1,0:T(8,128)(2,1)S(1)}, u32[]{:S(2)}, u32[]{:S(2)}) collective-permute-start(bf16[1024,128]{1,0:T(8,128)(2,1)S(1)} %constant_dynamic-update-slice_fusion.2.refs_2_), channel_id=1, source_target_pairs={{0,16},{1,17},{2,18},{3,19},{4,12},{5,13},{6,14},{7,15},{8,24},{9,... | collective-permute-start | bytes 786440 | tf_op jit(solution)/shard_map/ppermute | solution.py:73
  47.1 10.0 %collective-permute-start.16 = (bf16[1024,128]{1,0:T(8,128)(2,1)S(1)}, bf16[1024,128]{1,0:T(8,128)(2,1)S(1)}, u32[]{:S(2)}, u32[]{:S(2)}) collective-permute-start(bf16[1024,128]{1,0:T(8,128)(2,1)S(1)} %constant_dynamic-update-slice_fusion.refs_0_), channel_id=1, source_target_pairs={{0,16},{1,17},{2,18},{3,19},{4,12},{5,13},{6,14},{7,15},{8,24},{9,... | collective-permute-start | bytes 786440 | tf_op jit(solution)/shard_map/ppermute | solution.py:73
  48.7 8.4 %collective-permute-start.12 = (bf16[1024,128]{1,0:T(8,128)(2,1)S(1)}, bf16[1024,128]{1,0:T(8,128)(2,1)S(1)}, u32[]{:S(2)}, u32[]{:S(2)}) collective-permute-start(bf16[1024,128]{1,0:T(8,128)(2,1)S(1)} %collective-permute-done.11.refs_2_), channel_id=1, source_target_pairs={{0,4},{1,5},{2,6},{3,7},{4,0},{5,1},{6,2},{7,3},{8,12},{9,13},{10,... | collective-permute-start | bytes 786440 | tf_op jit(solution)/shard_map/ppermute | solution.py:41
  53.7 23.7 %collective-permute-start.15 = (bf16[128,2176]{1,0:T(8,128)(2,1)S(1)}, bf16[128,2176]{1,0:T(8,128)(2,1)S(1)}, u32[]{:S(2)}, u32[]{:S(2)}) collective-permute-start(bf16[128,2176]{1,0:T(8,128)(2,1)S(1)} %get-tuple-element.49), channel_id=1, source_target_pairs={{0,4},{1,5},{2,6},{3,7},{4,0},{5,1},{6,2},{7,3},{8,12},{9,13},{10,... | collective-permute-start | bytes 1671176 | tf_op jit(solution)/shard_map/ppermute | solution.py:41
  66.8 9.0 %collective-permute-start.32 = (bf16[64,2176]{1,0:T(8,128)(2,1)S(1)}, bf16[64,2176]{1,0:T(8,128)(2,1)S(1)}, u32[]{:S(2)}, u32[]{:S(2)}) collective-permute-start(bf16[64,2176]{1,0:T(8,128)(2,1)S(1)} %get-tuple-element.76), channel_id=1, source_target_pairs={{0,16},{1,17},{2,18},{3,19},{4,12},{5,13},{6,14},{7,15},{8,24},{9,... | collective-permute-start | bytes 835592 | tf_op jit(solution)/shard_map/ppermute | solution.py:73
  67.4 14.3 %collective-permute-start.23 = (bf16[64,2176]{1,0:T(8,128)(2,1)S(1)}, bf16[64,2176]{1,0:T(8,128)(2,1)S(1)}, u32[]{:S(2)}, u32[]{:S(2)}) collective-permute-start(bf16[64,2176]{1,0:T(8,128)(2,1)S(1)} %get-tuple-element.77), channel_id=1, source_target_pairs={{0,16},{1,17},{2,18},{3,19},{4,12},{5,13},{6,14},{7,15},{8,24},{9,... | collective-permute-start | bytes 835592 | tf_op jit(solution)/shard_map/ppermute | solution.py:73
  69.0 18.0 %collective-permute-start.31 = (bf16[64,2176]{1,0:T(8,128)(2,1)S(1)}, bf16[64,2176]{1,0:T(8,128)(2,1)S(1)}, u32[]{:S(2)}, u32[]{:S(2)}) collective-permute-start(bf16[64,2176]{1,0:T(8,128)(2,1)S(1)} %get-tuple-element.78), channel_id=1, source_target_pairs={{0,16},{1,17},{2,18},{3,19},{4,12},{5,13},{6,14},{7,15},{8,24},{9,... | collective-permute-start | bytes 835592 | tf_op jit(solution)/shard_map/ppermute | solution.py:73
  71.9 9.8 %collective-permute-start.27 = (bf16[64,2176]{1,0:T(8,128)(2,1)S(1)}, bf16[64,2176]{1,0:T(8,128)(2,1)S(1)}, u32[]{:S(2)}, u32[]{:S(2)}) collective-permute-start(bf16[64,2176]{1,0:T(8,128)(2,1)S(1)} %sum.1), channel_id=1, source_target_pairs={{0,8},{1,9},{2,10},{3,11},{4,20},{5,21},{6,22},{7,23},{8,0},{9,1},... | collective-permute-start | bytes 835592 | tf_op jit(solution)/shard_map/ppermute | solution.py:73
  75.9 11.1 %collective-permute-start.33 = (bf16[64,2176]{1,0:T(8,128)(2,1)S(1)}, bf16[64,2176]{1,0:T(8,128)(2,1)S(1)}, u32[]{:S(2)}, u32[]{:S(2)}) collective-permute-start(bf16[64,2176]{1,0:T(8,128)(2,1)S(1)} %add_convert_fusion), channel_id=1, source_target_pairs={{0,8},{1,9},{2,10},{3,11},{4,20},{5,21},{6,22},{7,23},{8,0},{9,1},... | collective-permute-start | bytes 835592 | tf_op jit(solution)/shard_map/ppermute | solution.py:73
  82.6 9.7 %collective-permute-start.29 = (bf16[16,2176]{1,0:T(8,128)(2,1)S(1)}, bf16[16,2176]{1,0:T(8,128)(2,1)S(1)}, u32[]{:S(2)}, u32[]{:S(2)}) collective-permute-start(bf16[16,2176]{1,0:T(8,128)(2,1)S(1)} %get-tuple-element.58), channel_id=1, source_target_pairs={{0,2},{1,3},{2,0},{3,1},{4,6},{5,7},{6,4},{7,5},{8,10},{9,11},{10,... | collective-permute-start | bytes 208904 | tf_op jit(solution)/shard_map/ppermute | solution.py:49
  84.0 8.2 %collective-permute-start.30 = (bf16[16,2176]{1,0:T(8,128)(2,1)S(1)}, bf16[16,2176]{1,0:T(8,128)(2,1)S(1)}, u32[]{:S(2)}, u32[]{:S(2)}) collective-permute-start(bf16[16,2176]{1,0:T(8,128)(2,1)S(1)} %get-tuple-element.59), channel_id=1, source_target_pairs={{0,3},{1,2},{2,1},{3,0},{4,7},{5,6},{6,5},{7,4},{8,11},{9,10},{10,... | collective-permute-start | bytes 208904 | tf_op jit(solution)/shard_map/ppermute | solution.py:49
  87.9 8.1 %collective-permute-start.35 = (bf16[16,2176]{1,0:T(8,128)(2,1)S(1)}, bf16[16,2176]{1,0:T(8,128)(2,1)S(1)}, u32[]{:S(2)}, u32[]{:S(2)}) collective-permute-start(bf16[16,2176]{1,0:T(8,128)(2,1)S(1)} %get-tuple-element.62), channel_id=1, source_target_pairs={{0,2},{1,3},{2,0},{3,1},{4,6},{5,7},{6,4},{7,5},{8,10},{9,11},{10,... | collective-permute-start | bytes 208904 | tf_op jit(solution)/shard_map/ppermute | solution.py:49
  96.1 11.7 %collective-permute-start.41 = (bf16[32,2176]{1,0:T(8,128)(2,1)S(1)}, bf16[32,2176]{1,0:T(8,128)(2,1)S(1)}, u32[]{:S(2)}, u32[]{:S(2)}) collective-permute-start(bf16[32,2176]{1,0:T(8,128)(2,1)S(1)} %pad_maximum_fusion.1), channel_id=1, source_target_pairs={{0,2},{1,3},{2,0},{3,1},{4,6},{5,7},{6,4},{7,5},{8,10},{9,11},{10,... | collective-permute-start | bytes 417800 | tf_op jit(solution)/shard_map/ppermute | solution.py:49
  98.3 9.5 %collective-permute-start.42 = (bf16[32,2176]{1,0:T(8,128)(2,1)S(1)}, bf16[32,2176]{1,0:T(8,128)(2,1)S(1)}, u32[]{:S(2)}, u32[]{:S(2)}) collective-permute-start(bf16[32,2176]{1,0:T(8,128)(2,1)S(1)} %pad_maximum_fusion.1), channel_id=1, source_target_pairs={{0,3},{1,2},{2,1},{3,0},{4,7},{5,6},{6,5},{7,4},{8,11},{9,10},{10,... | collective-permute-start | bytes 417800 | tf_op jit(solution)/shard_map/ppermute | solution.py:49
  99.8 9.6 %collective-permute-start.37 = (bf16[32,2176]{1,0:T(8,128)(2,1)S(1)}, bf16[32,2176]{1,0:T(8,128)(2,1)S(1)}, u32[]{:S(2)}, u32[]{:S(2)}) collective-permute-start(bf16[32,2176]{1,0:T(8,128)(2,1)S(1)} %pad_maximum_fusion.1), channel_id=1, source_target_pairs={{0,1},{1,0},{2,3},{3,2},{4,5},{5,4},{6,7},{7,6},{8,9},{9,8},{10,11... | collective-permute-start | bytes 417800 | tf_op jit(solution)/shard_map/ppermute | solution.py:49
  109.8 11.3 %collective-permute-start.38 = (bf16[64,2176]{1,0:T(8,128)(2,1)S(1)}, bf16[64,2176]{1,0:T(8,128)(2,1)S(1)}, u32[]{:S(2)}, u32[]{:S(2)}) collective-permute-start(bf16[64,2176]{1,0:T(8,128)(2,1)S(1)} %pad_maximum_fusion.refs_0_), channel_id=1, source_target_pairs={{0,8},{1,9},{2,10},{3,11},{4,20},{5,21},{6,22},{7,23},{8,0},{9,1},... | collective-permute-start | bytes 835592 | tf_op jit(solution)/shard_map/ppermute | solution.py:73
  111.2 9.8 %collective-permute-start.49 = (bf16[64,2176]{1,0:T(8,128)(2,1)S(1)}, bf16[64,2176]{1,0:T(8,128)(2,1)S(1)}, u32[]{:S(2)}, u32[]{:S(2)}) collective-permute-start(bf16[64,2176]{1,0:T(8,128)(2,1)S(1)} %constant_dynamic-update-slice_fusion.4.refs_2_), channel_id=1, source_target_pairs={{0,16},{1,17},{2,18},{3,19},{4,12},{5,13},{6,14},{7,15},{8,24},{9,... | collective-permute-start | bytes 835592 | tf_op jit(solution)/shard_map/ppermute | solution.py:73
  111.7 12.0 %collective-permute-start.46 = (bf16[64,2176]{1,0:T(8,128)(2,1)S(1)}, bf16[64,2176]{1,0:T(8,128)(2,1)S(1)}, u32[]{:S(2)}, u32[]{:S(2)}) collective-permute-start(bf16[64,2176]{1,0:T(8,128)(2,1)S(1)} %pad_maximum_fusion.refs_0_), channel_id=1, source_target_pairs={{0,16},{1,17},{2,18},{3,19},{4,12},{5,13},{6,14},{7,15},{8,24},{9,... | collective-permute-start | bytes 835592 | tf_op jit(solution)/shard_map/ppermute | solution.py:73
  115.1 8.6 %collective-permute-start.50 = (bf16[64,2176]{1,0:T(8,128)(2,1)S(1)}, bf16[64,2176]{1,0:T(8,128)(2,1)S(1)}, u32[]{:S(2)}, u32[]{:S(2)}) collective-permute-start(bf16[64,2176]{1,0:T(8,128)(2,1)S(1)} %collective-permute-done.43.refs_4_), channel_id=1, source_target_pairs={{0,4},{1,5},{2,6},{3,7},{4,0},{5,1},{6,2},{7,3},{8,12},{9,13},{10,... | collective-permute-start | bytes 835592 | tf_op jit(solution)/shard_map/ppermute | solution.py:41
  115.1 13.1 %collective-permute-start.44 = (bf16[64,2176]{1,0:T(8,128)(2,1)S(1)}, bf16[64,2176]{1,0:T(8,128)(2,1)S(1)}, u32[]{:S(2)}, u32[]{:S(2)}) collective-permute-start(bf16[64,2176]{1,0:T(8,128)(2,1)S(1)} %collective-permute-done.43.refs_4_), channel_id=1, source_target_pairs={{0,16},{1,17},{2,18},{3,19},{4,12},{5,13},{6,14},{7,15},{8,24},{9,... | collective-permute-start | bytes 835592 | tf_op jit(solution)/shard_map/ppermute | solution.py:73
  121.0 8.2 %collective-permute-start.47 = (bf16[64,2176]{1,0:T(8,128)(2,1)S(1)}, bf16[64,2176]{1,0:T(8,128)(2,1)S(1)}, u32[]{:S(2)}, u32[]{:S(2)}) collective-permute-start(bf16[64,2176]{1,0:T(8,128)(2,1)S(1)} %collective-permute-done.38.refs_0_), channel_id=1, source_target_pairs={{0,4},{1,5},{2,6},{3,7},{4,0},{5,1},{6,2},{7,3},{8,12},{9,13},{10,... | collective-permute-start | bytes 835592 | tf_op jit(solution)/shard_map/ppermute | solution.py:41
  121.1 7.8 %collective-permute-start.39 = (bf16[64,2176]{1,0:T(8,128)(2,1)S(1)}, bf16[64,2176]{1,0:T(8,128)(2,1)S(1)}, u32[]{:S(2)}, u32[]{:S(2)}) collective-permute-start(bf16[64,2176]{1,0:T(8,128)(2,1)S(1)} %collective-permute-done.38.refs_0_), channel_id=1, source_target_pairs={{0,16},{1,17},{2,18},{3,19},{4,12},{5,13},{6,14},{7,15},{8,24},{9,... | collective-permute-start | bytes 835592 | tf_op jit(solution)/shard_map/ppermute | solution.py:73
  (27 other events, 122.2 us)

commit v3 on v2

--- a/solution.py
+++ b/solution.py
@@ -282,7 +282,8 @@
     return outs[0], outs[1:]
 
 
-def last_body(count, multiplier, cap, base, fresh, where, c_ref, left_ref, *refs):
+def last_body(count, multiplier, cap, base, fresh, where, c_ref, *refs):
+    left_refs, refs = refs[: count // 2], refs[count // 2 :]
     right_refs, refs = refs[: 2 * count], refs[2 * count :]
     mom_ref, upd_ref, q_ref, buf = refs[-4:]
     step = pl.program_id(0)
@@ -295,23 +296,30 @@
             q_ref[...] = refs[0][...]
 
     hidden = c_ref.shape[2]
-    halves = [pick(right_refs[:count]), pick(right_refs[count:])]
     shard_count = hidden // q_ref.shape[1]
     piece = buf.shape[0] // (2 * shard_count)
-    for d in range(shard_count):
-        start = (where[2, 0] ^ d) * piece
-        half, at = divmod(d, shard_count // 2)
-        for i in (0, 1):
-            rows = halves[half][(2 * at + i) * piece : (2 * at + i + 1) * piece]
-            to = pl.multiple_of(start + i * piece * shard_count, piece)
-            buf[pl.ds(to, piece), :] = rows.astype(jnp.float32)
+    for j in range(count):
+
+        @pl.when(step == j)
+        def _():
+            for d in range(shard_count):
+                half, at = divmod(d, shard_count // 2)
+                ref = right_refs[half * count + j]
+                for i in (0, 1):
+                    rows = ref[(2 * at + i) * piece : (2 * at + i + 1) * piece, :]
+                    to = ((where[2, 0] ^ d) + i * shard_count) * piece
+                    buf[pl.ds(pl.multiple_of(to, piece), piece), :] = rows.astype(jnp.float32)
+
     arrived = buf[...]
     squares = arrived[:, hidden : hidden + 1]
     n_col = lax.rsqrt(squares + stability_offset)
     n_row = jnp.broadcast_to(n_col, (n_col.shape[0],) * 2).T[0:1, :]
     n_col = n_col * UP
-    left = (left_ref[0] * n_row).astype(jnp.bfloat16)
-    right = arrived[:, :hidden] * n_col
+    left = left_refs[0][0]
+    for j in range(1, count // 2):
+        left = jnp.where(step // 2 == j, left_refs[j][0], left)
+    left = (left * n_row).astype(jnp.bfloat16)
+    right = jnp.where(n_col > 0.0, arrived[:, :hidden] * n_col, 0.0)
     total = jnp.sum(right * right, axis=1, keepdims=True)
     scale = lax.rsqrt(total / right.shape[1] + stability_offset)
     low = jnp.dot(left, right.astype(jnp.bfloat16), preferred_element_type=jnp.float32)
@@ -326,13 +334,13 @@
     def _():
         share = q_ref.shape[1]
         start = pl.multiple_of(where[2, 0] * share, share)
-        own = buf[:, pl.ds(start, share)] * n_col * scale
+        own = jnp.where(n_col > 0.0, buf[:, pl.ds(start, share)] * n_col, 0.0) * scale
         q_ref[slot] = own.T.astype(jnp.bfloat16)
 
 
 def last_call(where, base, combined, left, rights, outs, cap, share, multiplier):
     experts, rows, hidden = combined.shape
-    count = len(rights) // 2
+    count, pairs = len(rights) // 2, len(left)
     rank, width = rights[0].shape
     rank *= 2
     block = pl.BlockSpec((1, rows, hidden), lambda i, w: (w[0, base + i], 0, 0))
@@ -343,9 +351,10 @@
         grid_spec=pltpu.PrefetchScalarGridSpec(
             num_scalar_prefetch=1,
             grid=(count,),
-            in_specs=[
-                block,
-                pl.BlockSpec((1, rows, rank), lambda i, w: (i, 0, 0)),
+            in_specs=[block]
+            + [
+                pl.BlockSpec((1, rows, rank), lambda i, w, j=j: (jnp.clip(i - 2 * j, 0, 1), 0, 0))
+                for j in range(len(left))
             ]
             + [pl.BlockSpec(memory_space=pltpu.VMEM)] * len(rights)
             + ([] if outs is None else [fixed((cap, share, rank)), anywhere, anywhere]),
@@ -357,7 +366,7 @@
             jax.ShapeDtypeStruct((experts, rows, hidden), jnp.bfloat16),
             jax.ShapeDtypeStruct((cap, share, rank), jnp.bfloat16),
         ],
-        input_output_aliases={} if outs is None else {4 + 2 * count: 0, 5 + 2 * count: 1},
+        input_output_aliases={} if outs is None else {3 + pairs + 2 * count: 0, 4 + pairs + 2 * count: 1},
         cost_estimate=pl.CostEstimate(
             flops=WEIGHT * count * 4 * rows * hidden * rank,
             bytes_accessed=count * 2 * (3 * rows + 2 * rank) * hidden,
@@ -365,7 +374,7 @@
         ),
         compiler_params=pltpu.CompilerParams(vmem_limit_bytes=GRANT),
         name="last",
-    )(where, combined, left, *rights, *extra)
+    )(where, combined, *left, *rights, *extra)
 
 
 def step(momentum, gradient, q_prev, owner_group, group_counts):
@@ -377,17 +386,15 @@
     links = Links(groups, shard_count)
     near, orders = links.orders()
 
-    names = range(1 << links.levels())
-    most = max(name.bit_count() for name in names)
-    sets = [[name for name in names if name.bit_count() == n] for n in range(most + 1)]
+    names = in_order(links.levels())
+    sets = [[n for n in names if n.bit_count() == i] for i in range(links.levels() + 1)]
 
     def distances(side):
         reach = lambda name, at: sum(bit for i, bit in enumerate(orders[at]) if name >> i & 1)
         return [
             reach(name, side ^ far) ^ (near if far else 0)
-            for members in sets
+            for name in names
             for far in (0, 1)
-            for name in members
         ]
 
     uppers = [r for r in range(groups) if not r & near]
@@ -405,24 +412,11 @@
     qs = [links.spread(part) for part in q_full]
     qs_far = [{n: links.swap_group(x, near) for n, x in part.items()} for part in qs]
 
-    lefts, rights, bases = [], {}, []
-    base = 0
-    for members in sets:
-        count = len(members)
-        left, outs = first_call(
-            where,
-            base,
-            combined,
-            [
-                side[half][n] for half in (0, 1) for side in (qs, qs_far) for n in members
-            ],
-            shard_count,
-        )
-        lefts.append(left)
-        for j, name in enumerate(members):
-            rights[name] = [outs[j], links.swap_group(outs[count + j], near)]
-        bases.append(base)
-        base += 2 * count
+    lefts, rights = {}, {}
+    for i, name in enumerate(names):
+        pieces = [side[half][name] for half in (0, 1) for side in (qs, qs_far)]
+        lefts[name], outs = first_call(where, 2 * i, combined, pieces, shard_count)
+        rights[name] = [outs[0], links.swap_group(outs[1], near)]
 
     own = rights.pop(0)
     sums = []
@@ -442,13 +436,21 @@
 
     multiplier = math.sqrt(block * groups * shard_count / rank)
     outs = None
-    for i, members in enumerate(sets):
+    for members in sets:
         pieces = [
-            side[half][n] for half in (0, 1) for side in (full, full_far) for n in members
+            side[half][n] for half in (0, 1) for n in members for side in (full, full_far)
         ]
-        outs = last_call(where, bases[i], combined, lefts[i], pieces, outs, cap, share, multiplier)
+        base = 2 * names.index(members[0])
+        left = [lefts[n] for n in members]
+        outs = last_call(
+            where, base, combined, left, pieces, outs, cap, share, multiplier
+        )
     momentum_next, update, q_next = outs
     return momentum_next, update, q_next[None]
+
+
+def in_order(levels):
+    return sorted(range(1 << levels), key=lambda name: (name.bit_count(), -name))
 
 
 def solution(mesh):

time: 140 us -> 141 us (level)
  waiting for transfers between devices: 51.1 us -> 56.6 us
  starting transfers between devices: 50.9 us -> 46.9 us
    ppermute x18, waiting for transfers between devices: 29.8 us -> 35.3 us  [cross(): return lax.ppermute(x, AXES, pairs)]
    ppermute x18, starting transfers between devices: 24.9 us -> 21.1 us  [cross(): return lax.ppermute(x, AXES, pairs)]
    pallas_call x3 -> x4, Pallas kernels: 8.38 us -> 8.77 us  [first_call(): pl.pallas_call(functools.partial(first_body, count, shard_count), grid_sp...]
  transfers between devices with their start and end apart: 54 -> 54, of which waited for: 14 -> 15; matrix products, arithmetic and copies ran while one was open for 0% -> 0% of each run, Pallas kernels for 16% -> 16%
where the time goes in v3:
time: 141 us
  waiting for transfers between devices  56.6 us (40%)
  starting transfers between devices  46.9 us (33%)
  Pallas kernels  27.6 us (20%)
  local copies, waits for them, and re-layouts  8.59 us (6%)
    ppermute x18, waiting for transfers between devices, cross(): return lax.ppermute(x, AXES, pairs)  35.3 us
    ppermute x18, starting transfers between devices, cross(): return lax.ppermute(x, AXES, pairs)  21.1 us
    ppermute x12, waiting for transfers between devices, swap_shard(): return lax.ppermute(x, AXES, pairs)  19.8 us
    ppermute x12, starting transfers between devices, swap_shard(): return lax.ppermute(x, AXES, pairs)  17.4 us
    pallas_call x3, Pallas kernels, last_call(): pl.pallas_call(functools.partial(last_body, count, multiplier, cap, base,...  13.9 us
    pallas_call x4, Pallas kernels, first_call(): pl.pallas_call(functools.partial(first_body, count, shard_count), grid_sp...  8.77 us
    unnamed x13, local copies, waits for them, and re-layouts  8.49 us
    ppermute x24, starting transfers between devices, swap_group(): return lax.ppermute(x, AXES, pairs)  8.46 us
  transfers between devices with their start and end apart: 54, of which 15 were waited for; matrix products, arithmetic and copies ran while one was open for 0% of the time, Pallas kernels for 16%

profile of v3, /device:TPU:0, one launch (start us, length us, event | category | flops | bytes accessed | tf_op | source)
XLA Modules:
  0.0 141.2 jit_solution(5313960411998074658)
XLA Ops:
  6.6 2.9 %collective-permute-start.1 = (bf16[512,128]{1,0:T(8,128)(2,1)S(1)}, bf16[512,128]{1,0:T(8,128)(2,1)S(1)}, u32[]{:S(2)}, u32[]{:S(2)}) collective-permute-start(bf16[512,128]{1,0:T(8,128)(2,1)S(1)} %get-tuple-element.81), channel_id=1, source_target_pairs={{0,8},{1,9},{2,10},{3,11},{4,12},{5,13},{6,14},{7,15},{8,0},{9,1},... | collective-permute-start | bytes 393224 | tf_op jit(solution)/shard_map/ppermute | solution.py:41
  11.0 3.1 %copy-done.3 = bf16[8,224,2048]{2,1,0:T(8,128)(2,1)S(1)} copy-done((bf16[8,224,2048]{2,1,0:T(8,128)(2,1)S(1)}, bf16[8,224,2048]{2,1,0:T(8,128)(2,1)}, u32[]{:S(2)}) %copy-start.3) | copy-done | bytes 7340056
  14.1 3.1 %copy-done.4 = bf16[8,224,2048]{2,1,0:T(8,128)(2,1)S(1)} copy-done((bf16[8,224,2048]{2,1,0:T(8,128)(2,1)S(1)}, bf16[8,224,2048]{2,1,0:T(8,128)(2,1)}, u32[]{:S(2)}) %copy-start.4) | copy-done | bytes 7340056
  17.2 1.7 %add.108.c_ref = bf16[8,224,2048]{2,1,0:T(8,128)(2,1)S(1)} custom-call(bf16[8,224,2048]{2,1,0:T(8,128)(2,1)S(1)} %copy-done.3, bf16[8,224,2048]{2,1,0:T(8,128)(2,1)S(1)} %copy-done.4), custom_call_target="tpu_custom_call" | custom-call | flops 7516192768 | bytes 22020096 | tf_op jit(solution)/shard_map/add/pallas_call | solution.py:155
  19.0 3.1 %collective-permute-start.8 = (bf16[512,128]{1,0:T(8,128)(2,1)S(1)}, bf16[512,128]{1,0:T(8,128)(2,1)S(1)}, u32[]{:S(2)}, u32[]{:S(2)}) collective-permute-start(bf16[512,128]{1,0:T(8,128)(2,1)S(1)} %fusion.6), channel_id=1, source_target_pairs={{0,2},{1,3},{2,0},{3,1},{4,6},{5,7},{6,4},{7,5},{8,10},{9,11},{10,... | collective-permute-start | bytes 393224 | tf_op jit(solution)/shard_map/ppermute | solution.py:49
  23.7 8.1 %collective-permute-done.8 = bf16[512,128]{1,0:T(8,128)(2,1)S(1)} collective-permute-done((bf16[512,128]{1,0:T(8,128)(2,1)S(1)}, bf16[512,128]{1,0:T(8,128)(2,1)S(1)}, u32[]{:S(2)}, u32[]{:S(2)}) %collective-permute-start.8) | collective-permute-done | bytes 131104 | tf_op jit(solution)/shard_map/ppermute | solution.py:49
  34.1 5.4 %collective-permute-done.10.refs_2_ = bf16[1024,128]{1,0:T(8,128)(2,1)S(1)} collective-permute-done((bf16[1024,128]{1,0:T(8,128)(2,1)S(1)}, bf16[1024,128]{1,0:T(8,128)(2,1)S(1)}, u32[]{:S(2)}, u32[]{:S(2)}) %collective-permute-start.10) | collective-permute-done | bytes 262176 | tf_op jit(solution)/shard_map/ppermute | solution.py:73
  41.0 4.1 %collective-permute-done.5.refs_0_ = bf16[1024,128]{1,0:T(8,128)(2,1)S(1)} collective-permute-done((bf16[1024,128]{1,0:T(8,128)(2,1)S(1)}, bf16[1024,128]{1,0:T(8,128)(2,1)S(1)}, u32[]{:S(2)}, u32[]{:S(2)}) %collective-permute-start.5) | collective-permute-done | bytes 262176 | tf_op jit(solution)/shard_map/ppermute | solution.py:73
  48.7 2.8 %collective-permute-done.6.refs_0_ = bf16[1024,128]{1,0:T(8,128)(2,1)S(1)} collective-permute-done((bf16[1024,128]{1,0:T(8,128)(2,1)S(1)}, bf16[1024,128]{1,0:T(8,128)(2,1)S(1)}, u32[]{:S(2)}, u32[]{:S(2)}) %collective-permute-start.6) | collective-permute-done | bytes 262176 | tf_op jit(solution)/shard_map/ppermute | solution.py:73
  51.5 2.2 %first.5 = (f32[2,224,128]{2,1,0:T(8,128)S(1)}, bf16[128,2176]{1,0:T(8,128)(2,1)S(1)}, bf16[128,2176]{1,0:T(8,128)(2,1)S(1)}) custom-call(s32[3,8]{1,0:T(4,128)S(1)} %get-tuple-element.40.where, bf16[8,224,2048]{2,1,0:T(8,128)(2,1)S(1)} %add.108.c_ref, bf16[1024,128]{1,0:T(8,128)(2,1)S(1)} %constant_dynamic-update-slice_fusion.refs_0_, ...), custom_call_target="tpu_custom_call" | custom-call | flops 3758096384 | bytes 3932160 | tf_op jit(solution)/shard_map/first/pallas_call | solution.py:262
  54.3 2.8 %collective-permute-done.16.refs_0_ = bf16[1024,128]{1,0:T(8,128)(2,1)S(1)} collective-permute-done((bf16[1024,128]{1,0:T(8,128)(2,1)S(1)}, bf16[1024,128]{1,0:T(8,128)(2,1)S(1)}, u32[]{:S(2)}, u32[]{:S(2)}) %collective-permute-start.16) | collective-permute-done | bytes 262176 | tf_op jit(solution)/shard_map/ppermute | solution.py:73
  57.7 2.2 %first.4 = (f32[2,224,128]{2,1,0:T(8,128)S(1)}, bf16[128,2176]{1,0:T(8,128)(2,1)S(1)}, bf16[128,2176]{1,0:T(8,128)(2,1)S(1)}) custom-call(s32[3,8]{1,0:T(4,128)S(1)} %get-tuple-element.40.where, bf16[8,224,2048]{2,1,0:T(8,128)(2,1)S(1)} %add.108.c_ref, bf16[1024,128]{1,0:T(8,128)(2,1)S(1)} %collective-permute-done.6.refs_0_, ...), custom_call_target="tpu_custom_call" | custom-call | flops 3758096384 | bytes 3932160 | tf_op jit(solution)/shard_map/first/pallas_call | solution.py:262
  60.4 2.2 %first.7 = (f32[2,224,128]{2,1,0:T(8,128)S(1)}, bf16[128,2176]{1,0:T(8,128)(2,1)S(1)}, bf16[128,2176]{1,0:T(8,128)(2,1)S(1)}) custom-call(s32[3,8]{1,0:T(4,128)S(1)} %get-tuple-element.40.where, bf16[8,224,2048]{2,1,0:T(8,128)(2,1)S(1)} %add.108.c_ref, bf16[1024,128]{1,0:T(8,128)(2,1)S(1)} %collective-permute-done.5.refs_0_, ...), custom_call_target="tpu_custom_call" | custom-call | flops 3758096384 | bytes 3932160 | tf_op jit(solution)/shard_map/first/pallas_call | solution.py:262
  62.8 2.2 %first.6 = (f32[2,224,128]{2,1,0:T(8,128)S(1)}, bf16[128,2176]{1,0:T(8,128)(2,1)S(1)}, bf16[128,2176]{1,0:T(8,128)(2,1)S(1)}) custom-call(s32[3,8]{1,0:T(4,128)S(1)} %get-tuple-element.40.where, bf16[8,224,2048]{2,1,0:T(8,128)(2,1)S(1)} %add.108.c_ref, bf16[1024,128]{1,0:T(8,128)(2,1)S(1)} %collective-permute-done.16.refs_0_, ...), custom_call_target="tpu_custom_call" | custom-call | flops 3758096384 | bytes 3932160 | tf_op jit(solution)/shard_map/first/pallas_call | solution.py:262
  65.6 1.6 %collective-permute-start.26 = (bf16[64,2176]{1,0:T(8,128)(2,1)S(1)}, bf16[64,2176]{1,0:T(8,128)(2,1)S(1)}, u32[]{:S(2)}, u32[]{:S(2)}) collective-permute-start(bf16[64,2176]{1,0:T(8,128)(2,1)S(1)} %get-tuple-element.77), channel_id=1, source_target_pairs={{0,16},{1,17},{2,18},{3,19},{4,12},{5,13},{6,14},{7,15},{8,24},{9,... | collective-permute-start | bytes 835592 | tf_op jit(solution)/shard_map/ppermute | solution.py:73
  67.8 1.6 %collective-permute-start.21 = (bf16[64,2176]{1,0:T(8,128)(2,1)S(1)}, bf16[64,2176]{1,0:T(8,128)(2,1)S(1)}, u32[]{:S(2)}, u32[]{:S(2)}) collective-permute-start(bf16[64,2176]{1,0:T(8,128)(2,1)S(1)} %get-tuple-element.79), channel_id=1, source_target_pairs={{0,16},{1,17},{2,18},{3,19},{4,12},{5,13},{6,14},{7,15},{8,24},{9,... | collective-permute-start | bytes 835592 | tf_op jit(solution)/shard_map/ppermute | solution.py:73
  69.9 2.3 %collective-permute-done.26.refs_2_ = bf16[64,2176]{1,0:T(8,128)(2,1)S(1)} collective-permute-done((bf16[64,2176]{1,0:T(8,128)(2,1)S(1)}, bf16[64,2176]{1,0:T(8,128)(2,1)S(1)}, u32[]{:S(2)}, u32[]{:S(2)}) %collective-permute-start.26) | collective-permute-done | bytes 278560 | tf_op jit(solution)/shard_map/ppermute | solution.py:73
  73.9 2.3 %collective-permute-done.32 = bf16[64,2176]{1,0:T(8,128)(2,1)S(1)} collective-permute-done((bf16[64,2176]{1,0:T(8,128)(2,1)S(1)}, bf16[64,2176]{1,0:T(8,128)(2,1)S(1)}, u32[]{:S(2)}, u32[]{:S(2)}) %collective-permute-start.32) | collective-permute-done | bytes 278560 | tf_op jit(solution)/shard_map/ppermute | solution.py:73
  76.3 1.6 %collective-permute-start.33 = (bf16[64,2176]{1,0:T(8,128)(2,1)S(1)}, bf16[64,2176]{1,0:T(8,128)(2,1)S(1)}, u32[]{:S(2)}, u32[]{:S(2)}) collective-permute-start(bf16[64,2176]{1,0:T(8,128)(2,1)S(1)} %add_convert_fusion), channel_id=1, source_target_pairs={{0,8},{1,9},{2,10},{3,11},{4,20},{5,21},{6,22},{7,23},{8,0},{9,1},... | collective-permute-start | bytes 835592 | tf_op jit(solution)/shard_map/ppermute | solution.py:73
  77.9 4.3 %collective-permute-done.21.refs_2_ = bf16[64,2176]{1,0:T(8,128)(2,1)S(1)} collective-permute-done((bf16[64,2176]{1,0:T(8,128)(2,1)S(1)}, bf16[64,2176]{1,0:T(8,128)(2,1)S(1)}, u32[]{:S(2)}, u32[]{:S(2)}) %collective-permute-start.21) | collective-permute-done | bytes 278560 | tf_op jit(solution)/shard_map/ppermute | solution.py:73
  84.4 3.0 %collective-permute-start.30 = (bf16[16,2176]{1,0:T(8,128)(2,1)S(1)}, bf16[16,2176]{1,0:T(8,128)(2,1)S(1)}, u32[]{:S(2)}, u32[]{:S(2)}) collective-permute-start(bf16[16,2176]{1,0:T(8,128)(2,1)S(1)} %get-tuple-element.60), channel_id=1, source_target_pairs={{0,3},{1,2},{2,1},{3,0},{4,7},{5,6},{6,5},{7,4},{8,11},{9,10},{10,... | collective-permute-start | bytes 208904 | tf_op jit(solution)/shard_map/ppermute | solution.py:49
  89.7 3.0 %collective-permute-start.36 = (bf16[16,2176]{1,0:T(8,128)(2,1)S(1)}, bf16[16,2176]{1,0:T(8,128)(2,1)S(1)}, u32[]{:S(2)}, u32[]{:S(2)}) collective-permute-start(bf16[16,2176]{1,0:T(8,128)(2,1)S(1)} %get-tuple-element.64), channel_id=1, source_target_pairs={{0,3},{1,2},{2,1},{3,0},{4,7},{5,6},{6,5},{7,4},{8,11},{9,10},{10,... | collective-permute-start | bytes 208904 | tf_op jit(solution)/shard_map/ppermute | solution.py:49
  92.7 3.7 %collective-permute-done.35 = bf16[16,2176]{1,0:T(8,128)(2,1)S(1)} collective-permute-done((bf16[16,2176]{1,0:T(8,128)(2,1)S(1)}, bf16[16,2176]{1,0:T(8,128)(2,1)S(1)}, u32[]{:S(2)}, u32[]{:S(2)}) %collective-permute-start.35) | collective-permute-done | bytes 69664 | tf_op jit(solution)/shard_map/ppermute | solution.py:49
  96.5 2.2 %collective-permute-start.41 = (bf16[32,2176]{1,0:T(8,128)(2,1)S(1)}, bf16[32,2176]{1,0:T(8,128)(2,1)S(1)}, u32[]{:S(2)}, u32[]{:S(2)}) collective-permute-start(bf16[32,2176]{1,0:T(8,128)(2,1)S(1)} %pad_maximum_fusion.1), channel_id=1, source_target_pairs={{0,2},{1,3},{2,0},{3,1},{4,6},{5,7},{6,4},{7,5},{8,10},{9,11},{10,... | collective-permute-start | bytes 417800 | tf_op jit(solution)/shard_map/ppermute | solution.py:49
  100.2 8.0 %collective-permute-done.41 = bf16[32,2176]{1,0:T(8,128)(2,1)S(1)} collective-permute-done((bf16[32,2176]{1,0:T(8,128)(2,1)S(1)}, bf16[32,2176]{1,0:T(8,128)(2,1)S(1)}, u32[]{:S(2)}, u32[]{:S(2)}) %collective-permute-start.41) | collective-permute-done | bytes 139296 | tf_op jit(solution)/shard_map/ppermute | solution.py:49
  108.3 1.6 %collective-permute-start.49 = (bf16[64,2176]{1,0:T(8,128)(2,1)S(1)}, bf16[64,2176]{1,0:T(8,128)(2,1)S(1)}, u32[]{:S(2)}, u32[]{:S(2)}) collective-permute-start(bf16[64,2176]{1,0:T(8,128)(2,1)S(1)} %constant_dynamic-update-slice_fusion.4.refs_3_), channel_id=1, source_target_pairs={{0,16},{1,17},{2,18},{3,19},{4,12},{5,13},{6,14},{7,15},{8,24},{9,... | collective-permute-start | bytes 835592 | tf_op jit(solution)/shard_map/ppermute | solution.py:73
  112.6 4.6 %collective-permute-done.49.refs_6_ = bf16[64,2176]{1,0:T(8,128)(2,1)S(1)} collective-permute-done((bf16[64,2176]{1,0:T(8,128)(2,1)S(1)}, bf16[64,2176]{1,0:T(8,128)(2,1)S(1)}, u32[]{:S(2)}, u32[]{:S(2)}) %collective-permute-start.49) | collective-permute-done | bytes 278560 | tf_op jit(solution)/shard_map/ppermute | solution.py:73
  117.2 2.3 %collective-permute-done.43.refs_8_ = bf16[64,2176]{1,0:T(8,128)(2,1)S(1)} collective-permute-done((bf16[64,2176]{1,0:T(8,128)(2,1)S(1)}, bf16[64,2176]{1,0:T(8,128)(2,1)S(1)}, u32[]{:S(2)}, u32[]{:S(2)}) %collective-permute-start.43) | collective-permute-done | bytes 278560 | tf_op jit(solution)/shard_map/ppermute | solution.py:73
  120.3 3.8 %collective-permute-done.38.refs_4_ = bf16[64,2176]{1,0:T(8,128)(2,1)S(1)} collective-permute-done((bf16[64,2176]{1,0:T(8,128)(2,1)S(1)}, bf16[64,2176]{1,0:T(8,128)(2,1)S(1)}, u32[]{:S(2)}, u32[]{:S(2)}) %collective-permute-start.38) | collective-permute-done | bytes 278560 | tf_op jit(solution)/shard_map/ppermute | solution.py:73
  126.2 3.9 %last.3 = (bf16[8,224,2048]{2,1,0:T(8,128)(2,1)}, bf16[8,224,2048]{2,1,0:T(8,128)(2,1)}, bf16[3,512,128]{2,1,0:T(8,128)(2,1)S(1)}) custom-call(s32[3,8]{1,0:T(4,128)S(1)} %get-tuple-element.40.where, bf16[8,224,2048]{2,1,0:T(8,128)(2,1)S(1)} %add.108.c_ref, f32[2,224,128]{2,1,0:T(8,128)S(1)} %get-tuple-element.67.refs_0_, ...), custom_call_target="tpu_custom_call" | custom-call | flops 3758096384 | bytes 7602176 | tf_op jit(solution)/shard_map/last/pallas_call | solution.py:349
  131.3 6.0 %last.4 = (bf16[8,224,2048]{2,1,0:T(8,128)(2,1)}, bf16[8,224,2048]{2,1,0:T(8,128)(2,1)}, bf16[3,512,128]{2,1,0:T(8,128)(2,1)S(1)}) custom-call(s32[3,8]{1,0:T(4,128)S(1)} %get-tuple-element.40.where, bf16[8,224,2048]{2,1,0:T(8,128)(2,1)S(1)} %add.108.c_ref, ...), custom_call_target="tpu_custom_call", output_to_operand_aliasing={{0}: (13, {}), {1}: (14, {})} | custom-call | flops 7516192768 | bytes 15204352 | tf_op jit(solution)/shard_map/last/pallas_call | solution.py:349
  137.3 4.0 %last.5 = (bf16[8,224,2048]{2,1,0:T(8,128)(2,1)}, bf16[8,224,2048]{2,1,0:T(8,128)(2,1)}, bf16[3,512,128]{2,1,0:T(8,128)(2,1)}) custom-call(s32[3,8]{1,0:T(4,128)S(1)} %get-tuple-element.40.where, bf16[8,224,2048]{2,1,0:T(8,128)(2,1)S(1)} %add.108.c_ref, f32[2,224,128]{2,1,0:T(8,128)S(1)} %get-tuple-element.48.refs_0_, ...), custom_call_target="tpu_custom_call", output_to_operand_aliasing={{0}: (8, {}), {1}: (9, {})} | custom-call | flops 3758096384 | bytes 7602176 | tf_op jit(solution)/shard_map/last/pallas_call | solution.py:349
  (115 shorter events, 34.9 us)
Async XLA Ops:
  6.6 12.3 %collective-permute-start.1 = (bf16[512,128]{1,0:T(8,128)(2,1)S(1)}, bf16[512,128]{1,0:T(8,128)(2,1)S(1)}, u32[]{:S(2)}, u32[]{:S(2)}) collective-permute-start(bf16[512,128]{1,0:T(8,128)(2,1)S(1)} %get-tuple-element.81), channel_id=1, source_target_pairs={{0,8},{1,9},{2,10},{3,11},{4,12},{5,13},{6,14},{7,15},{8,0},{9,1},... | collective-permute-start | bytes 393224 | tf_op jit(solution)/shard_map/ppermute | solution.py:41
  9.5 9.4 %collective-permute-start.2 = (bf16[512,128]{1,0:T(8,128)(2,1)S(1)}, bf16[512,128]{1,0:T(8,128)(2,1)S(1)}, u32[]{:S(2)}, u32[]{:S(2)}) collective-permute-start(bf16[512,128]{1,0:T(8,128)(2,1)S(1)} %get-tuple-element.83), channel_id=1, source_target_pairs={{0,16},{1,17},{2,18},{3,19},{4,20},{5,21},{6,22},{7,23},{8,24},{9,... | collective-permute-start | bytes 393224 | tf_op jit(solution)/shard_map/ppermute | solution.py:41
  11.0 7.9 %collective-permute-start.3 = (bf16[512,128]{1,0:T(8,128)(2,1)S(1)}, bf16[512,128]{1,0:T(8,128)(2,1)S(1)}, u32[]{:S(2)}, u32[]{:S(2)}) collective-permute-start(bf16[512,128]{1,0:T(8,128)(2,1)S(1)} %get-tuple-element.82), channel_id=1, source_target_pairs={{0,24},{1,25},{2,26},{3,27},{4,28},{5,29},{6,30},{7,31},{8,16},{9,... | collective-permute-start | bytes 393224 | tf_op jit(solution)/shard_map/ppermute | solution.py:41
  19.0 12.9 %collective-permute-start.8 = (bf16[512,128]{1,0:T(8,128)(2,1)S(1)}, bf16[512,128]{1,0:T(8,128)(2,1)S(1)}, u32[]{:S(2)}, u32[]{:S(2)}) collective-permute-start(bf16[512,128]{1,0:T(8,128)(2,1)S(1)} %fusion.6), channel_id=1, source_target_pairs={{0,2},{1,3},{2,0},{3,1},{4,6},{5,7},{6,4},{7,5},{8,10},{9,11},{10,... | collective-permute-start | bytes 393224 | tf_op jit(solution)/shard_map/ppermute | solution.py:49
  22.1 9.8 %collective-permute-start.9 = (bf16[512,128]{1,0:T(8,128)(2,1)S(1)}, bf16[512,128]{1,0:T(8,128)(2,1)S(1)}, u32[]{:S(2)}, u32[]{:S(2)}) collective-permute-start(bf16[512,128]{1,0:T(8,128)(2,1)S(1)} %fusion.6), channel_id=1, source_target_pairs={{0,3},{1,2},{2,1},{3,0},{4,7},{5,6},{6,5},{7,4},{8,11},{9,10},{10,... | collective-permute-start | bytes 393224 | tf_op jit(solution)/shard_map/ppermute | solution.py:49
  23.4 10.0 %collective-permute-start.4 = (bf16[512,128]{1,0:T(8,128)(2,1)S(1)}, bf16[512,128]{1,0:T(8,128)(2,1)S(1)}, u32[]{:S(2)}, u32[]{:S(2)}) collective-permute-start(bf16[512,128]{1,0:T(8,128)(2,1)S(1)} %fusion.6), channel_id=1, source_target_pairs={{0,1},{1,0},{2,3},{3,2},{4,5},{5,4},{6,7},{7,6},{8,9},{9,8},{10,11... | collective-permute-start | bytes 393224 | tf_op jit(solution)/shard_map/ppermute | solution.py:49
  33.5 11.6 %collective-permute-start.5 = (bf16[1024,128]{1,0:T(8,128)(2,1)S(1)}, bf16[1024,128]{1,0:T(8,128)(2,1)S(1)}, u32[]{:S(2)}, u32[]{:S(2)}) collective-permute-start(bf16[1024,128]{1,0:T(8,128)(2,1)S(1)} %constant_dynamic-update-slice_fusion.refs_0_), channel_id=1, source_target_pairs={{0,8},{1,9},{2,10},{3,11},{4,20},{5,21},{6,22},{7,23},{8,0},{9,1},... | collective-permute-start | bytes 786440 | tf_op jit(solution)/shard_map/ppermute | solution.py:73
  34.1 13.1 %collective-permute-start.14 = (bf16[1024,128]{1,0:T(8,128)(2,1)S(1)}, bf16[1024,128]{1,0:T(8,128)(2,1)S(1)}, u32[]{:S(2)}, u32[]{:S(2)}) collective-permute-start(bf16[1024,128]{1,0:T(8,128)(2,1)S(1)} %constant_dynamic-update-slice_fusion.2.refs_2_), channel_id=1, source_target_pairs={{0,4},{1,5},{2,6},{3,7},{4,0},{5,1},{6,2},{7,3},{8,12},{9,13},{10,... | collective-permute-start | bytes 786440 | tf_op jit(solution)/shard_map/ppermute | solution.py:41
  39.5 9.2 %collective-permute-start.11 = (bf16[1024,128]{1,0:T(8,128)(2,1)S(1)}, bf16[1024,128]{1,0:T(8,128)(2,1)S(1)}, u32[]{:S(2)}, u32[]{:S(2)}) collective-permute-start(bf16[1024,128]{1,0:T(8,128)(2,1)S(1)} %collective-permute-done.10.refs_2_), channel_id=1, source_target_pairs={{0,16},{1,17},{2,18},{3,19},{4,12},{5,13},{6,14},{7,15},{8,24},{9,... | collective-permute-start | bytes 786440 | tf_op jit(solution)/shard_map/ppermute | solution.py:73
  46.6 7.7 %collective-permute-start.18 = (bf16[1024,128]{1,0:T(8,128)(2,1)S(1)}, bf16[1024,128]{1,0:T(8,128)(2,1)S(1)}, u32[]{:S(2)}, u32[]{:S(2)}) collective-permute-start(bf16[1024,128]{1,0:T(8,128)(2,1)S(1)} %constant_dynamic-update-slice_fusion.2.refs_2_), channel_id=1, source_target_pairs={{0,16},{1,17},{2,18},{3,19},{4,12},{5,13},{6,14},{7,15},{8,24},{9,... | collective-permute-start | bytes 786440 | tf_op jit(solution)/shard_map/ppermute | solution.py:73
  47.1 10.0 %collective-permute-start.16 = (bf16[1024,128]{1,0:T(8,128)(2,1)S(1)}, bf16[1024,128]{1,0:T(8,128)(2,1)S(1)}, u32[]{:S(2)}, u32[]{:S(2)}) collective-permute-start(bf16[1024,128]{1,0:T(8,128)(2,1)S(1)} %constant_dynamic-update-slice_fusion.refs_0_), channel_id=1, source_target_pairs={{0,16},{1,17},{2,18},{3,19},{4,12},{5,13},{6,14},{7,15},{8,24},{9,... | collective-permute-start | bytes 786440 | tf_op jit(solution)/shard_map/ppermute | solution.py:73
  48.7 8.4 %collective-permute-start.12 = (bf16[1024,128]{1,0:T(8,128)(2,1)S(1)}, bf16[1024,128]{1,0:T(8,128)(2,1)S(1)}, u32[]{:S(2)}, u32[]{:S(2)}) collective-permute-start(bf16[1024,128]{1,0:T(8,128)(2,1)S(1)} %collective-permute-done.11.refs_2_), channel_id=1, source_target_pairs={{0,4},{1,5},{2,6},{3,7},{4,0},{5,1},{6,2},{7,3},{8,12},{9,13},{10,... | collective-permute-start | bytes 786440 | tf_op jit(solution)/shard_map/ppermute | solution.py:41
  53.7 24.2 %collective-permute-start.15 = (bf16[128,2176]{1,0:T(8,128)(2,1)S(1)}, bf16[128,2176]{1,0:T(8,128)(2,1)S(1)}, u32[]{:S(2)}, u32[]{:S(2)}) collective-permute-start(bf16[128,2176]{1,0:T(8,128)(2,1)S(1)} %get-tuple-element.50), channel_id=1, source_target_pairs={{0,4},{1,5},{2,6},{3,7},{4,0},{5,1},{6,2},{7,3},{8,12},{9,13},{10,... | collective-permute-start | bytes 1671176 | tf_op jit(solution)/shard_map/ppermute | solution.py:41
  67.2 9.0 %collective-permute-start.32 = (bf16[64,2176]{1,0:T(8,128)(2,1)S(1)}, bf16[64,2176]{1,0:T(8,128)(2,1)S(1)}, u32[]{:S(2)}, u32[]{:S(2)}) collective-permute-start(bf16[64,2176]{1,0:T(8,128)(2,1)S(1)} %get-tuple-element.78), channel_id=1, source_target_pairs={{0,16},{1,17},{2,18},{3,19},{4,12},{5,13},{6,14},{7,15},{8,24},{9,... | collective-permute-start | bytes 835592 | tf_op jit(solution)/shard_map/ppermute | solution.py:73
  67.8 14.3 %collective-permute-start.21 = (bf16[64,2176]{1,0:T(8,128)(2,1)S(1)}, bf16[64,2176]{1,0:T(8,128)(2,1)S(1)}, u32[]{:S(2)}, u32[]{:S(2)}) collective-permute-start(bf16[64,2176]{1,0:T(8,128)(2,1)S(1)} %get-tuple-element.79), channel_id=1, source_target_pairs={{0,16},{1,17},{2,18},{3,19},{4,12},{5,13},{6,14},{7,15},{8,24},{9,... | collective-permute-start | bytes 835592 | tf_op jit(solution)/shard_map/ppermute | solution.py:73
  69.4 18.0 %collective-permute-start.31 = (bf16[64,2176]{1,0:T(8,128)(2,1)S(1)}, bf16[64,2176]{1,0:T(8,128)(2,1)S(1)}, u32[]{:S(2)}, u32[]{:S(2)}) collective-permute-start(bf16[64,2176]{1,0:T(8,128)(2,1)S(1)} %get-tuple-element.80), channel_id=1, source_target_pairs={{0,16},{1,17},{2,18},{3,19},{4,12},{5,13},{6,14},{7,15},{8,24},{9,... | collective-permute-start | bytes 835592 | tf_op jit(solution)/shard_map/ppermute | solution.py:73
  72.3 9.8 %collective-permute-start.27 = (bf16[64,2176]{1,0:T(8,128)(2,1)S(1)}, bf16[64,2176]{1,0:T(8,128)(2,1)S(1)}, u32[]{:S(2)}, u32[]{:S(2)}) collective-permute-start(bf16[64,2176]{1,0:T(8,128)(2,1)S(1)} %sum.1), channel_id=1, source_target_pairs={{0,8},{1,9},{2,10},{3,11},{4,20},{5,21},{6,22},{7,23},{8,0},{9,1},... | collective-permute-start | bytes 835592 | tf_op jit(solution)/shard_map/ppermute | solution.py:73
  76.3 11.1 %collective-permute-start.33 = (bf16[64,2176]{1,0:T(8,128)(2,1)S(1)}, bf16[64,2176]{1,0:T(8,128)(2,1)S(1)}, u32[]{:S(2)}, u32[]{:S(2)}) collective-permute-start(bf16[64,2176]{1,0:T(8,128)(2,1)S(1)} %add_convert_fusion), channel_id=1, source_target_pairs={{0,8},{1,9},{2,10},{3,11},{4,20},{5,21},{6,22},{7,23},{8,0},{9,1},... | collective-permute-start | bytes 835592 | tf_op jit(solution)/shard_map/ppermute | solution.py:73
  83.0 9.6 %collective-permute-start.29 = (bf16[16,2176]{1,0:T(8,128)(2,1)S(1)}, bf16[16,2176]{1,0:T(8,128)(2,1)S(1)}, u32[]{:S(2)}, u32[]{:S(2)}) collective-permute-start(bf16[16,2176]{1,0:T(8,128)(2,1)S(1)} %get-tuple-element.59), channel_id=1, source_target_pairs={{0,2},{1,3},{2,0},{3,1},{4,6},{5,7},{6,4},{7,5},{8,10},{9,11},{10,... | collective-permute-start | bytes 208904 | tf_op jit(solution)/shard_map/ppermute | solution.py:49
  84.4 8.2 %collective-permute-start.30 = (bf16[16,2176]{1,0:T(8,128)(2,1)S(1)}, bf16[16,2176]{1,0:T(8,128)(2,1)S(1)}, u32[]{:S(2)}, u32[]{:S(2)}) collective-permute-start(bf16[16,2176]{1,0:T(8,128)(2,1)S(1)} %get-tuple-element.60), channel_id=1, source_target_pairs={{0,3},{1,2},{2,1},{3,0},{4,7},{5,6},{6,5},{7,4},{8,11},{9,10},{10,... | collective-permute-start | bytes 208904 | tf_op jit(solution)/shard_map/ppermute | solution.py:49
  88.3 8.1 %collective-permute-start.35 = (bf16[16,2176]{1,0:T(8,128)(2,1)S(1)}, bf16[16,2176]{1,0:T(8,128)(2,1)S(1)}, u32[]{:S(2)}, u32[]{:S(2)}) collective-permute-start(bf16[16,2176]{1,0:T(8,128)(2,1)S(1)} %get-tuple-element.63), channel_id=1, source_target_pairs={{0,2},{1,3},{2,0},{3,1},{4,6},{5,7},{6,4},{7,5},{8,10},{9,11},{10,... | collective-permute-start | bytes 208904 | tf_op jit(solution)/shard_map/ppermute | solution.py:49
  96.5 11.7 %collective-permute-start.41 = (bf16[32,2176]{1,0:T(8,128)(2,1)S(1)}, bf16[32,2176]{1,0:T(8,128)(2,1)S(1)}, u32[]{:S(2)}, u32[]{:S(2)}) collective-permute-start(bf16[32,2176]{1,0:T(8,128)(2,1)S(1)} %pad_maximum_fusion.1), channel_id=1, source_target_pairs={{0,2},{1,3},{2,0},{3,1},{4,6},{5,7},{6,4},{7,5},{8,10},{9,11},{10,... | collective-permute-start | bytes 417800 | tf_op jit(solution)/shard_map/ppermute | solution.py:49
  98.7 9.5 %collective-permute-start.42 = (bf16[32,2176]{1,0:T(8,128)(2,1)S(1)}, bf16[32,2176]{1,0:T(8,128)(2,1)S(1)}, u32[]{:S(2)}, u32[]{:S(2)}) collective-permute-start(bf16[32,2176]{1,0:T(8,128)(2,1)S(1)} %pad_maximum_fusion.1), channel_id=1, source_target_pairs={{0,3},{1,2},{2,1},{3,0},{4,7},{5,6},{6,5},{7,4},{8,11},{9,10},{10,... | collective-permute-start | bytes 417800 | tf_op jit(solution)/shard_map/ppermute | solution.py:49
  100.2 11.2 %collective-permute-start.37 = (bf16[32,2176]{1,0:T(8,128)(2,1)S(1)}, bf16[32,2176]{1,0:T(8,128)(2,1)S(1)}, u32[]{:S(2)}, u32[]{:S(2)}) collective-permute-start(bf16[32,2176]{1,0:T(8,128)(2,1)S(1)} %pad_maximum_fusion.1), channel_id=1, source_target_pairs={{0,1},{1,0},{2,3},{3,2},{4,5},{5,4},{6,7},{7,6},{8,9},{9,8},{10,11... | collective-permute-start | bytes 417800 | tf_op jit(solution)/shard_map/ppermute | solution.py:49
  108.3 8.9 %collective-permute-start.49 = (bf16[64,2176]{1,0:T(8,128)(2,1)S(1)}, bf16[64,2176]{1,0:T(8,128)(2,1)S(1)}, u32[]{:S(2)}, u32[]{:S(2)}) collective-permute-start(bf16[64,2176]{1,0:T(8,128)(2,1)S(1)} %constant_dynamic-update-slice_fusion.4.refs_3_), channel_id=1, source_target_pairs={{0,16},{1,17},{2,18},{3,19},{4,12},{5,13},{6,14},{7,15},{8,24},{9,... | collective-permute-start | bytes 835592 | tf_op jit(solution)/shard_map/ppermute | solution.py:73
  109.9 9.5 %collective-permute-start.43 = (bf16[64,2176]{1,0:T(8,128)(2,1)S(1)}, bf16[64,2176]{1,0:T(8,128)(2,1)S(1)}, u32[]{:S(2)}, u32[]{:S(2)}) collective-permute-start(bf16[64,2176]{1,0:T(8,128)(2,1)S(1)} %constant_dynamic-update-slice_fusion.4.refs_3_), channel_id=1, source_target_pairs={{0,8},{1,9},{2,10},{3,11},{4,20},{5,21},{6,22},{7,23},{8,0},{9,1},... | collective-permute-start | bytes 835592 | tf_op jit(solution)/shard_map/ppermute | solution.py:73
  111.5 8.0 %collective-permute-start.52 = (bf16[64,2176]{1,0:T(8,128)(2,1)S(1)}, bf16[64,2176]{1,0:T(8,128)(2,1)S(1)}, u32[]{:S(2)}, u32[]{:S(2)}) collective-permute-start(bf16[64,2176]{1,0:T(8,128)(2,1)S(1)} %pad_maximum_fusion.refs_1_), channel_id=1, source_target_pairs={{0,4},{1,5},{2,6},{3,7},{4,0},{5,1},{6,2},{7,3},{8,12},{9,13},{10,... | collective-permute-start | bytes 835592 | tf_op jit(solution)/shard_map/ppermute | solution.py:41
  111.5 12.5 %collective-permute-start.38 = (bf16[64,2176]{1,0:T(8,128)(2,1)S(1)}, bf16[64,2176]{1,0:T(8,128)(2,1)S(1)}, u32[]{:S(2)}, u32[]{:S(2)}) collective-permute-start(bf16[64,2176]{1,0:T(8,128)(2,1)S(1)} %pad_maximum_fusion.refs_1_), channel_id=1, source_target_pairs={{0,8},{1,9},{2,10},{3,11},{4,20},{5,21},{6,22},{7,23},{8,0},{9,1},... | collective-permute-start | bytes 835592 | tf_op jit(solution)/shard_map/ppermute | solution.py:73
  112.1 12.6 %collective-permute-start.46 = (bf16[64,2176]{1,0:T(8,128)(2,1)S(1)}, bf16[64,2176]{1,0:T(8,128)(2,1)S(1)}, u32[]{:S(2)}, u32[]{:S(2)}) collective-permute-start(bf16[64,2176]{1,0:T(8,128)(2,1)S(1)} %pad_maximum_fusion.refs_1_), channel_id=1, source_target_pairs={{0,16},{1,17},{2,18},{3,19},{4,12},{5,13},{6,14},{7,15},{8,24},{9,... | collective-permute-start | bytes 835592 | tf_op jit(solution)/shard_map/ppermute | solution.py:73
  117.2 9.1 %collective-permute-start.50 = (bf16[64,2176]{1,0:T(8,128)(2,1)S(1)}, bf16[64,2176]{1,0:T(8,128)(2,1)S(1)}, u32[]{:S(2)}, u32[]{:S(2)}) collective-permute-start(bf16[64,2176]{1,0:T(8,128)(2,1)S(1)} %collective-permute-done.49.refs_6_), channel_id=1, source_target_pairs={{0,4},{1,5},{2,6},{3,7},{4,0},{5,1},{6,2},{7,3},{8,12},{9,13},{10,... | collective-permute-start | bytes 835592 | tf_op jit(solution)/shard_map/ppermute | solution.py:41
  119.4 11.8 %collective-permute-start.51 = (bf16[64,2176]{1,0:T(8,128)(2,1)S(1)}, bf16[64,2176]{1,0:T(8,128)(2,1)S(1)}, u32[]{:S(2)}, u32[]{:S(2)}) collective-permute-start(bf16[64,2176]{1,0:T(8,128)(2,1)S(1)} %collective-permute-done.43.refs_8_), channel_id=1, source_target_pairs={{0,4},{1,5},{2,6},{3,7},{4,0},{5,1},{6,2},{7,3},{8,12},{9,13},{10,... | collective-permute-start | bytes 835592 | tf_op jit(solution)/shard_map/ppermute | solution.py:41
  119.4 10.7 %collective-permute-start.44 = (bf16[64,2176]{1,0:T(8,128)(2,1)S(1)}, bf16[64,2176]{1,0:T(8,128)(2,1)S(1)}, u32[]{:S(2)}, u32[]{:S(2)}) collective-permute-start(bf16[64,2176]{1,0:T(8,128)(2,1)S(1)} %collective-permute-done.43.refs_8_), channel_id=1, source_target_pairs={{0,16},{1,17},{2,18},{3,19},{4,12},{5,13},{6,14},{7,15},{8,24},{9,... | collective-permute-start | bytes 835592 | tf_op jit(solution)/shard_map/ppermute | solution.py:73
  (27 other events, 130.6 us)

commit v4 on v3

--- a/solution.py
+++ b/solution.py
@@ -414,8 +414,15 @@
 
     lefts, rights = {}, {}
     for i, name in enumerate(names):
-        pieces = [side[half][name] for half in (0, 1) for side in (qs, qs_far)]
-        lefts[name], outs = first_call(where, 2 * i, combined, pieces, shard_count)
+        own_side, far_side = ([side[0][name], side[1][name]] for side in (qs, qs_far))
+        if name == names[-1]:
+            far_left, far = first_call(where, 2 * i + 1, combined, far_side, shard_count)
+            left, kept = first_call(where, 2 * i, combined, own_side, shard_count)
+            lefts[name] = jnp.concatenate([left, far_left], axis=0)
+            outs = [kept[0], far[0]]
+        else:
+            pieces = [x for pair in zip(own_side, far_side) for x in pair]
+            lefts[name], outs = first_call(where, 2 * i, combined, pieces, shard_count)
         rights[name] = [outs[0], links.swap_group(outs[1], near)]
 
     own = rights.pop(0)

time: 141 us -> 144 us (1.021)
  starting transfers between devices: 46.9 us -> 51.9 us
  waiting for transfers between devices: 56.6 us -> 53.7 us
    ppermute x18, waiting for transfers between devices: 35.3 us -> 30 us  [cross(): return lax.ppermute(x, AXES, pairs)]
    ppermute x12, starting transfers between devices: 17.4 us -> 19.9 us  [swap_shard(): return lax.ppermute(x, AXES, pairs)]
    ppermute x12, waiting for transfers between devices: 19.8 us -> 22.1 us  [swap_shard(): return lax.ppermute(x, AXES, pairs)]
    ppermute x18, starting transfers between devices: 21.1 us -> 23.2 us  [cross(): return lax.ppermute(x, AXES, pairs)]
    pallas_call x4 -> x5, Pallas kernels: 8.77 us -> 9.12 us  [first_call(): pl.pallas_call(functools.partial(first_body, count, shard_count), grid_sp...]
  transfers between devices with their start and end apart: 54 -> 54, of which waited for: 15 -> 16; matrix products, arithmetic and copies ran while one was open for 0% -> 0% of each run, Pallas kernels for 16% -> 16%
where the time goes in v4:
time: 144 us
  waiting for transfers between devices  53.7 us (37%)
  starting transfers between devices  51.9 us (36%)
  Pallas kernels  27.9 us (19%)
  local copies, waits for them, and re-layouts  8.59 us (6%)
    ppermute x18, waiting for transfers between devices, cross(): return lax.ppermute(x, AXES, pairs)  30 us
    ppermute x18, starting transfers between devices, cross(): return lax.ppermute(x, AXES, pairs)  23.2 us
    ppermute x12, waiting for transfers between devices, swap_shard(): return lax.ppermute(x, AXES, pairs)  22.1 us
    ppermute x12, starting transfers between devices, swap_shard(): return lax.ppermute(x, AXES, pairs)  19.9 us
    pallas_call x3, Pallas kernels, last_call(): pl.pallas_call(functools.partial(last_body, count, multiplier, cap, base,...  13.9 us
    pallas_call x5, Pallas kernels, first_call(): pl.pallas_call(functools.partial(first_body, count, shard_count), grid_sp...  9.12 us
    ppermute x24, starting transfers between devices, swap_group(): return lax.ppermute(x, AXES, pairs)  8.91 us
    unnamed x13, local copies, waits for them, and re-layouts  8.49 us
  transfers between devices with their start and end apart: 54, of which 16 were waited for; matrix products, arithmetic and copies ran while one was open for 0% of the time, Pallas kernels for 16%

profile of v4, /device:TPU:0, one launch (start us, length us, event | category | flops | bytes accessed | tf_op | source)
XLA Modules:
  0.0 143.6 jit_solution(13431174405188200202)
XLA Ops:
  6.6 2.9 %collective-permute-start.1 = (bf16[512,128]{1,0:T(8,128)(2,1)S(1)}, bf16[512,128]{1,0:T(8,128)(2,1)S(1)}, u32[]{:S(2)}, u32[]{:S(2)}) collective-permute-start(bf16[512,128]{1,0:T(8,128)(2,1)S(1)} %get-tuple-element.83), channel_id=1, source_target_pairs={{0,8},{1,9},{2,10},{3,11},{4,12},{5,13},{6,14},{7,15},{8,0},{9,1},... | collective-permute-start | bytes 393224 | tf_op jit(solution)/shard_map/ppermute | solution.py:41
  11.0 3.1 %copy-done.3 = bf16[8,224,2048]{2,1,0:T(8,128)(2,1)S(1)} copy-done((bf16[8,224,2048]{2,1,0:T(8,128)(2,1)S(1)}, bf16[8,224,2048]{2,1,0:T(8,128)(2,1)}, u32[]{:S(2)}) %copy-start.3) | copy-done | bytes 7340056
  14.1 3.1 %copy-done.4 = bf16[8,224,2048]{2,1,0:T(8,128)(2,1)S(1)} copy-done((bf16[8,224,2048]{2,1,0:T(8,128)(2,1)S(1)}, bf16[8,224,2048]{2,1,0:T(8,128)(2,1)}, u32[]{:S(2)}) %copy-start.4) | copy-done | bytes 7340056
  17.2 1.7 %add.108.c_ref = bf16[8,224,2048]{2,1,0:T(8,128)(2,1)S(1)} custom-call(bf16[8,224,2048]{2,1,0:T(8,128)(2,1)S(1)} %copy-done.3, bf16[8,224,2048]{2,1,0:T(8,128)(2,1)S(1)} %copy-done.4), custom_call_target="tpu_custom_call" | custom-call | flops 7516192768 | bytes 22020096 | tf_op jit(solution)/shard_map/add/pallas_call | solution.py:155
  19.0 3.1 %collective-permute-start.7 = (bf16[512,128]{1,0:T(8,128)(2,1)S(1)}, bf16[512,128]{1,0:T(8,128)(2,1)S(1)}, u32[]{:S(2)}, u32[]{:S(2)}) collective-permute-start(bf16[512,128]{1,0:T(8,128)(2,1)S(1)} %fusion.6), channel_id=1, source_target_pairs={{0,2},{1,3},{2,0},{3,1},{4,6},{5,7},{6,4},{7,5},{8,10},{9,11},{10,... | collective-permute-start | bytes 393224 | tf_op jit(solution)/shard_map/ppermute | solution.py:49
  23.7 8.1 %collective-permute-done.7 = bf16[512,128]{1,0:T(8,128)(2,1)S(1)} collective-permute-done((bf16[512,128]{1,0:T(8,128)(2,1)S(1)}, bf16[512,128]{1,0:T(8,128)(2,1)S(1)}, u32[]{:S(2)}, u32[]{:S(2)}) %collective-permute-start.7) | collective-permute-done | bytes 131104 | tf_op jit(solution)/shard_map/ppermute | solution.py:49
  36.1 2.9 %collective-permute-done.9.refs_2_ = bf16[1024,128]{1,0:T(8,128)(2,1)S(1)} collective-permute-done((bf16[1024,128]{1,0:T(8,128)(2,1)S(1)}, bf16[1024,128]{1,0:T(8,128)(2,1)S(1)}, u32[]{:S(2)}, u32[]{:S(2)}) %collective-permute-start.9) | collective-permute-done | bytes 262176 | tf_op jit(solution)/shard_map/ppermute | solution.py:73
  39.0 2.8 %collective-permute-start.10 = (bf16[1024,128]{1,0:T(8,128)(2,1)S(1)}, bf16[1024,128]{1,0:T(8,128)(2,1)S(1)}, u32[]{:S(2)}, u32[]{:S(2)}) collective-permute-start(bf16[1024,128]{1,0:T(8,128)(2,1)S(1)} %collective-permute-done.9.refs_2_), channel_id=1, source_target_pairs={{0,16},{1,17},{2,18},{3,19},{4,12},{5,13},{6,14},{7,15},{8,24},{9,... | collective-permute-start | bytes 786440 | tf_op jit(solution)/shard_map/ppermute | solution.py:73
  41.8 2.8 %collective-permute-done.5.refs_0_ = bf16[1024,128]{1,0:T(8,128)(2,1)S(1)} collective-permute-done((bf16[1024,128]{1,0:T(8,128)(2,1)S(1)}, bf16[1024,128]{1,0:T(8,128)(2,1)S(1)}, u32[]{:S(2)}, u32[]{:S(2)}) %collective-permute-start.5) | collective-permute-done | bytes 262176 | tf_op jit(solution)/shard_map/ppermute | solution.py:73
  44.6 2.8 %collective-permute-start.6 = (bf16[1024,128]{1,0:T(8,128)(2,1)S(1)}, bf16[1024,128]{1,0:T(8,128)(2,1)S(1)}, u32[]{:S(2)}, u32[]{:S(2)}) collective-permute-start(bf16[1024,128]{1,0:T(8,128)(2,1)S(1)} %collective-permute-done.5.refs_0_), channel_id=1, source_target_pairs={{0,16},{1,17},{2,18},{3,19},{4,12},{5,13},{6,14},{7,15},{8,24},{9,... | collective-permute-start | bytes 786440 | tf_op jit(solution)/shard_map/ppermute | solution.py:73
  48.1 3.7 %collective-permute-done.6.refs_0_ = bf16[1024,128]{1,0:T(8,128)(2,1)S(1)} collective-permute-done((bf16[1024,128]{1,0:T(8,128)(2,1)S(1)}, bf16[1024,128]{1,0:T(8,128)(2,1)S(1)}, u32[]{:S(2)}, u32[]{:S(2)}) %collective-permute-start.6) | collective-permute-done | bytes 262176 | tf_op jit(solution)/shard_map/ppermute | solution.py:73
  51.8 2.2 %first.7 = (f32[2,224,128]{2,1,0:T(8,128)S(1)}, bf16[128,2176]{1,0:T(8,128)(2,1)S(1)}, bf16[128,2176]{1,0:T(8,128)(2,1)S(1)}) custom-call(s32[3,8]{1,0:T(4,128)S(1)} %get-tuple-element.41.where, bf16[8,224,2048]{2,1,0:T(8,128)(2,1)S(1)} %add.108.c_ref, bf16[1024,128]{1,0:T(8,128)(2,1)S(1)} %constant_dynamic-update-slice_fusion.refs_0_, ...), custom_call_target="tpu_custom_call" | custom-call | flops 3758096384 | bytes 3932160 | tf_op jit(solution)/shard_map/first/pallas_call | solution.py:262
  57.0 2.2 %first.9 = (f32[2,224,128]{2,1,0:T(8,128)S(1)}, bf16[128,2176]{1,0:T(8,128)(2,1)S(1)}, bf16[128,2176]{1,0:T(8,128)(2,1)S(1)}) custom-call(s32[3,8]{1,0:T(4,128)S(1)} %get-tuple-element.41.where, bf16[8,224,2048]{2,1,0:T(8,128)(2,1)S(1)} %add.108.c_ref, bf16[1024,128]{1,0:T(8,128)(2,1)S(1)} %collective-permute-done.5.refs_0_, ...), custom_call_target="tpu_custom_call" | custom-call | flops 3758096384 | bytes 3932160 | tf_op jit(solution)/shard_map/first/pallas_call | solution.py:262
  59.4 2.2 %first.8 = (f32[2,224,128]{2,1,0:T(8,128)S(1)}, bf16[128,2176]{1,0:T(8,128)(2,1)S(1)}, bf16[128,2176]{1,0:T(8,128)(2,1)S(1)}) custom-call(s32[3,8]{1,0:T(4,128)S(1)} %get-tuple-element.41.where, bf16[8,224,2048]{2,1,0:T(8,128)(2,1)S(1)} %add.108.c_ref, bf16[1024,128]{1,0:T(8,128)(2,1)S(1)} %collective-permute-done.16.refs_0_, ...), custom_call_target="tpu_custom_call" | custom-call | flops 3758096384 | bytes 3932160 | tf_op jit(solution)/shard_map/first/pallas_call | solution.py:262
  63.5 2.1 %collective-permute-start.26 = (bf16[64,2176]{1,0:T(8,128)(2,1)S(1)}, bf16[64,2176]{1,0:T(8,128)(2,1)S(1)}, u32[]{:S(2)}, u32[]{:S(2)}) collective-permute-start(bf16[64,2176]{1,0:T(8,128)(2,1)S(1)} %get-tuple-element.79), channel_id=1, source_target_pairs={{0,16},{1,17},{2,18},{3,19},{4,12},{5,13},{6,14},{7,15},{8,24},{9,... | collective-permute-start | bytes 835592 | tf_op jit(solution)/shard_map/ppermute | solution.py:73
  65.8 2.0 %collective-permute-start.21 = (bf16[64,2176]{1,0:T(8,128)(2,1)S(1)}, bf16[64,2176]{1,0:T(8,128)(2,1)S(1)}, u32[]{:S(2)}, u32[]{:S(2)}) collective-permute-start(bf16[64,2176]{1,0:T(8,128)(2,1)S(1)} %get-tuple-element.81), channel_id=1, source_target_pairs={{0,16},{1,17},{2,18},{3,19},{4,12},{5,13},{6,14},{7,15},{8,24},{9,... | collective-permute-start | bytes 835592 | tf_op jit(solution)/shard_map/ppermute | solution.py:73
  68.0 2.2 %collective-permute-done.26.refs_2_ = bf16[64,2176]{1,0:T(8,128)(2,1)S(1)} collective-permute-done((bf16[64,2176]{1,0:T(8,128)(2,1)S(1)}, bf16[64,2176]{1,0:T(8,128)(2,1)S(1)}, u32[]{:S(2)}, u32[]{:S(2)}) %collective-permute-start.26) | collective-permute-done | bytes 278560 | tf_op jit(solution)/shard_map/ppermute | solution.py:73
  71.8 2.1 %collective-permute-done.32 = bf16[64,2176]{1,0:T(8,128)(2,1)S(1)} collective-permute-done((bf16[64,2176]{1,0:T(8,128)(2,1)S(1)}, bf16[64,2176]{1,0:T(8,128)(2,1)S(1)}, u32[]{:S(2)}, u32[]{:S(2)}) %collective-permute-start.32) | collective-permute-done | bytes 278560 | tf_op jit(solution)/shard_map/ppermute | solution.py:73
  75.5 4.3 %collective-permute-done.21.refs_2_ = bf16[64,2176]{1,0:T(8,128)(2,1)S(1)} collective-permute-done((bf16[64,2176]{1,0:T(8,128)(2,1)S(1)}, bf16[64,2176]{1,0:T(8,128)(2,1)S(1)}, u32[]{:S(2)}, u32[]{:S(2)}) %collective-permute-start.21) | collective-permute-done | bytes 278560 | tf_op jit(solution)/shard_map/ppermute | solution.py:73
  80.7 3.4 %collective-permute-start.28 = (bf16[16,2176]{1,0:T(8,128)(2,1)S(1)}, bf16[16,2176]{1,0:T(8,128)(2,1)S(1)}, u32[]{:S(2)}, u32[]{:S(2)}) collective-permute-start(bf16[16,2176]{1,0:T(8,128)(2,1)S(1)} %get-tuple-element.60), channel_id=1, source_target_pairs={{0,1},{1,0},{2,3},{3,2},{4,5},{5,4},{6,7},{7,6},{8,9},{9,8},{10,11... | collective-permute-start | bytes 208904 | tf_op jit(solution)/shard_map/ppermute | solution.py:49
  84.0 1.9 %collective-permute-start.29 = (bf16[16,2176]{1,0:T(8,128)(2,1)S(1)}, bf16[16,2176]{1,0:T(8,128)(2,1)S(1)}, u32[]{:S(2)}, u32[]{:S(2)}) collective-permute-start(bf16[16,2176]{1,0:T(8,128)(2,1)S(1)} %get-tuple-element.61), channel_id=1, source_target_pairs={{0,2},{1,3},{2,0},{3,1},{4,6},{5,7},{6,4},{7,5},{8,10},{9,11},{10,... | collective-permute-start | bytes 208904 | tf_op jit(solution)/shard_map/ppermute | solution.py:49
  89.0 2.2 %collective-permute-start.35 = (bf16[16,2176]{1,0:T(8,128)(2,1)S(1)}, bf16[16,2176]{1,0:T(8,128)(2,1)S(1)}, u32[]{:S(2)}, u32[]{:S(2)}) collective-permute-start(bf16[16,2176]{1,0:T(8,128)(2,1)S(1)} %get-tuple-element.65), channel_id=1, source_target_pairs={{0,2},{1,3},{2,0},{3,1},{4,6},{5,7},{6,4},{7,5},{8,10},{9,11},{10,... | collective-permute-start | bytes 208904 | tf_op jit(solution)/shard_map/ppermute | solution.py:49
  93.4 4.0 %collective-permute-done.35 = bf16[16,2176]{1,0:T(8,128)(2,1)S(1)} collective-permute-done((bf16[16,2176]{1,0:T(8,128)(2,1)S(1)}, bf16[16,2176]{1,0:T(8,128)(2,1)S(1)}, u32[]{:S(2)}, u32[]{:S(2)}) %collective-permute-start.35) | collective-permute-done | bytes 69664 | tf_op jit(solution)/shard_map/ppermute | solution.py:49
  97.4 2.3 %collective-permute-start.41 = (bf16[32,2176]{1,0:T(8,128)(2,1)S(1)}, bf16[32,2176]{1,0:T(8,128)(2,1)S(1)}, u32[]{:S(2)}, u32[]{:S(2)}) collective-permute-start(bf16[32,2176]{1,0:T(8,128)(2,1)S(1)} %pad_maximum_fusion.2), channel_id=1, source_target_pairs={{0,2},{1,3},{2,0},{3,1},{4,6},{5,7},{6,4},{7,5},{8,10},{9,11},{10,... | collective-permute-start | bytes 417800 | tf_op jit(solution)/shard_map/ppermute | solution.py:49
  99.8 1.6 %collective-permute-start.42 = (bf16[32,2176]{1,0:T(8,128)(2,1)S(1)}, bf16[32,2176]{1,0:T(8,128)(2,1)S(1)}, u32[]{:S(2)}, u32[]{:S(2)}) collective-permute-start(bf16[32,2176]{1,0:T(8,128)(2,1)S(1)} %pad_maximum_fusion.2), channel_id=1, source_target_pairs={{0,3},{1,2},{2,1},{3,0},{4,7},{5,6},{6,5},{7,4},{8,11},{9,10},{10,... | collective-permute-start | bytes 417800 | tf_op jit(solution)/shard_map/ppermute | solution.py:49
  101.4 9.2 %collective-permute-done.41 = bf16[32,2176]{1,0:T(8,128)(2,1)S(1)} collective-permute-done((bf16[32,2176]{1,0:T(8,128)(2,1)S(1)}, bf16[32,2176]{1,0:T(8,128)(2,1)S(1)}, u32[]{:S(2)}, u32[]{:S(2)}) %collective-permute-start.41) | collective-permute-done | bytes 139296 | tf_op jit(solution)/shard_map/ppermute | solution.py:49
  115.0 4.7 %collective-permute-done.49.refs_6_ = bf16[64,2176]{1,0:T(8,128)(2,1)S(1)} collective-permute-done((bf16[64,2176]{1,0:T(8,128)(2,1)S(1)}, bf16[64,2176]{1,0:T(8,128)(2,1)S(1)}, u32[]{:S(2)}, u32[]{:S(2)}) %collective-permute-start.49) | collective-permute-done | bytes 278560 | tf_op jit(solution)/shard_map/ppermute | solution.py:73
  119.7 2.1 %collective-permute-done.43.refs_8_ = bf16[64,2176]{1,0:T(8,128)(2,1)S(1)} collective-permute-done((bf16[64,2176]{1,0:T(8,128)(2,1)S(1)}, bf16[64,2176]{1,0:T(8,128)(2,1)S(1)}, u32[]{:S(2)}, u32[]{:S(2)}) %collective-permute-start.43) | collective-permute-done | bytes 278560 | tf_op jit(solution)/shard_map/ppermute | solution.py:73
  122.6 4.0 %collective-permute-done.38.refs_4_ = bf16[64,2176]{1,0:T(8,128)(2,1)S(1)} collective-permute-done((bf16[64,2176]{1,0:T(8,128)(2,1)S(1)}, bf16[64,2176]{1,0:T(8,128)(2,1)S(1)}, u32[]{:S(2)}, u32[]{:S(2)}) %collective-permute-start.38) | collective-permute-done | bytes 278560 | tf_op jit(solution)/shard_map/ppermute | solution.py:73
  128.6 3.9 %last.3 = (bf16[8,224,2048]{2,1,0:T(8,128)(2,1)}, bf16[8,224,2048]{2,1,0:T(8,128)(2,1)}, bf16[3,512,128]{2,1,0:T(8,128)(2,1)S(1)}) custom-call(s32[3,8]{1,0:T(4,128)S(1)} %get-tuple-element.41.where, bf16[8,224,2048]{2,1,0:T(8,128)(2,1)S(1)} %add.108.c_ref, f32[2,224,128]{2,1,0:T(8,128)S(1)} %get-tuple-element.69.refs_0_, ...), custom_call_target="tpu_custom_call" | custom-call | flops 3758096384 | bytes 7602176 | tf_op jit(solution)/shard_map/last/pallas_call | solution.py:349
  133.6 6.0 %last.4 = (bf16[8,224,2048]{2,1,0:T(8,128)(2,1)}, bf16[8,224,2048]{2,1,0:T(8,128)(2,1)}, bf16[3,512,128]{2,1,0:T(8,128)(2,1)S(1)}) custom-call(s32[3,8]{1,0:T(4,128)S(1)} %get-tuple-element.41.where, bf16[8,224,2048]{2,1,0:T(8,128)(2,1)S(1)} %add.108.c_ref, ...), custom_call_target="tpu_custom_call", output_to_operand_aliasing={{0}: (13, {}), {1}: (14, {})} | custom-call | flops 7516192768 | bytes 15204352 | tf_op jit(solution)/shard_map/last/pallas_call | solution.py:349
  139.7 3.9 %last.5 = (bf16[8,224,2048]{2,1,0:T(8,128)(2,1)}, bf16[8,224,2048]{2,1,0:T(8,128)(2,1)}, bf16[3,512,128]{2,1,0:T(8,128)(2,1)}) custom-call(s32[3,8]{1,0:T(4,128)S(1)} %get-tuple-element.41.where, bf16[8,224,2048]{2,1,0:T(8,128)(2,1)S(1)} %add.108.c_ref, f32[2,224,128]{2,1,0:T(8,128)S(1)} %pad_maximum_fusion.1.refs_0_, ...), custom_call_target="tpu_custom_call", output_to_operand_aliasing={{0}: (8, {}), {1}: (9, {})} | custom-call | flops 3758096384 | bytes 7602176 | tf_op jit(solution)/shard_map/last/pallas_call | solution.py:349
  (117 shorter events, 37.1 us)
Async XLA Ops:
  6.6 12.3 %collective-permute-start.1 = (bf16[512,128]{1,0:T(8,128)(2,1)S(1)}, bf16[512,128]{1,0:T(8,128)(2,1)S(1)}, u32[]{:S(2)}, u32[]{:S(2)}) collective-permute-start(bf16[512,128]{1,0:T(8,128)(2,1)S(1)} %get-tuple-element.83), channel_id=1, source_target_pairs={{0,8},{1,9},{2,10},{3,11},{4,12},{5,13},{6,14},{7,15},{8,0},{9,1},... | collective-permute-start | bytes 393224 | tf_op jit(solution)/shard_map/ppermute | solution.py:41
  9.5 9.4 %collective-permute-start.2 = (bf16[512,128]{1,0:T(8,128)(2,1)S(1)}, bf16[512,128]{1,0:T(8,128)(2,1)S(1)}, u32[]{:S(2)}, u32[]{:S(2)}) collective-permute-start(bf16[512,128]{1,0:T(8,128)(2,1)S(1)} %get-tuple-element.85), channel_id=1, source_target_pairs={{0,16},{1,17},{2,18},{3,19},{4,20},{5,21},{6,22},{7,23},{8,24},{9,... | collective-permute-start | bytes 393224 | tf_op jit(solution)/shard_map/ppermute | solution.py:41
  19.0 12.9 %collective-permute-start.7 = (bf16[512,128]{1,0:T(8,128)(2,1)S(1)}, bf16[512,128]{1,0:T(8,128)(2,1)S(1)}, u32[]{:S(2)}, u32[]{:S(2)}) collective-permute-start(bf16[512,128]{1,0:T(8,128)(2,1)S(1)} %fusion.6), channel_id=1, source_target_pairs={{0,2},{1,3},{2,0},{3,1},{4,6},{5,7},{6,4},{7,5},{8,10},{9,11},{10,... | collective-permute-start | bytes 393224 | tf_op jit(solution)/shard_map/ppermute | solution.py:49
  22.1 9.8 %collective-permute-start.8 = (bf16[512,128]{1,0:T(8,128)(2,1)S(1)}, bf16[512,128]{1,0:T(8,128)(2,1)S(1)}, u32[]{:S(2)}, u32[]{:S(2)}) collective-permute-start(bf16[512,128]{1,0:T(8,128)(2,1)S(1)} %fusion.6), channel_id=1, source_target_pairs={{0,3},{1,2},{2,1},{3,0},{4,7},{5,6},{6,5},{7,4},{8,11},{9,10},{10,... | collective-permute-start | bytes 393224 | tf_op jit(solution)/shard_map/ppermute | solution.py:49
  23.4 10.0 %collective-permute-start.4 = (bf16[512,128]{1,0:T(8,128)(2,1)S(1)}, bf16[512,128]{1,0:T(8,128)(2,1)S(1)}, u32[]{:S(2)}, u32[]{:S(2)}) collective-permute-start(bf16[512,128]{1,0:T(8,128)(2,1)S(1)} %fusion.6), channel_id=1, source_target_pairs={{0,1},{1,0},{2,3},{3,2},{4,5},{5,4},{6,7},{7,6},{8,9},{9,8},{10,11... | collective-permute-start | bytes 393224 | tf_op jit(solution)/shard_map/ppermute | solution.py:49
  33.5 11.1 %collective-permute-start.5 = (bf16[1024,128]{1,0:T(8,128)(2,1)S(1)}, bf16[1024,128]{1,0:T(8,128)(2,1)S(1)}, u32[]{:S(2)}, u32[]{:S(2)}) collective-permute-start(bf16[1024,128]{1,0:T(8,128)(2,1)S(1)} %constant_dynamic-update-slice_fusion.refs_0_), channel_id=1, source_target_pairs={{0,8},{1,9},{2,10},{3,11},{4,20},{5,21},{6,22},{7,23},{8,0},{9,1},... | collective-permute-start | bytes 786440 | tf_op jit(solution)/shard_map/ppermute | solution.py:73
  34.1 13.4 %collective-permute-start.18 = (bf16[1024,128]{1,0:T(8,128)(2,1)S(1)}, bf16[1024,128]{1,0:T(8,128)(2,1)S(1)}, u32[]{:S(2)}, u32[]{:S(2)}) collective-permute-start(bf16[1024,128]{1,0:T(8,128)(2,1)S(1)} %constant_dynamic-update-slice_fusion.2.refs_2_), channel_id=1, source_target_pairs={{0,16},{1,17},{2,18},{3,19},{4,12},{5,13},{6,14},{7,15},{8,24},{9,... | collective-permute-start | bytes 786440 | tf_op jit(solution)/shard_map/ppermute | solution.py:73
  35.6 11.9 %collective-permute-start.14 = (bf16[1024,128]{1,0:T(8,128)(2,1)S(1)}, bf16[1024,128]{1,0:T(8,128)(2,1)S(1)}, u32[]{:S(2)}, u32[]{:S(2)}) collective-permute-start(bf16[1024,128]{1,0:T(8,128)(2,1)S(1)} %constant_dynamic-update-slice_fusion.2.refs_2_), channel_id=1, source_target_pairs={{0,4},{1,5},{2,6},{3,7},{4,0},{5,1},{6,2},{7,3},{8,12},{9,13},{10,... | collective-permute-start | bytes 786440 | tf_op jit(solution)/shard_map/ppermute | solution.py:41
  35.6 11.9 %collective-permute-start.13 = (bf16[1024,128]{1,0:T(8,128)(2,1)S(1)}, bf16[1024,128]{1,0:T(8,128)(2,1)S(1)}, u32[]{:S(2)}, u32[]{:S(2)}) collective-permute-start(bf16[1024,128]{1,0:T(8,128)(2,1)S(1)} %constant_dynamic-update-slice_fusion.refs_0_), channel_id=1, source_target_pairs={{0,4},{1,5},{2,6},{3,7},{4,0},{5,1},{6,2},{7,3},{8,12},{9,13},{10,... | collective-permute-start | bytes 786440 | tf_op jit(solution)/shard_map/ppermute | solution.py:41
  39.0 9.0 %collective-permute-start.10 = (bf16[1024,128]{1,0:T(8,128)(2,1)S(1)}, bf16[1024,128]{1,0:T(8,128)(2,1)S(1)}, u32[]{:S(2)}, u32[]{:S(2)}) collective-permute-start(bf16[1024,128]{1,0:T(8,128)(2,1)S(1)} %collective-permute-done.9.refs_2_), channel_id=1, source_target_pairs={{0,16},{1,17},{2,18},{3,19},{4,12},{5,13},{6,14},{7,15},{8,24},{9,... | collective-permute-start | bytes 786440 | tf_op jit(solution)/shard_map/ppermute | solution.py:73
  47.5 9.0 %collective-permute-start.23 = (bf16[1024,128]{1,0:T(8,128)(2,1)S(1)}, bf16[1024,128]{1,0:T(8,128)(2,1)S(1)}, u32[]{:S(2)}, u32[]{:S(2)}) collective-permute-start(bf16[1024,128]{1,0:T(8,128)(2,1)S(1)} %collective-permute-done.9.refs_2_), channel_id=1, source_target_pairs={{0,4},{1,5},{2,6},{3,7},{4,0},{5,1},{6,2},{7,3},{8,12},{9,13},{10,... | collective-permute-start | bytes 786440 | tf_op jit(solution)/shard_map/ppermute | solution.py:41
  47.6 9.4 %collective-permute-start.22 = (bf16[1024,128]{1,0:T(8,128)(2,1)S(1)}, bf16[1024,128]{1,0:T(8,128)(2,1)S(1)}, u32[]{:S(2)}, u32[]{:S(2)}) collective-permute-start(bf16[1024,128]{1,0:T(8,128)(2,1)S(1)} %collective-permute-done.5.refs_0_), channel_id=1, source_target_pairs={{0,4},{1,5},{2,6},{3,7},{4,0},{5,1},{6,2},{7,3},{8,12},{9,13},{10,... | collective-permute-start | bytes 786440 | tf_op jit(solution)/shard_map/ppermute | solution.py:41
  54.6 20.9 %collective-permute-start.15 = (bf16[128,2176]{1,0:T(8,128)(2,1)S(1)}, bf16[128,2176]{1,0:T(8,128)(2,1)S(1)}, u32[]{:S(2)}, u32[]{:S(2)}) collective-permute-start(bf16[128,2176]{1,0:T(8,128)(2,1)S(1)} %get-tuple-element.52), channel_id=1, source_target_pairs={{0,4},{1,5},{2,6},{3,7},{4,0},{5,1},{6,2},{7,3},{8,12},{9,13},{10,... | collective-permute-start | bytes 1671176 | tf_op jit(solution)/shard_map/ppermute | solution.py:41
  59.2 8.7 %collective-permute-start.24 = (bf16[128,2176]{1,0:T(8,128)(2,1)S(1)}, bf16[128,2176]{1,0:T(8,128)(2,1)S(1)}, u32[]{:S(2)}, u32[]{:S(2)}) collective-permute-start(bf16[128,2176]{1,0:T(8,128)(2,1)S(1)} %get-tuple-element.56), channel_id=1, source_target_pairs={{0,4},{1,5},{2,6},{3,7},{4,0},{5,1},{6,2},{7,3},{8,12},{9,13},{10,... | collective-permute-start | bytes 1671176 | tf_op jit(solution)/shard_map/ppermute | solution.py:41
  65.6 8.2 %collective-permute-start.32 = (bf16[64,2176]{1,0:T(8,128)(2,1)S(1)}, bf16[64,2176]{1,0:T(8,128)(2,1)S(1)}, u32[]{:S(2)}, u32[]{:S(2)}) collective-permute-start(bf16[64,2176]{1,0:T(8,128)(2,1)S(1)} %get-tuple-element.80), channel_id=1, source_target_pairs={{0,16},{1,17},{2,18},{3,19},{4,12},{5,13},{6,14},{7,15},{8,24},{9,... | collective-permute-start | bytes 835592 | tf_op jit(solution)/shard_map/ppermute | solution.py:73
  65.8 14.0 %collective-permute-start.21 = (bf16[64,2176]{1,0:T(8,128)(2,1)S(1)}, bf16[64,2176]{1,0:T(8,128)(2,1)S(1)}, u32[]{:S(2)}, u32[]{:S(2)}) collective-permute-start(bf16[64,2176]{1,0:T(8,128)(2,1)S(1)} %get-tuple-element.81), channel_id=1, source_target_pairs={{0,16},{1,17},{2,18},{3,19},{4,12},{5,13},{6,14},{7,15},{8,24},{9,... | collective-permute-start | bytes 835592 | tf_op jit(solution)/shard_map/ppermute | solution.py:73
  67.9 19.5 %collective-permute-start.31 = (bf16[64,2176]{1,0:T(8,128)(2,1)S(1)}, bf16[64,2176]{1,0:T(8,128)(2,1)S(1)}, u32[]{:S(2)}, u32[]{:S(2)}) collective-permute-start(bf16[64,2176]{1,0:T(8,128)(2,1)S(1)} %get-tuple-element.82), channel_id=1, source_target_pairs={{0,16},{1,17},{2,18},{3,19},{4,12},{5,13},{6,14},{7,15},{8,24},{9,... | collective-permute-start | bytes 835592 | tf_op jit(solution)/shard_map/ppermute | solution.py:73
  70.3 9.6 %collective-permute-start.27 = (bf16[64,2176]{1,0:T(8,128)(2,1)S(1)}, bf16[64,2176]{1,0:T(8,128)(2,1)S(1)}, u32[]{:S(2)}, u32[]{:S(2)}) collective-permute-start(bf16[64,2176]{1,0:T(8,128)(2,1)S(1)} %sum.1), channel_id=1, source_target_pairs={{0,8},{1,9},{2,10},{3,11},{4,20},{5,21},{6,22},{7,23},{8,0},{9,1},... | collective-permute-start | bytes 835592 | tf_op jit(solution)/shard_map/ppermute | solution.py:73
  74.0 13.4 %collective-permute-start.33 = (bf16[64,2176]{1,0:T(8,128)(2,1)S(1)}, bf16[64,2176]{1,0:T(8,128)(2,1)S(1)}, u32[]{:S(2)}, u32[]{:S(2)}) collective-permute-start(bf16[64,2176]{1,0:T(8,128)(2,1)S(1)} %add_convert_fusion), channel_id=1, source_target_pairs={{0,8},{1,9},{2,10},{3,11},{4,20},{5,21},{6,22},{7,23},{8,0},{9,1},... | collective-permute-start | bytes 835592 | tf_op jit(solution)/shard_map/ppermute | solution.py:73
  80.7 10.6 %collective-permute-start.28 = (bf16[16,2176]{1,0:T(8,128)(2,1)S(1)}, bf16[16,2176]{1,0:T(8,128)(2,1)S(1)}, u32[]{:S(2)}, u32[]{:S(2)}) collective-permute-start(bf16[16,2176]{1,0:T(8,128)(2,1)S(1)} %get-tuple-element.60), channel_id=1, source_target_pairs={{0,1},{1,0},{2,3},{3,2},{4,5},{5,4},{6,7},{7,6},{8,9},{9,8},{10,11... | collective-permute-start | bytes 208904 | tf_op jit(solution)/shard_map/ppermute | solution.py:49
  84.0 8.6 %collective-permute-start.29 = (bf16[16,2176]{1,0:T(8,128)(2,1)S(1)}, bf16[16,2176]{1,0:T(8,128)(2,1)S(1)}, u32[]{:S(2)}, u32[]{:S(2)}) collective-permute-start(bf16[16,2176]{1,0:T(8,128)(2,1)S(1)} %get-tuple-element.61), channel_id=1, source_target_pairs={{0,2},{1,3},{2,0},{3,1},{4,6},{5,7},{6,4},{7,5},{8,10},{9,11},{10,... | collective-permute-start | bytes 208904 | tf_op jit(solution)/shard_map/ppermute | solution.py:49
  89.0 8.4 %collective-permute-start.35 = (bf16[16,2176]{1,0:T(8,128)(2,1)S(1)}, bf16[16,2176]{1,0:T(8,128)(2,1)S(1)}, u32[]{:S(2)}, u32[]{:S(2)}) collective-permute-start(bf16[16,2176]{1,0:T(8,128)(2,1)S(1)} %get-tuple-element.65), channel_id=1, source_target_pairs={{0,2},{1,3},{2,0},{3,1},{4,6},{5,7},{6,4},{7,5},{8,10},{9,11},{10,... | collective-permute-start | bytes 208904 | tf_op jit(solution)/shard_map/ppermute | solution.py:49
  97.4 13.2 %collective-permute-start.41 = (bf16[32,2176]{1,0:T(8,128)(2,1)S(1)}, bf16[32,2176]{1,0:T(8,128)(2,1)S(1)}, u32[]{:S(2)}, u32[]{:S(2)}) collective-permute-start(bf16[32,2176]{1,0:T(8,128)(2,1)S(1)} %pad_maximum_fusion.2), channel_id=1, source_target_pairs={{0,2},{1,3},{2,0},{3,1},{4,6},{5,7},{6,4},{7,5},{8,10},{9,11},{10,... | collective-permute-start | bytes 417800 | tf_op jit(solution)/shard_map/ppermute | solution.py:49
  99.8 10.9 %collective-permute-start.42 = (bf16[32,2176]{1,0:T(8,128)(2,1)S(1)}, bf16[32,2176]{1,0:T(8,128)(2,1)S(1)}, u32[]{:S(2)}, u32[]{:S(2)}) collective-permute-start(bf16[32,2176]{1,0:T(8,128)(2,1)S(1)} %pad_maximum_fusion.2), channel_id=1, source_target_pairs={{0,3},{1,2},{2,1},{3,0},{4,7},{5,6},{6,5},{7,4},{8,11},{9,10},{10,... | collective-permute-start | bytes 417800 | tf_op jit(solution)/shard_map/ppermute | solution.py:49
  101.4 12.4 %collective-permute-start.37 = (bf16[32,2176]{1,0:T(8,128)(2,1)S(1)}, bf16[32,2176]{1,0:T(8,128)(2,1)S(1)}, u32[]{:S(2)}, u32[]{:S(2)}) collective-permute-start(bf16[32,2176]{1,0:T(8,128)(2,1)S(1)} %pad_maximum_fusion.2), channel_id=1, source_target_pairs={{0,1},{1,0},{2,3},{3,2},{4,5},{5,4},{6,7},{7,6},{8,9},{9,8},{10,11... | collective-permute-start | bytes 417800 | tf_op jit(solution)/shard_map/ppermute | solution.py:49
  110.7 8.9 %collective-permute-start.49 = (bf16[64,2176]{1,0:T(8,128)(2,1)S(1)}, bf16[64,2176]{1,0:T(8,128)(2,1)S(1)}, u32[]{:S(2)}, u32[]{:S(2)}) collective-permute-start(bf16[64,2176]{1,0:T(8,128)(2,1)S(1)} %constant_dynamic-update-slice_fusion.4.refs_3_), channel_id=1, source_target_pairs={{0,16},{1,17},{2,18},{3,19},{4,12},{5,13},{6,14},{7,15},{8,24},{9,... | collective-permute-start | bytes 835592 | tf_op jit(solution)/shard_map/ppermute | solution.py:73
  112.3 9.5 %collective-permute-start.43 = (bf16[64,2176]{1,0:T(8,128)(2,1)S(1)}, bf16[64,2176]{1,0:T(8,128)(2,1)S(1)}, u32[]{:S(2)}, u32[]{:S(2)}) collective-permute-start(bf16[64,2176]{1,0:T(8,128)(2,1)S(1)} %constant_dynamic-update-slice_fusion.4.refs_3_), channel_id=1, source_target_pairs={{0,8},{1,9},{2,10},{3,11},{4,20},{5,21},{6,22},{7,23},{8,0},{9,1},... | collective-permute-start | bytes 835592 | tf_op jit(solution)/shard_map/ppermute | solution.py:73
  113.9 12.7 %collective-permute-start.38 = (bf16[64,2176]{1,0:T(8,128)(2,1)S(1)}, bf16[64,2176]{1,0:T(8,128)(2,1)S(1)}, u32[]{:S(2)}, u32[]{:S(2)}) collective-permute-start(bf16[64,2176]{1,0:T(8,128)(2,1)S(1)} %pad_maximum_fusion.refs_1_), channel_id=1, source_target_pairs={{0,8},{1,9},{2,10},{3,11},{4,20},{5,21},{6,22},{7,23},{8,0},{9,1},... | collective-permute-start | bytes 835592 | tf_op jit(solution)/shard_map/ppermute | solution.py:73
  114.5 12.5 %collective-permute-start.46 = (bf16[64,2176]{1,0:T(8,128)(2,1)S(1)}, bf16[64,2176]{1,0:T(8,128)(2,1)S(1)}, u32[]{:S(2)}, u32[]{:S(2)}) collective-permute-start(bf16[64,2176]{1,0:T(8,128)(2,1)S(1)} %pad_maximum_fusion.refs_1_), channel_id=1, source_target_pairs={{0,16},{1,17},{2,18},{3,19},{4,12},{5,13},{6,14},{7,15},{8,24},{9,... | collective-permute-start | bytes 835592 | tf_op jit(solution)/shard_map/ppermute | solution.py:73
  119.7 8.9 %collective-permute-start.50 = (bf16[64,2176]{1,0:T(8,128)(2,1)S(1)}, bf16[64,2176]{1,0:T(8,128)(2,1)S(1)}, u32[]{:S(2)}, u32[]{:S(2)}) collective-permute-start(bf16[64,2176]{1,0:T(8,128)(2,1)S(1)} %collective-permute-done.49.refs_6_), channel_id=1, source_target_pairs={{0,4},{1,5},{2,6},{3,7},{4,0},{5,1},{6,2},{7,3},{8,12},{9,13},{10,... | collective-permute-start | bytes 835592 | tf_op jit(solution)/shard_map/ppermute | solution.py:41
  121.9 11.8 %collective-permute-start.51 = (bf16[64,2176]{1,0:T(8,128)(2,1)S(1)}, bf16[64,2176]{1,0:T(8,128)(2,1)S(1)}, u32[]{:S(2)}, u32[]{:S(2)}) collective-permute-start(bf16[64,2176]{1,0:T(8,128)(2,1)S(1)} %collective-permute-done.43.refs_8_), channel_id=1, source_target_pairs={{0,4},{1,5},{2,6},{3,7},{4,0},{5,1},{6,2},{7,3},{8,12},{9,13},{10,... | collective-permute-start | bytes 835592 | tf_op jit(solution)/shard_map/ppermute | solution.py:41
  121.9 10.7 %collective-permute-start.44 = (bf16[64,2176]{1,0:T(8,128)(2,1)S(1)}, bf16[64,2176]{1,0:T(8,128)(2,1)S(1)}, u32[]{:S(2)}, u32[]{:S(2)}) collective-permute-start(bf16[64,2176]{1,0:T(8,128)(2,1)S(1)} %collective-permute-done.43.refs_8_), channel_id=1, source_target_pairs={{0,16},{1,17},{2,18},{3,19},{4,12},{5,13},{6,14},{7,15},{8,24},{9,... | collective-permute-start | bytes 835592 | tf_op jit(solution)/shard_map/ppermute | solution.py:73
  (27 other events, 138.2 us)
